TPU v7x, 32 devices: a whole 2x2x4 slice. The times are simulated.
32 devices in a mesh: dp: 8 (over z, core), fsdp: 4 (over y, x).
Axes of the slice: x: 2, y: 2, z: 4, core: 2. Of those that a mesh axis runs over, the one named last changes fastest.
Arguments:
- tokens: bfloat16 [32, 1024, 768], P(('dp', 'fsdp')), may hold values from -8 to 8
- hidden_token_indicator: int32 [32, 1024], P(('dp', 'fsdp')), may hold values 0 or 1
- lengths: int32 [32], P(('dp', 'fsdp')), may hold values from 256 to 1024, as said below
- time_ids: int32 [32], P(('dp', 'fsdp')), may hold values from 0 to 999
- cotangent: bfloat16 [32, 1024, 768], P(('dp', 'fsdp')), may hold values from -6 to 6
- gain_one: bfloat16 [768], P('fsdp'), may hold values from 0.5 to 1.5
- w_qkv: bfloat16 [768, 2304], P('fsdp'), may hold values from -0.21875 to 0.21875
- w_out: bfloat16 [768, 768], P('fsdp'), may hold values from -0.875 to 0.875
- gain_two: bfloat16 [768], P('fsdp'), may hold values from 0.5 to 1.5
- w_fc1: bfloat16 [768, 3072], P('fsdp'), may hold values from -0.21875 to 0.21875
- b_fc1: bfloat16 [3072], P('fsdp'), may hold values from -3 to 3
- w_fc2: bfloat16 [3072, 768], P('fsdp'), may hold values from -0.109375 to 0.109375
- b_fc2: bfloat16 [768], P('fsdp'), may hold values from -3 to 3
- w_ada: bfloat16 [4608, 128], P('fsdp'), may hold values from -0.5 to 0.5
- b_ada: bfloat16 [4608], P('fsdp'), may hold values from -3 to 3
- mask_embed: bfloat16 [768], P('fsdp'), may hold values from -5 to 5
- time_table: float32 [1000, 128], replicated, may hold values from -5 to 5
Outputs:
- output: bfloat16 [32, 1024, 768], P(('dp', 'fsdp'))
- input_grad: bfloat16 [32, 1024, 768], P(('dp', 'fsdp'))
- gain_one_grad: float32 [768], P('fsdp')
- w_qkv_grad: float32 [768, 2304], P('fsdp')
- w_out_grad: float32 [768, 768], P('fsdp')
- gain_two_grad: float32 [768], P('fsdp')
- w_fc1_grad: float32 [768, 3072], P('fsdp')
- b_fc1_grad: float32 [3072], P('fsdp')
- w_fc2_grad: float32 [3072, 768], P('fsdp')
- b_fc2_grad: float32 [768], P('fsdp')
- w_ada_grad: float32 [4608, 128], P('fsdp')
- b_ada_grad: float32 [4608], P('fsdp')
- mask_embed_grad: float32 [768], P('fsdp')
- time_table_grad: float32 [1000, 128], replicated
- rms_stats: float32 [3], replicated
Inputs may be any that keep to these rules, and one draw needn't show every extreme that they name: `lengths`: the valid tokens of a sequence are its leading positions; in every draw some sequence has all 1024 valid.
All inputs are finite; a program needn't handle non-finite values. No bound on the sum of `hidden_token_indicator` on one device may be relied on, other than what follows from the above.
Results may differ from a plain program's by a relative error of at most 0.02.
Values may be sent and summed in bfloat16 or wider, within the bound.
A program may use at most 192 MiB of HBM per device.

v0:
```python
import jax
import jax.numpy as jnp
from jax import lax
from jax.sharding import PartitionSpec as P

HD = 64


eps = 1e-05
highest = lax.Precision.HIGHEST


def layer_norm(values):
    centred = values - jnp.mean(values, axis=-1, keepdims=True)
    return centred * lax.rsqrt(jnp.mean(centred * centred, axis=-1, keepdims=True) + eps)


def modulated(values, gain_vec, scale_vec, shift_vec):
    return layer_norm(values) * gain_vec * (1.0 + scale_vec) + shift_vec


def gelu_tanh(values):
    return jax.nn.gelu(values, approximate=True)


def rotary_tables(length, head_width):
    midpoint_span = head_width // 2
    position = jnp.arange(length, dtype=jnp.float32)
    reciprocal_factor = 1.0 / 10000.0 ** (
        jnp.arange(midpoint_span, dtype=jnp.float32) * 2.0 / head_width
    )
    angles = position[:, None] * reciprocal_factor[None, :]
    angles = jnp.concatenate([angles, angles], axis=-1)
    return (jnp.cos(angles)[:, None, :], jnp.sin(angles)[:, None, :])


def rotary(values, cosine_table, sine_table):
    midpoint_span = values.shape[-1] // 2
    turned = jnp.concatenate([-values[..., midpoint_span:], values[..., :midpoint_span]], axis=-1)
    return values * cosine_table + turned * sine_table


def project(left, right):
    return jnp.einsum("bsi,ij->bsj", left, right, preferred_element_type=jnp.float32)


def project_back(grad_low, right):
    return jnp.einsum("bsj,ij->bsi", grad_low, right, preferred_element_type=jnp.float32)


def weight_grad(left, grad_low):
    return jnp.einsum("bsi,bsj->ij", left, grad_low, preferred_element_type=jnp.float32)


def token_major(values):
    head_count, batch_rows, length, head_width = values.shape
    return values.transpose(1, 2, 0, 3).reshape(batch_rows, length, head_count * head_width)


def head_slice(values, head_pos):
    return lax.dynamic_slice_in_dim(values, head_pos * HD, HD, axis=2)


def per_device(
    tokens,
    hidden_token_indicator,
    lengths,
    time_ids,
    cotangent,
    gain_one,
    w_qkv,
    w_out,
    gain_two,
    w_fc1,
    b_fc1,
    w_fc2,
    b_fc2,
    w_ada,
    b_ada,
    mask_embed,
    time_table,
):
    gathered = (
        lax.all_gather(gain_one, "fsdp", axis=0, tiled=True),
        lax.all_gather(w_qkv, "fsdp", axis=0, tiled=True),
        lax.all_gather(w_out, "fsdp", axis=0, tiled=True),
        lax.all_gather(gain_two, "fsdp", axis=0, tiled=True),
        lax.all_gather(w_fc1, "fsdp", axis=0, tiled=True),
        lax.all_gather(b_fc1, "fsdp", axis=0, tiled=True),
        lax.all_gather(w_fc2, "fsdp", axis=0, tiled=True),
        lax.all_gather(b_fc2, "fsdp", axis=0, tiled=True),
        lax.all_gather(w_ada, "fsdp", axis=0, tiled=True),
        lax.all_gather(b_ada, "fsdp", axis=0, tiled=True),
        lax.all_gather(mask_embed, "fsdp", axis=0, tiled=True),
    )
    (
        gain_one_all,
        qkv_all,
        out_all,
        gain_two_all,
        fc1_all,
        fc1_bias_all,
        fc2_all,
        fc2_bias_all,
        ada_all,
        ada_bias_all,
        embed_all,
    ) = gathered
    batch_rows, length, model_width = tokens.shape
    head_count = model_width // HD
    score_scale = HD ** (-0.5)
    arrange_rows = lambda values: values
    flag_on = (hidden_token_indicator == 1)[..., None]
    hidden0 = jnp.where(flag_on, embed_all.astype(jnp.float32), tokens.astype(jnp.float32))
    table_count = time_table.shape[0]
    one_hot = (time_ids[:, None] == jnp.arange(table_count)[None, :]).astype(jnp.float32)
    cond_pre = jnp.dot(one_hot, time_table, precision=highest)
    cond_vec = jax.nn.silu(cond_pre)
    modulation = jnp.dot(
        cond_vec, ada_all.astype(jnp.float32).T, precision=highest
    ) + ada_bias_all.astype(jnp.float32)
    shift_a, scale_a, gate_a, shift_m, scale_m, gate_m = jnp.split(
        modulation[:, None, :], 6, axis=-1
    )
    norm_one = modulated(hidden0, gain_one_all.astype(jnp.float32), scale_a, shift_a).astype(
        jnp.bfloat16
    )
    projected = project(norm_one, qkv_all)
    cosine_table, sine_table = rotary_tables(length, HD)

    def rotate_all(values):
        shaped = values.reshape(batch_rows, length, head_count, HD)
        return rotary(shaped, cosine_table, sine_table).reshape(batch_rows, length, model_width)

    queries = rotate_all(projected[..., :model_width]).astype(jnp.bfloat16)
    keys_rot = rotate_all(projected[..., model_width : 2 * model_width]).astype(jnp.bfloat16)
    values_in = projected[..., 2 * model_width :].astype(jnp.bfloat16)
    key_valid = jnp.arange(length)[None, None, :] < lengths[:, None, None]

    def head_scores(query_per_head, lookup_vectors_each_branch):
        raw_scores = (
            jnp.einsum(
                "vsi,vai->vsa",
                query_per_head,
                lookup_vectors_each_branch,
                preferred_element_type=jnp.float32,
            )
            * score_scale
        )
        return jnp.where(key_valid, raw_scores, -1e30)

    def head_forward(head_pos):
        query_per_head = head_slice(queries, head_pos)
        lookup_vectors_each_branch = head_slice(keys_rot, head_pos)
        value_per_head = head_slice(values_in, head_pos)
        scores = head_scores(query_per_head, lookup_vectors_each_branch)
        top_score = jnp.max(scores, axis=-1, keepdims=True)
        total_log = top_score + jnp.log(
            jnp.sum(jnp.exp(scores - top_score), axis=-1, keepdims=True)
        )
        attention_weights = jnp.exp(scores - total_log).astype(jnp.bfloat16)
        return (
            jnp.einsum(
                "qsu,quw->qsw",
                attention_weights,
                value_per_head,
                preferred_element_type=jnp.float32,
            ),
            total_log,
        )

    head_outs, total_logs = lax.map(head_forward, jnp.arange(head_count))
    attended = token_major(head_outs).astype(jnp.bfloat16)
    attn_proj = project(attended, out_all)
    branch_a = gate_a * attn_proj
    hidden1 = hidden0 + branch_a
    norm_two = modulated(hidden1, gain_two_all.astype(jnp.float32), scale_m, shift_m).astype(
        jnp.bfloat16
    )
    hidden_pre = project(norm_two, fc1_all) + fc1_bias_all.astype(jnp.float32)
    active = gelu_tanh(hidden_pre).astype(jnp.bfloat16)
    mlp_proj = project(active, fc2_all) + fc2_bias_all.astype(jnp.float32)
    branch_m = gate_m * mlp_proj
    block_out = hidden1 + branch_m
    valid_rows = (jnp.arange(length)[None, :] < lengths[:, None]).astype(jnp.float32)[..., None]
    stat_terms = jnp.stack(
        [
            jnp.sum(valid_rows * block_out * block_out),
            jnp.sum(valid_rows * branch_a * branch_a),
            jnp.sum(valid_rows * branch_m * branch_m),
            jnp.sum(lengths).astype(jnp.float32),
        ]
    )
    back_set = (
        lax.all_gather(gain_one, "fsdp", axis=0, tiled=True),
        lax.all_gather(w_qkv, "fsdp", axis=0, tiled=True),
        lax.all_gather(w_out, "fsdp", axis=0, tiled=True),
        lax.all_gather(gain_two, "fsdp", axis=0, tiled=True),
        lax.all_gather(w_fc1, "fsdp", axis=0, tiled=True),
        lax.all_gather(w_fc2, "fsdp", axis=0, tiled=True),
        lax.all_gather(w_ada, "fsdp", axis=0, tiled=True),
    )
    gain_one_back, qkv_back, out_back, gain_two_back, fc1_back, fc2_back, ada_back = back_set
    grad_out = cotangent.astype(jnp.float32)
    grad_gate_m = jnp.sum(grad_out * mlp_proj, axis=1, keepdims=True)
    grad_mlp = (gate_m * grad_out).astype(jnp.bfloat16)
    grad_fc2_bias = jnp.sum(grad_mlp.astype(jnp.float32), axis=(0, 1))
    grad_fc2 = weight_grad(arrange_rows(active), grad_mlp)
    grad_active = project_back(grad_mlp, fc2_back)
    gelu_pull = jax.vjp(gelu_tanh, hidden_pre)[1]
    grad_pre = gelu_pull(grad_active)[0].astype(jnp.bfloat16)
    grad_fc1_bias = jnp.sum(grad_pre.astype(jnp.float32), axis=(0, 1))
    grad_fc1 = weight_grad(arrange_rows(norm_two), grad_pre)
    grad_norm_two = project_back(grad_pre, fc1_back)
    norm_pull_two = jax.vjp(
        modulated, hidden1, gain_two_back.astype(jnp.float32), scale_m, shift_m
    )[1]
    grad_h1_part, grad_gain_two, grad_scale_m, grad_shift_m = norm_pull_two(grad_norm_two)
    grad_hidden1 = grad_out + grad_h1_part
    grad_gate_a = jnp.sum(grad_hidden1 * attn_proj, axis=1, keepdims=True)
    grad_attn_proj = (gate_a * grad_hidden1).astype(jnp.bfloat16)
    grad_out_w = weight_grad(arrange_rows(attended), grad_attn_proj)
    grad_attended = project_back(grad_attn_proj, out_back).astype(jnp.bfloat16)

    def head_backward(head_pos):
        query_per_head = head_slice(queries, head_pos)
        lookup_vectors_each_branch = head_slice(keys_rot, head_pos)
        value_per_head = head_slice(values_in, head_pos)
        head_gradient = head_slice(grad_attended, head_pos)
        scores = head_scores(query_per_head, lookup_vectors_each_branch)
        probs_full = jnp.exp(scores - total_logs[head_pos])
        probability_gradient = jnp.einsum(
            "vsi,vai->vsa", head_gradient, value_per_head, preferred_element_type=jnp.float32
        )
        row_total = jnp.sum(probs_full * probability_gradient, axis=-1, keepdims=True)
        logit_derivative = (probs_full * (probability_gradient - row_total)).astype(jnp.bfloat16)
        grad_query = (
            jnp.einsum(
                "qsu,quw->qsw",
                logit_derivative,
                lookup_vectors_each_branch,
                preferred_element_type=jnp.float32,
            )
            * score_scale
        )
        grad_key = (
            jnp.einsum(
                "hro,hrs->hos", logit_derivative, query_per_head, preferred_element_type=jnp.float32
            )
            * score_scale
        )
        grad_value = jnp.einsum(
            "hro,hrs->hos",
            probs_full.astype(jnp.bfloat16),
            head_gradient,
            preferred_element_type=jnp.float32,
        )
        return (grad_query, grad_key, grad_value)

    grad_q_heads, grad_k_heads, grad_v_heads = lax.map(head_backward, jnp.arange(head_count))
    rotate_pull = jax.vjp(rotate_all, jnp.zeros((batch_rows, length, model_width), jnp.float32))[1]
    grad_projected = jnp.concatenate(
        [
            rotate_pull(token_major(grad_q_heads))[0],
            rotate_pull(token_major(grad_k_heads))[0],
            token_major(grad_v_heads),
        ],
        axis=-1,
    ).astype(jnp.bfloat16)
    grad_qkv = weight_grad(arrange_rows(norm_one), grad_projected)
    grad_norm_one = project_back(grad_projected, qkv_back)
    norm_pull_one = jax.vjp(
        modulated, hidden0, gain_one_back.astype(jnp.float32), scale_a, shift_a
    )[1]
    grad_h0_part, grad_gain_one, grad_scale_a, grad_shift_a = norm_pull_one(grad_norm_one)
    grad_hidden0 = grad_hidden1 + grad_h0_part
    grad_embed = jnp.sum(jnp.where(flag_on, grad_hidden0, 0.0), axis=(0, 1))
    input_grad = jnp.where(flag_on, 0.0, grad_hidden0).astype(jnp.bfloat16)
    grad_mod = jnp.concatenate(
        [grad_shift_a, grad_scale_a, grad_gate_a, grad_shift_m, grad_scale_m, grad_gate_m], axis=-1
    )[:, 0, :]
    grad_mod_rows = arrange_rows(grad_mod)
    grad_ada = jnp.dot(grad_mod_rows.T, cond_vec, precision=highest)
    grad_ada_bias = jnp.sum(grad_mod_rows, axis=0)
    grad_cond = jnp.dot(grad_mod, ada_back.astype(jnp.float32), precision=highest)
    silu_pull = jax.vjp(jax.nn.silu, cond_pre)[1]
    grad_cond_pre = silu_pull(grad_cond)[0]
    grad_table = jnp.dot(one_hot.T, grad_cond_pre, precision=highest)
    table_sum, stat_sum = lax.psum((grad_table, stat_terms), ("dp", "fsdp"))
    rms_stats = jnp.sqrt(stat_sum[:3] / (stat_sum[3] * model_width))
    group_sums = (
        lax.psum_scatter(
            arrange_rows(grad_gain_one).astype(jnp.bfloat16),
            "fsdp",
            scatter_dimension=0,
            tiled=True,
        ).astype(jnp.float32),
        lax.psum_scatter(
            grad_qkv.astype(jnp.bfloat16), "fsdp", scatter_dimension=0, tiled=True
        ).astype(jnp.float32),
        lax.psum_scatter(
            grad_out_w.astype(jnp.bfloat16), "fsdp", scatter_dimension=0, tiled=True
        ).astype(jnp.float32),
        lax.psum_scatter(
            arrange_rows(grad_gain_two).astype(jnp.bfloat16),
            "fsdp",
            scatter_dimension=0,
            tiled=True,
        ).astype(jnp.float32),
        lax.psum_scatter(
            grad_fc1.astype(jnp.bfloat16), "fsdp", scatter_dimension=0, tiled=True
        ).astype(jnp.float32),
        lax.psum_scatter(
            arrange_rows(grad_fc1_bias).astype(jnp.bfloat16),
            "fsdp",
            scatter_dimension=0,
            tiled=True,
        ).astype(jnp.float32),
        lax.psum_scatter(
            grad_fc2.astype(jnp.bfloat16), "fsdp", scatter_dimension=0, tiled=True
        ).astype(jnp.float32),
        lax.psum_scatter(
            arrange_rows(grad_fc2_bias).astype(jnp.bfloat16),
            "fsdp",
            scatter_dimension=0,
            tiled=True,
        ).astype(jnp.float32),
        lax.psum_scatter(
            grad_ada.astype(jnp.bfloat16), "fsdp", scatter_dimension=0, tiled=True
        ).astype(jnp.float32),
        lax.psum_scatter(
            grad_ada_bias.astype(jnp.bfloat16), "fsdp", scatter_dimension=0, tiled=True
        ).astype(jnp.float32),
        lax.psum_scatter(
            arrange_rows(grad_embed).astype(jnp.bfloat16), "fsdp", scatter_dimension=0, tiled=True
        ).astype(jnp.float32),
    )
    reduced = (
        lax.psum(group_sums[0].astype(jnp.bfloat16), "dp").astype(jnp.float32),
        lax.psum(group_sums[1].astype(jnp.bfloat16), "dp").astype(jnp.float32),
        lax.psum(group_sums[2].astype(jnp.bfloat16), "dp").astype(jnp.float32),
        lax.psum(group_sums[3].astype(jnp.bfloat16), "dp").astype(jnp.float32),
        lax.psum(group_sums[4].astype(jnp.bfloat16), "dp").astype(jnp.float32),
        lax.psum(group_sums[5].astype(jnp.bfloat16), "dp").astype(jnp.float32),
        lax.psum(group_sums[6].astype(jnp.bfloat16), "dp").astype(jnp.float32),
        lax.psum(group_sums[7].astype(jnp.bfloat16), "dp").astype(jnp.float32),
        lax.psum(group_sums[8].astype(jnp.bfloat16), "dp").astype(jnp.float32),
        lax.psum(group_sums[9].astype(jnp.bfloat16), "dp").astype(jnp.float32),
        lax.psum(group_sums[10].astype(jnp.bfloat16), "dp").astype(jnp.float32),
    )
    return (
        block_out.astype(jnp.bfloat16),
        input_grad,
        reduced[0],
        reduced[1],
        reduced[2],
        reduced[3],
        reduced[4],
        reduced[5],
        reduced[6],
        reduced[7],
        reduced[8],
        reduced[9],
        reduced[10],
        table_sum,
        rms_stats,
    )


def solution(mesh):
    placed = (
        P(("dp", "fsdp"), None, None),
        P(("dp", "fsdp"), None),
        P(("dp", "fsdp")),
        P(("dp", "fsdp")),
        P(("dp", "fsdp"), None, None),
        P("fsdp"),
        P("fsdp", None),
        P("fsdp", None),
        P("fsdp"),
        P("fsdp", None),
        P("fsdp"),
        P("fsdp", None),
        P("fsdp"),
        P("fsdp", None),
        P("fsdp"),
        P("fsdp"),
        P(),
    )
    return jax.shard_map(
        per_device,
        mesh=mesh,
        in_specs=placed,
        out_specs=(
            P(("dp", "fsdp"), None, None),
            P(("dp", "fsdp"), None, None),
            P("fsdp"),
            P("fsdp", None),
            P("fsdp", None),
            P("fsdp"),
            P("fsdp", None),
            P("fsdp"),
            P("fsdp", None),
            P("fsdp"),
            P("fsdp", None),
            P("fsdp"),
            P("fsdp"),
            P(),
            P(),
        ),
        check_vma=False,
    )
```

profile of v0, /device:TPU:0, one launch (start us, length us, event | category | flops | bytes accessed | tf_op | source)
XLA Modules:
  0.0 996.2 jit_solution(2653263404285587105)
XLA Ops:
  14.3 12.2 %all-reduce.17 = (bf16[768]{0:T(1024)(128)(2,1)S(1)}, bf16[768]{0:T(1024)(128)(2,1)S(1)}, bf16[768]{0:T(1024)(128)(2,1)S(1)}, bf16[768]{0:T(1024)(128)(2,1)S(1)}) all-reduce(bf16[768]{0:T(1024)(128)(2,1)S(1)} %dynamic-update-slice.1, bf16[768]{0:T(1024)(128)(2,1)S(1)} %dynamic-update-slice, ...), channel_id=1, replica_groups=mesh['dp'=8,'fsdp'=4] {'fsdp'}, use_global_device_ids=true, to_apply=%add.5 | all-reduce | flops 3072 | bytes 12288
  28.7 7.1 all-gather
  51.8 9.0 all-gather.1
  65.2 24.2 %all-gather.10.cloned.1.call-done = bf16[768,2304]{1,0:T(8,128)(2,1)} async-done(((bf16[192,2304]{1,0:T(8,128)(2,1)}), bf16[768,2304]{1,0:T(8,128)(2,1)}) %all-gather.10.cloned.1.call-update) | async-done | bytes 3538960 | tf_op jit(solution)/shard_map/all_gather | solution.py:85
  89.5 6.4 convolution_bitcast_fusion
  126.0 10.1 %add_convert_fusion.1 = (bf16[1,1024,768]{2,1,0:T(8,128)(2,1)S(1)}, bf16[1,1024,768]{2,1,0:T(8,128)(2,1)}) fusion(f32[1,1024,768]{2,1,0:T(8,128)} %copy.48, f32[1,1024,768]{2,1,0:T(8,128)} %copy.45, f32[1,1024,768]{2,1,0:T(8,128)} %copy.42, f32[1,1024,2304]{2,1,0:T(8,128)} %copy-done.3, f32[1,1024,768]{2,1,0:T(8,128)} %copy.44), kind=kLoop, calls=%fused_computation.124 | loop fusion | flops 6291456 | bytes 22020096 | tf_op jit(solution)/shard_map/convert_element_type | solution.py:136
  136.1 90.5 %while.30 = (s32[]{:T(128)}, bf16[12,1,1024,64]{2,3,1,0:T(8,128)(2,1)}, f32[12,1,1024,1]{2,3,1,0:T(1,128)S(1)}, s32[12]{0:T(128)S(1)}, bf16[1,1024,768]{2,1,0:T(...) while((s32[]{:T(128)}, ...), condition=%wide.region_5.6_spmd.clone.clone, body=%wide.region_2.5_spmd.clone.sunk.clone | while | flops 279969792 | bytes 13674147 | solution.py:172
  226.6 5.6 fusion.122
  234.5 15.2 %multiply_convert_fusion.1 = (bf16[1024,3072]{1,0:T(8,128)(2,1)}, f32[1024,3072]{1,0:T(8,128)}) fusion(f32[3072]{0:T(1024)S(1)} %bitcast.279, bf16[768,3072]{1,0:T(8,128)(2,1)} %all-gather.14.cloned.1.call-done, f32[1,1024,768]{2,1,0:T(8,128)} %copy-done.8, f32[768]{0:T(1024)S(1)} %get-tuple-element.180, f32[768]{0:T(1024)S(1)} %get-tuple-element.181, ...), kind=kOutput, calls=%fused_computation.72 | convolution fusion | flops 4868014080 | bytes 26768384 | tf_op jit(solution)/shard_map/bsi,ij->bsj/dot_general | solution.py:44
  249.7 16.7 %fusion.128 = (bf16[3072]{0:T(1024)(128)(2,1)S(1)}, bf16[1024,3072]{1,0:T(8,128)(2,1)S(1)}) fusion(f32[1024,3072]{1,0:T(8,128)} %get-tuple-element.282, f32[3072]{0:T(1024)S(1)} %bitcast.280, bf16[3072,768]{1,0:T(8,128)(2,1)} %all-gather.16.cloned.1.call-done, bf16[1,1024,768]{2,1,0:T(8,128)(2,1)} %param.25, f32[768]{0:T(1024)S(1)} %get-tuple-element.179), kind=kOutput, calls=%fused_computation.208 | convolution fusion | flops 4903400448 | bytes 25187328 | tf_op jit(solution)/shard_map/bsj,ij->bsi/dot_general | solution.py:48
  266.5 5.1 fusion.129
  272.4 11.2 %fusion.66 = (f32[]{:T(128)}, f32[768]{0:T(1024)S(1)}, f32[1024]{0:T(1024)S(1)}, bf16[768]{0:T(1024)(128)(2,1)S(1)}, f32[768]{0:T(1024)S(1)}, /*index=5*/bf16[1,1024,768]{2,1,0:T(8,128)(2,1)}, f32[1024,768]{1,0:T(8,128)}) fusion(f32[1024]{0:T(1024)S(1)} %fusion.100, f32[1,1024,768]{2,1,0:T(8,128)S(1)} %copy-done.9, f32[768]{0:T(1024)S(1)} %convert_element_type.216, ...), kind=kOutput, calls=%fused_computation.88 | convolution fusion | flops 4848349184 | bytes 23629316 | tf_op jit(solution)/shard_map/bsi,ij->bsj/dot_general | solution.py:44
  289.8 4.8 fusion.90
  294.6 231.6 %while.31 = (s32[]{:T(128)}, f32[12,1,1024,64]{2,3,1,0:T(8,128)}, f32[12,1,1024,64]{2,3,1,0:T(8,128)}, bf16[12,1,1024,64]{2,3,1,0:T(8,128)(2,1)}, s32[12]{0:T(12...) while((s32[]{:T(128)}, f32[12,1,1024,64]{2,3,1,0:T(8,128)}, ...), condition=%wide.region_12.13_spmd.clone.clone, body=%wide.region_10.12_spmd.clone.sunk.clone | while | flops 686948352 | bytes 50892536 | solution.py:260
  302.0 3.9 multiply_reduce_fusion.5
  340.7 3.8 multiply_reduce_fusion.5
  359.9 3.8 multiply_reduce_fusion.5
  514.2 3.8 multiply_reduce_fusion.5
  533.4 4.9 fusion.78
  538.4 9.5 fusion.71
  558.9 8.8 convolution_convert_fusion.2
  567.8 10.5 %convolution_convert_fusion.1 = bf16[768,3072]{1,0:T(8,128)(2,1)} fusion(bf16[1024,3072]{1,0:T(8,128)(2,1)} %copy-done.50, f32[1,1024,768]{2,1,0:T(8,128)} %copy-done.8, f32[768]{0:T(1024)S(1)} %get-tuple-element.180, f32[768]{0:T(1024)S(1)} %get-tuple-element.181, f32[768]{0:T(1024)S(1)} %convert_element_type.212, f32[1024]{0:T(1024)S(1)} %fusion.102, ...), kind=kOutput, calls=%fused_computation.75 | convolution fusion | flops 4838916096 | bytes 14173184 | tf_op jit(solution)/shard_map/bsi,bsj->ij/dot_general | solution.py:52
  579.7 10.0 %convolution_convert_fusion = bf16[3072,768]{1,0:T(8,128)(2,1)} fusion(bf16[1024,3072]{1,0:T(8,128)(2,1)} %get-tuple-element.281, bf16[1,1024,768]{2,1,0:T(8,128)(2,1)S(1)} %copy-done.14, f32[768]{0:T(1024)S(1)} %get-tuple-element.179), kind=kOutput, calls=%fused_computation.74 | convolution fusion | flops 4836556800 | bytes 12585984 | tf_op jit(solution)/shard_map/bsi,bsj->ij/dot_general | solution.py:52
  589.8 48.2 %reduce-scatter.6.cloned.1.call-done = bf16[192,2304]{1,0:T(8,128)(2,1)} async-done(((bf16[768,2304]{1,0:T(8,128)(2,1)}), bf16[192,2304]{1,0:T(8,128)(2,1)}) %reduce-scatter.6.cloned.1.call-update) | async-done | bytes 884752 | tf_op jit(solution)/shard_map/reduce_scatter | solution.py:298
  638.0 60.0 %reduce-scatter.10.cloned.1.call-done = bf16[192,3072]{1,0:T(8,128)(2,1)} async-done(((bf16[768,3072]{1,0:T(8,128)(2,1)}), bf16[192,3072]{1,0:T(8,128)(2,1)}) %reduce-scatter.10.cloned.1.call-update) | async-done | bytes 1179664 | tf_op jit(solution)/shard_map/reduce_scatter | solution.py:310
  698.0 59.8 %reduce-scatter.12.cloned.1.call-done = bf16[768,768]{1,0:T(8,128)(2,1)} async-done(((bf16[3072,768]{1,0:T(8,128)(2,1)}), bf16[768,768]{1,0:T(8,128)(2,1)}) %reduce-scatter.12.cloned.1.call-update) | async-done | bytes 1179664 | tf_op jit(solution)/shard_map/reduce_scatter | solution.py:319
  761.6 4.7 fusion.67
  768.7 40.6 %psum.103 = f32[4]{0:T(128)S(1)} all-reduce(f32[4]{0:T(128)S(1)} %pad_maximum_fusion.6), channel_id=1, replica_groups=mesh['dp'=8,'fsdp'=4] {'dp','fsdp'}, use_global_device_ids=true, to_apply=%region_52.53 | all-reduce | flops 4 | bytes 32 | tf_op jit(solution)/shard_map/psum | solution.py:289
  809.9 17.0 %all-reduce.16 = (bf16[768]{0:T(1024)(128)(2,1)S(1)}, bf16[768]{0:T(1024)(128)(2,1)S(1)}, bf16[3072]{0:T(1024)(128)(2,1)S(1)}, bf16[768]{0:T(1024)(128)(2,1)S(1)...) all-reduce(bf16[768]{0:T(1024)(128)(2,1)S(1)} %get-tuple-element.17, ...), channel_id=2, replica_groups=mesh['dp'=8,'fsdp'=4] {'fsdp'}, use_global_device_ids=true, to_apply=%region_16.17.clone | all-reduce | flops 10752 | bytes 43008
  827.4 14.9 %all-reduce.14 = (bf16[192]{0:T(256)(128)(2,1)S(1)}, bf16[192]{0:T(256)(128)(2,1)S(1)}, bf16[768]{0:T(1024)(128)(2,1)S(1)}, bf16[192]{0:T(256)(128)(2,1)S(1)}, b...) all-reduce(bf16[192]{0:T(256)(128)(2,1)S(1)} %dynamic-slice.5, ...), channel_id=1, replica_groups=mesh['dp'=8,'fsdp'=4] {'dp'}, use_global_device_ids=true, to_apply=%region_17.18 | all-reduce | flops 2688 | bytes 10752 | tf_op jit(solution)/shard_map/psum | solution.py:339
  847.0 5.6 all-reduce.23.cloned.1.call-done
  860.3 127.1 %all-reduce.21.cloned.1.call-done = f32[1000,128]{1,0:T(8,128)} async-done(((f32[1000,128]{1,0:T(8,128)}), f32[1000,128]{1,0:T(8,128)}) %all-reduce.21.cloned.1.call-update) | async-done | bytes 512016 | tf_op jit(solution)/shard_map/psum | solution.py:289
  (446 shorter events, 376.1 us)
Async XLA Ops:
  7.2 54.3 %copy-start = (f32[1000,128]{1,0:T(8,128)S(1)}, f32[1000,128]{1,0:T(8,128)}, u32[]{:S(2)}) copy-start(f32[1000,128]{1,0:T(8,128)} %param.37) | copy-start | bytes 1536004
  7.2 6.1 copy-start.46
  7.2 6.4 copy-start.47
  7.2 6.6 copy-start.48
  7.2 6.8 copy-start.49
  7.3 19.2 %copy-start.37 = (s32[1,1024]{1,0:T(1,128)S(1)}, s32[1,1024]{1,0:T(1,128)}, u32[]{:S(2)}) copy-start(s32[1,1024]{1,0:T(1,128)} %param.22) | copy-start | bytes 12292
  7.3 19.2 %copy-start.4 = (bf16[1,1024,768]{2,1,0:T(8,128)(2,1)S(1)}, bf16[1,1024,768]{2,1,0:T(8,128)(2,1)}, u32[]{:S(2)}) copy-start(bf16[1,1024,768]{2,1,0:T(8,128)(2,1)} %param.21) | copy-start | bytes 4718596
  7.3 55.0 %all-gather.8.cloned.1.call-start = ((), (), s32[]{:S(2)}) async-start(), calls=%async_computation.5 | async-start | bytes 1474560 | tf_op jit(solution)/shard_map/all_gather | solution.py:92
  8.0 81.4 %all-gather.10.cloned.1.call-start = ((), (), s32[]{:S(2)}) async-start(), calls=%async_computation.6 | async-start | bytes 4423680 | tf_op jit(solution)/shard_map/all_gather | solution.py:85
  8.8 217.8 %all-gather.12.cloned.1.call-start = ((), (), s32[]{:S(2)}) async-start(), calls=%async_computation.7 | async-start | bytes 1474560 | tf_op jit(solution)/shard_map/all_gather | solution.py:86
  9.5 225.0 %all-gather.14.cloned.1.call-start = ((), (), s32[]{:S(2)}) async-start(), calls=%async_computation.8 | async-start | bytes 5898240 | tf_op jit(solution)/shard_map/all_gather | solution.py:88
  10.1 18.6 %copy-start.38 = (bf16[1152]{0:T(1024)(128)(2,1)S(1)}, bf16[1152]{0:T(1024)(128)(2,1)}, u32[]{:S(2)}) copy-start(bf16[1152]{0:T(1024)(128)(2,1)} %param.35) | copy-start | bytes 6916
  10.1 239.6 %all-gather.16.cloned.1.call-start = ((), (), s32[]{:S(2)}) async-start(), calls=%async_computation.9 | async-start | bytes 5898240 | tf_op jit(solution)/shard_map/all_gather | solution.py:90
  10.7 579.1 %reduce-scatter.8.cloned.1.call-start = ((), (), s32[]{:S(2)}) async-start(), calls=%async_computation.11 | async-start | bytes 1474560 | tf_op jit(solution)/shard_map/reduce_scatter | solution.py:301
  27.1 62.4 %copy-start.25 = (f32[1024]{0:T(1024)}, f32[1024]{0:T(1024)S(1)}, u32[]{:S(2)}) copy-start(f32[1024]{0:T(1024)S(1)} %broadcast_multiply_fusion.2) | copy-start | bytes 12292
  28.0 61.5 %copy-start.29 = (f32[1024]{0:T(1024)}, f32[1024]{0:T(1024)S(1)}, u32[]{:S(2)}) copy-start(f32[1024]{0:T(1024)S(1)} %fusion.101) | copy-start | bytes 12292
  28.0 61.5 %copy-start.31 = (f32[768]{0:T(1024)}, f32[768]{0:T(1024)S(1)}, u32[]{:S(2)}) copy-start(f32[768]{0:T(1024)S(1)} %convert_element_type.205) | copy-start | bytes 9220
  37.0 6.3 copy-start.18
  65.2 30.7 %copy-start.33 = (f32[768]{0:T(1024)}, f32[768]{0:T(1024)S(1)}, u32[]{:S(2)}) copy-start(f32[768]{0:T(1024)S(1)} %get-tuple-element.183) | copy-start | bytes 9220
  65.2 30.7 %copy-start.39 = (f32[768]{0:T(1024)}, f32[768]{0:T(1024)S(1)}, u32[]{:S(2)}) copy-start(f32[768]{0:T(1024)S(1)} %get-tuple-element.182) | copy-start | bytes 9220
  249.7 16.7 %copy-start.45 = (bf16[768,3072]{1,0:T(8,128)(2,1)S(1)}, bf16[768,3072]{1,0:T(8,128)(2,1)}, u32[]{:S(2)}) copy-start(bf16[768,3072]{1,0:T(8,128)(2,1)} %all-gather.14.cloned.1.call-done) | copy-start | bytes 14155780
  266.4 6.0 copy-start.44
  289.7 300.1 %reduce-scatter.14.cloned.1.call-start = ((), (), s32[]{:S(2)}) async-start(), calls=%async_computation.14 | async-start | bytes 1474560 | tf_op jit(solution)/shard_map/reduce_scatter | solution.py:328
  294.6 231.6 %copy-start.19 = (f32[1024,64]{0,1:T(8,128)S(1)}, f32[1024,64]{0,1:T(8,128)}, u32[]{:S(2)}) copy-start(f32[1024,64]{0,1:T(8,128)} %copy-done.18) | copy-start | bytes 786436
  558.9 79.2 %reduce-scatter.6.cloned.1.call-start = ((), (), s32[]{:S(2)}) async-start(), calls=%async_computation.10 | async-start | bytes 4423680 | tf_op jit(solution)/shard_map/reduce_scatter | solution.py:298
  567.8 130.3 %reduce-scatter.10.cloned.1.call-start = ((), (), s32[]{:S(2)}) async-start(), calls=%async_computation.12 | async-start | bytes 5898240 | tf_op jit(solution)/shard_map/reduce_scatter | solution.py:310
  578.3 179.6 %reduce-scatter.12.cloned.1.call-start = ((), (), s32[]{:S(2)}) async-start(), calls=%async_computation.13 | async-start | bytes 5898240 | tf_op jit(solution)/shard_map/reduce_scatter | solution.py:319
  589.7 170.3 %copy-start.15 = (bf16[4608,128]{1,0:T(8,128)(2,1)S(1)}, bf16[4608,128]{1,0:T(8,128)(2,1)}, u32[]{:S(2)}) copy-start(bf16[4608,128]{1,0:T(8,128)(2,1)} %all-gather.8.cloned.1.call-done) | copy-start | bytes 3538948
  589.7 170.4 %copy-start.36 = (f32[128]{0:T(128)S(1)}, f32[128]{0:T(128)}, u32[]{:S(2)}) copy-start(f32[128]{0:T(128)} %copy-done.35) | copy-start | bytes 1540
  589.7 262.8 %all-reduce.23.cloned.1.call-start = ((), (), s32[]{:S(2)}) async-start(), calls=%async_computation.16 | async-start | bytes 7667712 | tf_op jit(solution)/shard_map/psum | solution.py:340
  757.9 229.5 %all-reduce.21.cloned.1.call-start = ((), (), s32[]{:S(2)}) async-start(), calls=%async_computation.15 | async-start | bytes 1024000 | tf_op jit(solution)/shard_map/psum | solution.py:289
  855.7 133.5 %copy-start.1 = (f32[1000,128]{1,0:T(8,128)S(1)}, f32[1000,128]{1,0:T(8,128)}, u32[]{:S(2)}) copy-start(f32[1000,128]{1,0:T(8,128)} %param.37) | copy-start | bytes 1536004
  (42 other events, 149.4 us)
Sparse Core Ops, SparseCore 0:
  9.9 30.4 all-gather.7
  42.3 47.1 all-gather.9
  91.3 27.5 all-gather.11
  120.6 56.9 all-gather.13
  179.3 56.9 all-gather.15
  289.9 28.7 reduce-scatter.7
  559.0 28.7 reduce-scatter.13
  590.8 47.1 reduce-scatter.5
  641.0 56.9 reduce-scatter.9
  700.9 56.9 reduce-scatter.11
  760.6 91.8 all-reduce.22
  858.3 129.0 all-reduce.20
where the time goes:
time: 1010 us; the launch traced here: 996 us
  matrix products  335 us (33%)
  waiting for transfers between devices  328 us (32%)
  other arithmetic  112 us (11%)
  blocking collectives  101 us (10%)
  local copies, waits for them, and re-layouts  63.1 us (6%)
  loops' own time  35.7 us (4%)
  between operations  19.7 us (2%)
    psum x1, waiting for transfers between devices, per_device(): table_sum, stat_sum = lax.psum((grad_table, stat_terms), ('dp', 'fsdp'))  127 us
    dot_general x24, matrix products, head_scores(): jnp.einsum('vsi,vai->vsa', query_per_head, lookup_vectors_each_branch, pr...  66.5 us
    reduce_scatter x1, waiting for transfers between devices, per_device(): lax.psum_scatter(grad_fc1.astype(jnp.bfloat16), 'fsdp', scatter_dimension...  60 us
    reduce_scatter x1, waiting for transfers between devices, per_device(): lax.psum_scatter(grad_fc2.astype(jnp.bfloat16), 'fsdp', scatter_dimension...  59.8 us
    reduce_scatter x1, waiting for transfers between devices, per_device(): lax.psum_scatter(grad_qkv.astype(jnp.bfloat16), 'fsdp', scatter_dimension...  48.2 us
    dot_general x12, matrix products, head_backward(): jnp.einsum('vsi,vai->vsa', head_gradient, value_per_head, preferred_eleme...  46.3 us
    psum x1, blocking collectives, per_device(): table_sum, stat_sum = lax.psum((grad_table, stat_terms), ('dp', 'fsdp'))  40.6 us
    dot_general x4, matrix products, project(): jnp.einsum('bsi,ij->bsj', left, right, preferred_element_type=jnp.float32)  38.5 us
  transfers between devices with their start and end apart: 12, of which 6 were waited for; matrix products, arithmetic and copies ran while one was open for 46% of the time, Pallas kernels for 0%

commit v1 on v0

v1 whole, which is shorter than its diff:
```python
import functools, math
import jax, jax.numpy as jnp
from jax import lax
from jax.experimental import pallas as pl
from jax.experimental.pallas import tpu as pltpu

HD = 64
EPS = 1e-5
LOG2E = math.log2(math.e)
QSCALE = LOG2E * HD ** -0.5
f32, bf16 = jnp.float32, jnp.bfloat16
NT = (((1,), (1,)), ((), ()))
NN = (((1,), (0,)), ((), ()))
TN = (((0,), (0,)), ((), ()))

def dot(a, b, dims=NN):
    return lax.dot_general(a, b, dims, preferred_element_type=f32)

def norm_parts(x):
    mean = jnp.mean(x, axis=-1, keepdims=True)
    cen = x - mean
    rs = lax.rsqrt(jnp.mean(cen * cen, axis=-1, keepdims=True) + EPS)
    return cen * rs, rs

def swap_halves(u):
    lane = lax.broadcasted_iota(jnp.int32, u.shape, 1)
    return jnp.where(lane % HD < HD // 2, pltpu.roll(u, 96, 1), pltpu.roll(u, 32, 1))

def pre_kernel(tok_ref, flag_ref, vec_ref, w_ref, cos_ref, sin_ref, n1_ref, qkv_ref):
    emb, gain, scale, shift = (vec_ref[i:i + 1, :] for i in range(4))
    h0 = jnp.where(flag_ref[...] == 1, emb, tok_ref[...].astype(f32))
    n, _ = norm_parts(h0)
    n1 = (n * gain * (1.0 + scale) + shift).astype(bf16)
    n1_ref[...] = n1
    d = n1.shape[1]
    cos, sin = cos_ref[...], sin_ref[...]
    for part in range(3):
        y = dot(n1, w_ref[:, part * d:(part + 1) * d])
        for c in range(d // 128):
            lo = part * d + c * 128
            u = y[:, c * 128:(c + 1) * 128]
            if part < 2:
                u = u * cos + swap_halves(u) * sin
                if part == 0:
                    u = u * QSCALE
            qkv_ref[:, lo:lo + 128] = u.astype(bf16)

def pre_call(tok, flag, vecs, w, cos, sin, rows=256):
    s, d = tok.shape
    return pl.pallas_call(
        pre_kernel, grid=(s // rows,),
        in_specs=[pl.BlockSpec((rows, d), lambda i: (i, 0)), pl.BlockSpec((rows, 1), lambda i: (i, 0)),
                  pl.BlockSpec((8, d), lambda i: (0, 0)), pl.BlockSpec((d, 3 * d), lambda i: (0, 0)),
                  pl.BlockSpec((rows, 128), lambda i: (i, 0)), pl.BlockSpec((rows, 128), lambda i: (i, 0))],
        out_specs=[pl.BlockSpec((rows, d), lambda i: (i, 0)), pl.BlockSpec((rows, 3 * d), lambda i: (i, 0))],
        out_shape=[jax.ShapeDtypeStruct((s, d), bf16), jax.ShapeDtypeStruct((s, 3 * d), bf16)],
        cost_estimate=pl.CostEstimate(flops=2 * s * d * 3 * d, bytes_accessed=12 * s * d, transcendentals=0),
        name="pre")(tok, flag, vecs, w, cos, sin)

def attn_fwd_kernel(len_ref, q_ref, k_ref, v_ref, o_ref, lse_ref, *, rows):
    p = pl.program_id(0)
    s = q_ref.shape[0]
    length = len_ref[0]
    lane = lax.broadcasted_iota(jnp.int32, (s, 128), 1)
    pos = lax.broadcasted_iota(jnp.int32, (s, 128), 0)
    lane_q = lax.broadcasted_iota(jnp.int32, (rows, 128), 1)
    k = k_ref[...].astype(f32)
    v = v_ref[...].astype(f32)
    kx, vx = [], []
    for h in (0, 1):
        extra = HD * (1 - h)
        mine = (lane >= HD) if h else (lane < HD)
        bias = jnp.where(pos >= length, -1e30, 0.0)
        kx.append(jnp.where(mine, k, jnp.where(lane == extra, bias, 0.0)).astype(bf16))
        vx.append(jnp.where(mine, v, jnp.where(lane == extra, 1.0, 0.0)).astype(bf16))
    for b in range(s // rows):
        q = q_ref[b * rows:(b + 1) * rows, :].astype(f32)
        outs, lses = [], []
        for h in (0, 1):
            extra = HD * (1 - h)
            mine = (lane_q >= HD) if h else (lane_q < HD)
            qx = jnp.where(mine, q, jnp.where(lane_q == extra, 1.0, 0.0)).astype(bf16)
            sc = dot(qx, kx[h], NT)
            m = jnp.max(sc, axis=1, keepdims=True)
            pr = jnp.exp2(sc - m).astype(bf16)
            o = dot(pr, vx[h])
            tot = o[:, extra:extra + 1]
            outs.append(o * (1.0 / tot))
            lses.append(m + jnp.log(tot) * LOG2E)
        o_ref[b * rows:(b + 1) * rows, :] = jnp.where(lane_q < HD, outs[0], outs[1]).astype(bf16)
        old = jnp.where(p == 0, 0.0, lse_ref[b * rows:(b + 1) * rows, :])
        lse_ref[b * rows:(b + 1) * rows, :] = jnp.where(
            lane_q == 2 * p, lses[0], jnp.where(lane_q == 2 * p + 1, lses[1], old))

def attn_fwd_call(length, qkv, rows=256):
    s, d3 = qkv.shape
    d = d3 // 3
    np_ = d // 128
    return pl.pallas_call(
        functools.partial(attn_fwd_kernel, rows=rows), grid=(np_,),
        in_specs=[pl.BlockSpec(memory_space=pltpu.SMEM),
                  pl.BlockSpec((s, 128), lambda i: (0, i)),
                  pl.BlockSpec((s, 128), lambda i: (0, np_ + i)),
                  pl.BlockSpec((s, 128), lambda i: (0, 2 * np_ + i))],
        out_specs=[pl.BlockSpec((s, 128), lambda i: (0, i)), pl.BlockSpec((s, 128), lambda i: (0, 0))],
        out_shape=[jax.ShapeDtypeStruct((s, d), bf16), jax.ShapeDtypeStruct((s, 128), f32)],
        cost_estimate=pl.CostEstimate(flops=8 * s * s * d, bytes_accessed=8 * s * d, transcendentals=s * s * 12),
        name="attn_fwd")(length, qkv, qkv, qkv)

def split3(x):
    hi = x.astype(bf16).astype(f32)
    r = x - hi
    mid = r.astype(bf16).astype(f32)
    return hi, mid, r - mid

def attn_bwd_kernel(len_ref, q_ref, k_ref, v_ref, o_ref, g_ref, lse_ref, cos_ref, sin_ref,
                    dq_ref, dk_ref, dv_ref, dqs, *, rows):
    p = pl.program_id(0)
    s = q_ref.shape[0]
    length = len_ref[0]
    lane = lax.broadcasted_iota(jnp.int32, (s, 128), 1)
    pos = lax.broadcasted_iota(jnp.int32, (s, 128), 0)
    lane_q = lax.broadcasted_iota(jnp.int32, (rows, 128), 1)
    k = k_ref[...].astype(f32)
    v = v_ref[...].astype(f32)
    bias = jnp.where(pos >= length, -1e30, 0.0)
    dks, dvs = [], []
    for h in (0, 1):
        e = HD * (1 - h)
        mine = (lane >= HD) if h else (lane < HD)
        mine_q = (lane_q >= HD) if h else (lane_q < HD)
        ones = jnp.where((lane >= e) & (lane < e + 3), 1.0, 0.0)
        kx = jnp.where(mine, k, jnp.where(lane == e + 3, bias, ones)).astype(bf16)
        vx = jnp.where(mine, v, ones).astype(bf16)
        kt = jnp.where(mine, k, 0.0).T.astype(bf16)
        dk = jnp.zeros((s, 128), f32)
        dv = jnp.zeros((s, 128), f32)
        for b in range(s // rows):
            sl = slice(b * rows, (b + 1) * rows)
            qb = q_ref[sl, :]
            gb = g_ref[sl, :]
            q = qb.astype(f32)
            g = gb.astype(f32)
            lse = jnp.sum(jnp.where(lane_q == 2 * p + h, lse_ref[sl, :], 0.0), axis=1, keepdims=True)
            dd = jnp.sum(jnp.where(mine_q, g * o_ref[sl, :].astype(f32), 0.0), axis=1, keepdims=True)
            l0, l1, l2 = split3(-lse)
            d0, d1, d2 = split3(-dd)
            qx = jnp.where(mine_q, q, jnp.where(lane_q == e, l0, jnp.where(lane_q == e + 1, l1, jnp.where(
                lane_q == e + 2, l2, jnp.where(lane_q == e + 3, 1.0, 0.0))))).astype(bf16)
            gx = jnp.where(mine_q, g, jnp.where(lane_q == e, d0, jnp.where(lane_q == e + 1, d1, jnp.where(
                lane_q == e + 2, d2, 0.0)))).astype(bf16)
            pt = jnp.exp2(dot(kx, qx, NT))
            dst = (pt * dot(vx, gx, NT)).astype(bf16)
            dv = dv + dot(pt.astype(bf16), gb)
            dk = dk + dot(dst, qb)
            dqt = dot(kt, dst)
            if h == 0:
                dqs[:, sl] = dqt
            else:
                dqs[:, sl] = dqs[:, sl] + dqt
        dks.append(dk)
        dvs.append(dv)
    cos, sin = cos_ref[...], sin_ref[...]
    dq = dqs[...].T * (HD ** -0.5)
    dk = jnp.where(lane < HD, dks[0], dks[1]) * (1.0 / LOG2E)
    dq_ref[...] = (dq * cos - swap_halves(dq) * sin).astype(bf16)
    dk_ref[...] = (dk * cos - swap_halves(dk) * sin).astype(bf16)
    dv_ref[...] = jnp.where(lane < HD, dvs[0], dvs[1]).astype(bf16)

def attn_bwd_call(length, qkv, att, gatt, lse, cos, sin, rows=256):
    s, d3 = qkv.shape
    d = d3 // 3
    np_ = d // 128
    col = pl.BlockSpec((s, 128), lambda i: (0, i))
    const = pl.BlockSpec((s, 128), lambda i: (0, 0))
    return pl.pallas_call(
        functools.partial(attn_bwd_kernel, rows=rows), grid=(np_,),
        in_specs=[pl.BlockSpec(memory_space=pltpu.SMEM), col,
                  pl.BlockSpec((s, 128), lambda i: (0, np_ + i)),
                  pl.BlockSpec((s, 128), lambda i: (0, 2 * np_ + i)), col, col, const, const, const],
        out_specs=[col, col, col],
        out_shape=[jax.ShapeDtypeStruct((s, d), bf16)] * 3,
        scratch_shapes=[pltpu.VMEM((128, s), f32)],
        cost_estimate=pl.CostEstimate(flops=20 * s * s * d, bytes_accessed=16 * s * d, transcendentals=s * s * 12),
        name="attn_bwd")(length, qkv, qkv, qkv, att, gatt, lse, cos, sin)

def gelu_both(v):
    a, b = 0.7978845608028654, 0.044715
    v2 = v * v
    t = jnp.tanh(a * v * (1.0 + b * v2))
    half = 0.5 + 0.5 * t
    return v * half, half + (0.5 * a) * v * (1.0 - t * t) * (1.0 + 3.0 * b * v2)

def colsum(x):
    return jnp.sum(x, axis=0, keepdims=True)

def mid_kernel(len_ref, att_ref, tok_ref, flag_ref, cot_ref, vec_ref, b1_ref, wo_ref, w1_ref, w2_ref,
               out_ref, gh1_ref, gatt_ref, n2_ref, act_ref, gm_ref, gpre_ref, gap_ref, sum_ref, sb1_ref,
               gp_s, *, cut):
    i = pl.program_id(0)
    rows, d = att_ref.shape
    ff = w1_ref.shape[1]
    emb, gain, scale, shift, gate_a, gate_m, b2 = (vec_ref[r:r + 1, :] for r in range(7))
    h0 = jnp.where(flag_ref[...] == 1, emb, tok_ref[...].astype(f32))
    ap = dot(att_ref[...], wo_ref[...])
    br_a = gate_a * ap
    h1 = h0 + br_a
    n, rs = norm_parts(h1)
    n2 = (n * gain * (1.0 + scale) + shift).astype(bf16)
    n2_ref[...] = n2
    mp = jnp.zeros((rows, d), f32) + b2
    for j in range(ff // cut):
        sl = slice(j * cut, (j + 1) * cut)
        act, gp = gelu_both(dot(n2, w1_ref[:, sl]) + b1_ref[:, sl])
        act = act.astype(bf16)
        act_ref[:, sl] = act
        gp_s[:, sl] = gp
        mp = mp + dot(act, w2_ref[sl, :])
    br_m = gate_m * mp
    bo = h1 + br_m
    out_ref[...] = bo.astype(bf16)
    pos = lax.broadcasted_iota(jnp.int32, (rows, 1), 0) + i * rows
    valid = jnp.where(pos < len_ref[0], 1.0, 0.0)
    cot = cot_ref[...].astype(f32)
    gm = (gate_m * cot).astype(bf16)
    gm_ref[...] = gm
    gn2 = jnp.zeros((rows, d), f32)
    sb1 = []
    for j in range(ff // cut):
        sl = slice(j * cut, (j + 1) * cut)
        gpre = (dot(gm, w2_ref[sl, :], NT) * gp_s[:, sl]).astype(bf16)
        gpre_ref[:, sl] = gpre
        sb1.append(colsum(gpre.astype(f32)))
        gn2 = gn2 + dot(gpre, w1_ref[:, sl], NT)
    e = gn2 * (gain * (1.0 + scale))
    gh1 = cot + rs * (e - jnp.mean(e, axis=1, keepdims=True) - n * jnp.mean(e * n, axis=1, keepdims=True))
    gh1_ref[...] = gh1
    gap = (gate_a * gh1).astype(bf16)
    gap_ref[...] = gap
    gatt_ref[...] = dot(gap, wo_ref[...], NT).astype(bf16)
    new = jnp.concatenate([
        colsum(cot * mp), colsum(gm.astype(f32)), colsum(gn2 * n), colsum(gn2), colsum(gh1 * ap),
        colsum(valid * bo * bo), colsum(valid * br_a * br_a), colsum(valid * br_m * br_m)], axis=0)
    sb1 = jnp.concatenate(sb1, axis=1)
    @pl.when(i == 0)
    def _():
        sum_ref[...] = new
        sb1_ref[...] = sb1
    @pl.when(i > 0)
    def _():
        sum_ref[...] += new
        sb1_ref[...] += sb1

def mid_call(length, att, tok, flag, cot, vec, b1, wo, w1, w2, rows=256, cut=768):
    s, d = tok.shape
    ff = w1.shape[1]
    row = lambda c: pl.BlockSpec((rows, c), lambda i: (i, 0))
    whole = lambda a: pl.BlockSpec(a.shape, lambda i: (0, 0))
    sd = jax.ShapeDtypeStruct
    return pl.pallas_call(
        functools.partial(mid_kernel, cut=cut), grid=(s // rows,),
        in_specs=[pl.BlockSpec(memory_space=pltpu.SMEM), row(d), row(d), row(1), row(d), whole(vec), whole(b1),
                  whole(wo), whole(w1), whole(w2)],
        out_specs=[row(d), row(d), row(d), row(d), row(ff), row(d), row(ff), row(d),
                   pl.BlockSpec((8, d), lambda i: (0, 0)), pl.BlockSpec((1, ff), lambda i: (0, 0))],
        out_shape=[sd((s, d), bf16), sd((s, d), f32), sd((s, d), bf16), sd((s, d), bf16), sd((s, ff), bf16),
                   sd((s, d), bf16), sd((s, ff), bf16), sd((s, d), bf16), sd((8, d), f32), sd((1, ff), f32)],
        scratch_shapes=[pltpu.VMEM((rows, ff), f32)],
        compiler_params=pltpu.CompilerParams(vmem_limit_bytes=60000 * 1024),
        cost_estimate=pl.CostEstimate(flops=2 * s * d * (2 * d + 4 * ff), bytes_accessed=30 * s * d,
                                      transcendentals=s * ff),
        name="mid")(length, att, tok, flag, cot, vec, b1, wo, w1, w2)

def post_kernel(dq_ref, dk_ref, dv_ref, tok_ref, flag_ref, gh1_ref, vec_ref, w_ref, ig_ref, sum_ref):
    i = pl.program_id(0)
    d = tok_ref.shape[1]
    emb, gain, scale = (vec_ref[r:r + 1, :] for r in range(3))
    masked = flag_ref[...] == 1
    h0 = jnp.where(masked, emb, tok_ref[...].astype(f32))
    n, rs = norm_parts(h0)
    gn1 = dot(dq_ref[...], w_ref[:, :d], NT) + dot(dk_ref[...], w_ref[:, d:2 * d], NT) + dot(
        dv_ref[...], w_ref[:, 2 * d:], NT)
    e = gn1 * (gain * (1.0 + scale))
    gh0 = gh1_ref[...] + rs * (e - jnp.mean(e, axis=1, keepdims=True) - n * jnp.mean(e * n, axis=1, keepdims=True))
    ig_ref[...] = jnp.where(masked, 0.0, gh0).astype(bf16)
    zero = jnp.zeros((5, d), f32)
    new = jnp.concatenate([colsum(gn1 * n), colsum(gn1), colsum(jnp.where(masked, gh0, 0.0)), zero], axis=0)
    @pl.when(i == 0)
    def _():
        sum_ref[...] = new
    @pl.when(i > 0)
    def _():
        sum_ref[...] += new

def post_call(dq, dk, dv, tok, flag, gh1, vec, w, rows=256):
    s, d = tok.shape
    row = lambda c: pl.BlockSpec((rows, c), lambda i: (i, 0))
    whole = lambda a: pl.BlockSpec(a.shape, lambda i: (0, 0))
    sd = jax.ShapeDtypeStruct
    return pl.pallas_call(
        post_kernel, grid=(s // rows,),
        in_specs=[row(d), row(d), row(d), row(d), row(1), row(d), whole(vec), whole(w)],
        out_specs=[row(d), pl.BlockSpec((8, d), lambda i: (0, 0))],
        out_shape=[sd((s, d), bf16), sd((8, d), f32)],
        cost_estimate=pl.CostEstimate(flops=6 * s * d * d, bytes_accessed=16 * s * d, transcendentals=0),
        name="post")(dq, dk, dv, tok, flag, gh1, vec, w)

def wgrad_kernel(a_ref, b_ref, o_ref):
    o_ref[...] = dot(a_ref[...], b_ref[...], TN).astype(bf16)

def wgrad_call(a, b, cols=768, bcols=768):
    s, m = a.shape
    n = b.shape[1]
    return pl.pallas_call(
        wgrad_kernel, grid=(m // cols, n // bcols),
        in_specs=[pl.BlockSpec((s, cols), lambda i, j: (0, i)), pl.BlockSpec((s, bcols), lambda i, j: (0, j))],
        out_specs=pl.BlockSpec((cols, bcols), lambda i, j: (i, j)),
        out_shape=jax.ShapeDtypeStruct((m, n), bf16),
        cost_estimate=pl.CostEstimate(flops=2 * s * m * n, bytes_accessed=2 * (s * (m + n) + m * n),
                                      transcendentals=0),
        name="wgrad")(a, b)
from jax.sharding import PartitionSpec as P

highest = lax.Precision.HIGHEST


def rotary_tables(length):
    half = HD // 2
    rate = 1.0 / 10000.0 ** (jnp.arange(half, dtype=f32) * 2.0 / HD)
    angle = jnp.arange(length, dtype=f32)[:, None] * rate[None, :]
    angle = jnp.concatenate([angle] * (128 // half), axis=-1)
    sign = jnp.where(jnp.arange(128) % HD < half, -1.0, 1.0)
    return jnp.cos(angle), jnp.sin(angle) * sign


def per_device(shape, tokens, hidden_token_indicator, lengths, time_ids, cotangent, gain_one, w_qkv, w_out, gain_two,
               w_fc1, b_fc1, w_fc2, b_fc2, w_ada, b_ada, mask_embed, time_table):
    groups = shape["fsdp"]
    s, d = tokens.shape[1:]
    ff = b_fc1.shape[0] * groups
    gather = lambda w: lax.all_gather(w, "fsdp", axis=0, tiled=True)
    tok, cot = tokens[0], cotangent[0]
    flag = hidden_token_indicator.reshape(s, 1)
    sizes = [v.shape[0] for v in (gain_one, gain_two, b_fc2, mask_embed, b_fc1, b_ada)]
    packed = gather(jnp.concatenate([gain_one, gain_two, b_fc2, mask_embed, b_fc1, b_ada])[None])
    cuts = [sum(sizes[:i]) for i in range(len(sizes) + 1)]
    gain1, gain2, b2, emb, b1, bada = (
        packed[:, cuts[i]:cuts[i + 1]].reshape(1, -1).astype(f32) for i in range(len(sizes)))
    ada_all, qkv_all, out_all, fc1_all, fc2_all = (gather(w) for w in (w_ada, w_qkv, w_out, w_fc1, w_fc2))
    cond_pre = lax.dynamic_slice_in_dim(time_table, time_ids[0], 1, axis=0)
    cond = jax.nn.silu(cond_pre)
    modulation = jnp.dot(cond, ada_all.astype(f32).T, precision=highest) + bada
    shift_a, scale_a, gate_a, shift_m, scale_m, gate_m = (modulation[:, i * d:(i + 1) * d] for i in range(6))
    cos, sin = rotary_tables(s)
    zero = jnp.zeros((1, d), f32)
    vec_pre = jnp.concatenate([emb, gain1, scale_a, shift_a] + [zero] * 4, axis=0)
    vec_mid = jnp.concatenate([emb, gain2, scale_m, shift_m, gate_a, gate_m, b2, zero], axis=0)
    n1, qkv = pre_call(tok, flag, vec_pre, qkv_all, cos, sin)
    att, lse = attn_fwd_call(lengths, qkv)
    out, gh1, gatt, n2, act, gm, gpre, gap, sums, gb1 = mid_call(
        lengths, att, tok, flag, cot, vec_mid, b1, out_all, fc1_all, fc2_all)
    g_fc2 = wgrad_call(act, gm)
    g_fc1 = wgrad_call(n2, gpre)
    g_out = wgrad_call(att, gap)
    dq, dk, dv = attn_bwd_call(lengths, qkv, att, gatt, lse, cos, sin)
    g_qkv = jnp.concatenate([wgrad_call(n1, x) for x in (dq, dk, dv)], axis=1)
    igrad, sums1 = post_call(dq, dk, dv, tok, flag, gh1, vec_pre, qkv_all)
    ggm, gb2, a2, s2, gga, st0, st1, st2 = (sums[i:i + 1] for i in range(8))
    a1, s1, gemb = (sums1[i:i + 1] for i in range(3))
    gmod = jnp.concatenate([s1, a1 * gain1, gga, s2, a2 * gain2, ggm], axis=1)
    small = jnp.concatenate([(1.0 + scale_a) * a1, (1.0 + scale_m) * a2, gb2, gemb, gb1, gmod], axis=1)
    stats = jnp.concatenate([jnp.sum(st0).reshape(1, 1), jnp.sum(st1).reshape(1, 1), jnp.sum(st2).reshape(1, 1),
                             lengths.astype(f32).reshape(1, 1), time_ids.astype(f32).reshape(1, 1)], axis=1)
    row = jnp.concatenate([small, cond_pre, stats, jnp.zeros((1, 123), f32)], axis=1)
    rows = lax.all_gather(row, ("dp", "fsdp"), axis=0, tiled=True)
    width = small.shape[1]
    conds, tail = rows[:, width:width + cond.shape[1]], rows[:, width + cond.shape[1]:]
    gmods = rows[:, width - gmod.shape[1]:width]
    silu_c, pull = jax.vjp(jax.nn.silu, conds)
    grad_cond = pull(jnp.dot(gmods, ada_all.astype(f32), precision=highest))[0]
    hot = (jnp.arange(time_table.shape[0])[:, None] == tail[:, 4].astype(jnp.int32)[None, :]).astype(f32)
    table = jnp.dot(hot, grad_cond, precision=highest)
    totals = jnp.sum(tail[:, :4], axis=0)
    rms = jnp.sqrt(totals[:3] / (totals[3] * d))
    me = lax.axis_index("fsdp")
    parts, base = [], 0
    for size in sizes:
        parts.append(jnp.sum(lax.dynamic_slice_in_dim(rows, base + me * size, size, axis=1), axis=0))
        base += size * groups
    g1, g2, gb2, gemb, gb1, gbada = parts
    n_ada = w_ada.shape[0]
    mods = lax.dynamic_slice_in_dim(rows, width - gmod.shape[1] + me * n_ada, n_ada, axis=1)
    g_ada = lax.dot_general(mods, silu_c, (((0,), (0,)), ((), ())), precision=highest)

    def reduce(g):
        part = lax.psum_scatter(g, "fsdp", scatter_dimension=0, tiled=True)
        return lax.psum(part, "dp").astype(f32)

    return (out[None], igrad[None], g1, reduce(g_qkv), reduce(g_out), g2, reduce(g_fc1), gb1, reduce(g_fc2), gb2,
            g_ada, gbada, gemb, table, rms)


def solution(mesh):
    both = ("dp", "fsdp")
    f1, f2 = P("fsdp"), P("fsdp", None)
    placed = (P(both, None, None), P(both, None), P(both), P(both), P(both, None, None), f1, f2, f2, f1, f2, f1, f2, f1,
              f2, f1, f1, P())
    outs = (P(both, None, None), P(both, None, None), f1, f2, f2, f1, f2, f1, f2, f1, f2, f1, f1, P(), P())
    return jax.shard_map(functools.partial(per_device, dict(mesh.shape)), mesh=mesh, in_specs=placed, out_specs=outs,
                         check_vma=False)
```

time: 1010 us -> 657 us (0.65); the launches traced: 996 us -> 656 us
  matrix products: 335 us -> 6.2 us
  Pallas kernels: 0 us -> 158 us
  waiting for transfers between devices: 328 us -> 437 us
  other arithmetic: 112 us -> 20.2 us
  blocking collectives: 101 us -> 9.75 us
  local copies, waits for them, and re-layouts: 63.1 us -> 8.2 us
  loops' own time: 35.7 us -> 0 us
    dot_general x99 -> x4, matrix products: 335 us -> 6.2 us  [the longest x1 2.3 us: per_device(): modulation = jnp.dot(cond, ada_all.astype(f32).T, precision=highest) + bada]
    all_gather x5 -> x6, waiting for transfers between devices: 24.2 us -> 227 us  [the longest x5 169 us: per_device(): gather = lambda w: lax.all_gather(w, 'fsdp', axis=0, tiled=True)]
    pallas_call x0 -> x11, Pallas kernels: none -> 158 us  [the longest x1 37.7 us: mid_call(): pl.pallas_call(functools.partial(mid_kernel, cut=cut), grid=(s // rows,),...]
    psum x2 -> x1, waiting for transfers between devices: 133 us -> 73.4 us  [reduce(): return lax.psum(part, 'dp').astype(f32)]
    psum x2 -> x0, blocking collectives: 55.5 us -> none  [the longest x1 40.6 us: per_device(): table_sum, stat_sum = lax.psum((grad_table, stat_terms), ('dp', 'fsdp'))]
    convert_element_type x33 -> x7, other arithmetic: 43.1 us -> 7.04 us  [the longest x4 6.78 us: reduce(): return lax.psum(part, 'dp').astype(f32)]
    another operation x2 -> x0, loops' own time: 35.7 us -> none  [the longest x1 27 us: per_device(): lax.map(head_backward, jnp.arange(head_count))]
    reduce_scatter x5 -> x4, waiting for transfers between devices: 168 us -> 133 us  [reduce(): part = lax.psum_scatter(g, 'fsdp', scatter_dimension=0, tiled=True)]
  transfers between devices with their start and end apart: 12 -> 11, of which waited for: 6 -> 9; matrix products, arithmetic and copies ran while one was open for 46% -> 4% of each run, Pallas kernels for 0% -> 18%
where the time goes in v1:
time: 657 us; the launch traced here: 656 us
  waiting for transfers between devices  437 us (67%)
  Pallas kernels  158 us (24%)
  other arithmetic  20.2 us (3%)
  between operations  16.1 us (2%)
  blocking collectives  9.75 us (1%)
  local copies, waits for them, and re-layouts  8.2 us (1%)
    all_gather x5, waiting for transfers between devices, per_device(): gather = lambda w: lax.all_gather(w, 'fsdp', axis=0, tiled=True)  169 us
    reduce_scatter x4, waiting for transfers between devices, reduce(): part = lax.psum_scatter(g, 'fsdp', scatter_dimension=0, tiled=True)  133 us
    psum x1, waiting for transfers between devices, reduce(): return lax.psum(part, 'dp').astype(f32)  73.4 us
    all_gather x1, waiting for transfers between devices, per_device(): rows = lax.all_gather(row, ('dp', 'fsdp'), axis=0, tiled=True)  57.9 us
    pallas_call x1, Pallas kernels, mid_call(): pl.pallas_call(functools.partial(mid_kernel, cut=cut), grid=(s // rows,),...  37.7 us
    pallas_call x1, Pallas kernels, attn_bwd_call(): pl.pallas_call(functools.partial(attn_bwd_kernel, rows=rows), grid=(np_,)...  37.5 us
    pallas_call x6, Pallas kernels, wgrad_call(): pl.pallas_call(wgrad_kernel, grid=(m // cols, n // bcols), in_specs=[pl.B...  36.2 us
    pallas_call x1, Pallas kernels, attn_fwd_call(): pl.pallas_call(functools.partial(attn_fwd_kernel, rows=rows), grid=(np_,)...  26.5 us
  transfers between devices with their start and end apart: 11, of which 9 were waited for; matrix products, arithmetic and copies ran while one was open for 4% of the time, Pallas kernels for 18%

profile of v1, /device:TPU:0, one launch (start us, length us, event | category | flops | bytes accessed | tf_op | source)
XLA Modules:
  0.0 656.1 jit_solution(2403546746642802121)
XLA Ops:
  11.5 9.8 %all-gather.1 = bf16[4,1,2688]{2,1,0:T(2,128)(2,1)S(1)} all-gather(bf16[1,1,2688]{2,1,0:T(2,128)(2,1)S(1)} %reshape.172), channel_id=2, replica_groups=mesh['dp'=8,'fsdp'=4] {'fsdp'}, dimensions={0}, use_global_device_ids=true | all-gather | bytes 26880 | tf_op jit(solution)/shard_map/all_gather | solution.py:341
  24.2 3.0 sine_multiply_fusion
  27.2 13.0 %all-gather.10.cloned.1.call-done = bf16[4608,128]{1,0:T(8,128)(2,1)} async-done(((bf16[1152,128]{1,0:T(8,128)(2,1)}), bf16[4608,128]{1,0:T(8,128)(2,1)}) %all-gather.10.cloned.1.call-update) | async-done | bytes 1179664 | tf_op jit(solution)/shard_map/all_gather | solution.py:341
  40.2 2.3 convolution_reduce_fusion
  43.9 45.3 %all-gather.12.cloned.1.call-done.w_ref = bf16[768,2304]{1,0:T(8,128)(2,1)} async-done(((bf16[192,2304]{1,0:T(8,128)(2,1)}), bf16[768,2304]{1,0:T(8,128)(2,1)}) %all-gather.12.cloned.1.call-update) | async-done | bytes 3538960 | tf_op jit(solution)/shard_map/all_gather | solution.py:341
  89.2 9.6 %pre.1 = (bf16[1024,768]{1,0:T(8,128)(2,1)}, bf16[1024,2304]{1,0:T(8,128)(2,1)}) custom-call(bf16[1024,768]{1,0:T(8,128)(2,1)} %bitcast.40, s32[1024,1]{1,0:T(8,128)} %copy.38.flag_ref, f32[8,768]{1,0:T(8,128)} %concatenate.23.vec_ref, bf16[768,2304]{1,0:T(8,128)(2,1)} %all-gather.12.cloned.1.call-done.w_ref, f32[1024,128]{1,0:T(8,128)} %get-tuple-element.67.cos_ref, ...), custom_call_target="tpu_custom_call" | custom-call | flops 3623878656 | bytes 9437184 | tf_op jit(solution)/shard_map/pre/pallas_call | solution.py:50
  98.8 26.5 %attn_fwd.1 = (bf16[1024,768]{1,0:T(8,128)(2,1)}, f32[1024,128]{1,0:T(8,128)}) custom-call(s32[1]{0:T(128)S(6)} %copy.57.len_ref, bf16[1024,2304]{1,0:T(8,128)(2,1)} %get-tuple-element.34.q_ref.k_ref.v_ref, bf16[1024,2304]{1,0:T(8,128)(2,1)} %get-tuple-element.34.q_ref.k_ref.v_ref, bf16[1024,2304]{1,0:T(8,128)(2,1)} %get-tuple-element.34.q_ref.k_ref.v_ref), custom_call_target="tpu_custom_call" | custom-call | flops 6442450944 | bytes 6291456 | tf_op jit(solution)/shard_map/attn_fwd/pallas_call | solution.py:99
  125.3 52.0 %all-gather.16.cloned.1.call-done.w1_ref = bf16[768,3072]{1,0:T(8,128)(2,1)} async-done(((bf16[192,3072]{1,0:T(8,128)(2,1)}), bf16[768,3072]{1,0:T(8,128)(2,1)}) %all-gather.16.cloned.1.call-update) | async-done | bytes 4718608 | tf_op jit(solution)/shard_map/all_gather | solution.py:341
  177.4 58.7 %all-gather.18.cloned.1.call-done.w2_ref = bf16[3072,768]{1,0:T(8,128)(2,1)} async-done(((bf16[768,768]{1,0:T(8,128)(2,1)}), bf16[3072,768]{1,0:T(8,128)(2,1)}) %all-gather.18.cloned.1.call-update) | async-done | bytes 4718608 | tf_op jit(solution)/shard_map/all_gather | solution.py:341
  236.0 37.7 %mid.1 = (bf16[1024,768]{1,0:T(8,128)(2,1)}, f32[1024,768]{1,0:T(8,128)}, bf16[1024,768]{1,0:T(8,128)(2,1)}, bf16[1024,768]{1,0:T(8,128)(2,1)}, bf16[1024,3072]{...) custom-call(s32[1]{0:T(128)S(6)} %copy.57.len_ref, ...), custom_call_target="tpu_custom_call" | custom-call | flops 21743271936 | bytes 23592960 | tf_op jit(solution)/shard_map/mid/pallas_call | solution.py:260
  273.7 4.3 wgrad.9
  278.1 37.5 %attn_bwd.1 = (bf16[1024,768]{1,0:T(8,128)(2,1)}, bf16[1024,768]{1,0:T(8,128)(2,1)}, bf16[1024,768]{1,0:T(8,128)(2,1)}) custom-call(s32[1]{0:T(128)S(6)} %copy.57.len_ref, bf16[1024,2304]{1,0:T(8,128)(2,1)} %get-tuple-element.34.q_ref.k_ref.v_ref, bf16[1024,2304]{1,0:T(8,128)(2,1)} %get-tuple-element.34.q_ref.k_ref.v_ref, ...), custom_call_target="tpu_custom_call" | custom-call | flops 16106127360 | bytes 12582912 | tf_op jit(solution)/shard_map/attn_bwd/pallas_call | solution.py:176
  315.6 4.3 wgrad.6
  319.9 4.3 wgrad.7
  324.3 4.5 wgrad.8
  328.7 2.9 pad_maximum_fusion
  331.7 9.2 %wgrad.11 = bf16[3072,768]{1,0:T(8,128)(2,1)} custom-call(bf16[1024,3072]{1,0:T(8,128)(2,1)} %get-tuple-element.51.a_ref, bf16[1024,768]{1,0:T(8,128)(2,1)} %get-tuple-element.52.b_ref), custom_call_target="tpu_custom_call" | custom-call | flops 4831838208 | bytes 12582912 | tf_op jit(solution)/shard_map/wgrad/pallas_call | solution.py:314
  341.0 9.5 %wgrad.10 = bf16[768,3072]{1,0:T(8,128)(2,1)} custom-call(bf16[1024,768]{1,0:T(8,128)(2,1)} %get-tuple-element.49.a_ref, bf16[1024,3072]{1,0:T(8,128)(2,1)} %get-tuple-element.50.b_ref), custom_call_target="tpu_custom_call" | custom-call | flops 4831838208 | bytes 12582912 | tf_op jit(solution)/shard_map/wgrad/pallas_call | solution.py:314
  350.6 10.6 %post.1 = (bf16[1024,768]{1,0:T(8,128)(2,1)}, f32[8,768]{1,0:T(8,128)}) custom-call(bf16[1024,768]{1,0:T(8,128)(2,1)} %get-tuple-element.39.dq_ref.b_ref, bf16[1024,768]{1,0:T(8,128)(2,1)} %get-tuple-element.40.dk_ref.b_ref, bf16[1024,768]{1,0:T(8,128)(2,1)} %get-tuple-element.41.dv_ref.b_ref, bf16[1024,768]{1,0:T(8,128)(2,1)} %bitcast.42, ...), custom_call_target="tpu_custom_call" | custom-call | flops 3623878656 | bytes 12582912 | tf_op jit(solution)/shard_map/post/pallas_call | solution.py:300
  362.8 2.7 concatenate.26
  365.5 13.5 %reduce-scatter.5.cloned.1.call-done = bf16[192,2304]{1,0:T(8,128)(2,1)} async-done(((bf16[768,2304]{1,0:T(8,128)(2,1)}), bf16[192,2304]{1,0:T(8,128)(2,1)}) %reduce-scatter.5.cloned.1.call-update) | async-done | bytes 884752 | tf_op jit(solution)/shard_map/reduce_scatter | solution.py:396
  379.0 60.0 %reduce-scatter.11.cloned.1.call-done = bf16[768,768]{1,0:T(8,128)(2,1)} async-done(((bf16[3072,768]{1,0:T(8,128)(2,1)}), bf16[768,768]{1,0:T(8,128)(2,1)}) %reduce-scatter.11.cloned.1.call-update) | async-done | bytes 1179664 | tf_op jit(solution)/shard_map/reduce_scatter | solution.py:396
  439.0 60.0 %reduce-scatter.9.cloned.1.call-done = bf16[192,3072]{1,0:T(8,128)(2,1)} async-done(((bf16[768,3072]{1,0:T(8,128)(2,1)}), bf16[192,3072]{1,0:T(8,128)(2,1)}) %reduce-scatter.9.cloned.1.call-update) | async-done | bytes 1179664 | tf_op jit(solution)/shard_map/reduce_scatter | solution.py:396
  499.0 57.9 %all-gather.20.cloned.1.call-done = f32[32,1,11008]{2,1,0:T(1,128)} async-done(((f32[1,1,11008]{2,1,0:T(1,128)}), f32[32,1,11008]{2,1,0:T(1,128)}) %all-gather.20.cloned.1.call-update) | async-done | bytes 1409040 | tf_op jit(solution)/shard_map/all_gather | solution.py:375
  556.9 1.4 copy.51
  559.6 1.6 dynamic-slice_reduce_fusion
  561.2 1.8 dynamic-slice_reduce_fusion.1
  563.1 1.7 fusion.26
  567.4 1.9 fusion.5
  569.3 73.4 %all-reduce.3.cloned.1.call-done = (bf16[192,2304]{1,0:T(8,128)(2,1)}, bf16[192,768]{1,0:T(8,128)(2,1)}, bf16[192,3072]{1,0:T(8,128)(2,1)}, bf16[768,768]{1,0:T(8,128)(2,1)}) async-done(((bf16[192,2304]{1,0:T(8,128)(2,1)}, bf16[192,768]{1,0:T(8,128)(2,1)}, bf16[192,3072]{1,0:T(8,128)(2,1)}, bf16[768,768]{1,0:T(8,128)(2,1)}), (bf16[192,2304]{1,0:T(8,128)(2,1)}, bf16[192,768]{1,0:T(8,128)(2,1)}, ...) | async-done | bytes 3538960 | tf_op jit(solution)/shard_map/psum | solution.py:397
  642.7 3.0 convert_element_type.115
  645.8 1.6 convert_element_type.116
  (93 shorter events, 14.4 us)
Async XLA Ops:
  7.2 16.9 %copy-start = (f32[1000,128]{1,0:T(8,128)S(1)}, f32[1000,128]{1,0:T(8,128)}, u32[]{:S(2)}) copy-start(f32[1000,128]{1,0:T(8,128)} %param.33) | copy-start | bytes 1536004
  7.2 33.0 %all-gather.10.cloned.1.call-start = ((), (), s32[]{:S(2)}) async-start(), calls=%async_computation.4 | async-start | bytes 1474560 | tf_op jit(solution)/shard_map/all_gather | solution.py:341
  7.9 3.4 copy-start.11
  7.9 3.4 copy-start.12
  8.0 3.4 copy-start.13
  8.0 3.4 copy-start.14
  8.0 3.4 copy-start.15
  8.0 3.4 copy-start.16
  8.0 81.2 %all-gather.12.cloned.1.call-start = ((), (), s32[]{:S(2)}) async-start(), calls=%async_computation.5 | async-start | bytes 4423680 | tf_op jit(solution)/shard_map/all_gather | solution.py:341
  8.7 13.0 %copy-start.10 = (s32[1,1024]{1,0:T(1,128)S(1)}, s32[1,1024]{1,0:T(1,128)}, u32[]{:S(2)}) copy-start(s32[1,1024]{1,0:T(1,128)} %param.18) | copy-start | bytes 12292
  8.8 116.6 %all-gather.14.cloned.1.call-start = ((), (), s32[]{:S(2)}) async-start(), calls=%async_computation.6 | async-start | bytes 1474560 | tf_op jit(solution)/shard_map/all_gather | solution.py:341
  9.5 167.9 %all-gather.16.cloned.1.call-start = ((), (), s32[]{:S(2)}) async-start(), calls=%async_computation.7 | async-start | bytes 5898240 | tf_op jit(solution)/shard_map/all_gather | solution.py:341
  10.1 226.0 %all-gather.18.cloned.1.call-start = ((), (), s32[]{:S(2)}) async-start(), calls=%async_computation.8 | async-start | bytes 5898240 | tf_op jit(solution)/shard_map/all_gather | solution.py:341
  10.7 354.9 %reduce-scatter.7.cloned.1.call-start = ((), (), s32[]{:S(2)}) async-start(), calls=%async_computation.10 | async-start | bytes 1474560 | tf_op jit(solution)/shard_map/reduce_scatter | solution.py:396
  278.1 100.9 %reduce-scatter.5.cloned.1.call-start = ((), (), s32[]{:S(2)}) async-start(), calls=%async_computation.9 | async-start | bytes 4423680 | tf_op jit(solution)/shard_map/reduce_scatter | solution.py:396
  324.3 4.5 copy-start.4
  324.3 4.5 copy-start.5
  331.7 107.3 %reduce-scatter.11.cloned.1.call-start = ((), (), s32[]{:S(2)}) async-start(), calls=%async_computation.12 | async-start | bytes 5898240 | tf_op jit(solution)/shard_map/reduce_scatter | solution.py:396
  341.0 158.0 %reduce-scatter.9.cloned.1.call-start = ((), (), s32[]{:S(2)}) async-start(), calls=%async_computation.11 | async-start | bytes 5898240 | tf_op jit(solution)/shard_map/reduce_scatter | solution.py:396
  350.6 206.4 %all-gather.20.cloned.1.call-start = ((), (), s32[]{:S(2)}) async-start(), calls=%async_computation.13 | async-start | bytes 1453056 | tf_op jit(solution)/shard_map/all_gather | solution.py:375
  350.6 11.5 %copy-start.8 = (f32[8,768]{1,0:T(8,128)S(1)}, f32[8,768]{1,0:T(8,128)}, u32[]{:S(2)}) copy-start(f32[8,768]{1,0:T(8,128)} %get-tuple-element.45) | copy-start | bytes 73732
  350.6 12.2 %copy-start.9 = (f32[1,3072]{1,0:T(1,128)S(1)}, f32[1,3072]{1,0:T(1,128)}, u32[]{:S(2)}) copy-start(f32[1,3072]{1,0:T(1,128)} %get-tuple-element.46) | copy-start | bytes 36868
  365.5 277.3 %all-reduce.3.cloned.1.call-start = ((), (), s32[]{:S(2)}) async-start(), calls=%async_computation.14 | async-start | bytes 7077888 | tf_op jit(solution)/shard_map/psum | solution.py:397
  499.0 66.4 %copy-start.2 = (bf16[4608,128]{1,0:T(8,128)(2,1)S(1)}, bf16[4608,128]{1,0:T(8,128)(2,1)}, u32[]{:S(2)}) copy-start(bf16[4608,128]{1,0:T(8,128)(2,1)} %all-gather.10.cloned.1.call-done) | copy-start | bytes 3538948
  642.7 3.0 copy-start.3
  645.8 1.6 copy-start.6
  647.3 1.3 copy-start.7
  647.4 2.2 copy-start.1
Sparse Core Ops, SparseCore 0:
  9.8 30.3 all-gather.9
  42.1 47.1 all-gather.11
  91.1 27.5 all-gather.13
  120.4 56.9 all-gather.15
  179.0 56.9 all-gather.17
  278.2 28.6 reduce-scatter.6
  331.8 47.1 reduce-scatter.4
  382.0 56.9 reduce-scatter.10
  442.0 56.9 reduce-scatter.8
  502.3 54.5 all-gather.19
  559.6 83.1 all-reduce.2

commit v2 on v1

--- a/solution.py
+++ b/solution.py
@@ -319,6 +319,486 @@
         cost_estimate=pl.CostEstimate(flops=2 * s * m * n, bytes_accessed=2 * (s * (m + n) + m * n),
                                       transcendentals=0),
         name="wgrad")(a, b)
+
+MESH = pl.DeviceIdType.MESH
+
+
+def flip(i, b):
+    return i + 2 ** b * (1 - 2 * ((i // 2 ** b) % 2))
+
+
+def xor(i, mask):
+    b = 0
+    while mask >> b:
+        if (mask >> b) & 1:
+            i = flip(i, b)
+        b += 1
+    return i
+
+
+def subsets(bits):
+    masks = [0]
+    for b in bits:
+        masks = masks + [m | (1 << b) for m in masks]
+    return masks
+
+
+def log2(n):
+    return n.bit_length() - 1
+
+
+class Place:
+    def __init__(self, shape):
+        self.groups, self.lines = shape["fsdp"], shape["dp"]
+        self.bits = log2(self.groups)
+        self.orders = [list(range(self.bits)), list(range(self.bits))[::-1]]
+        self.me = lax.axis_index("fsdp")
+        self.dp = lax.axis_index("dp")
+        self.core = self.dp % 2
+        self.partner = flip(self.dp, 0)
+
+
+def remote(src, dst, ssem, rsem, where):
+    return pltpu.make_async_remote_copy(src_ref=src, dst_ref=dst, send_sem=ssem, recv_sem=rsem, device_id=where,
+                                        device_id_type=MESH)
+
+
+class Gather:
+    def __init__(self, place, ins, outs, sems):
+        self.p, self.ins, self.outs = place, ins, outs
+        self.ss, self.rs, self.fs, self.fr, self.os, self.orr = sems
+
+    @staticmethod
+    def scratch(count, groups):
+        a = pltpu.SemaphoreType.DMA((count, 2, groups - 1))
+        b = pltpu.SemaphoreType.DMA((count,))
+        return [a, a, a, a, b, b]
+
+    def send(self, w, color, t, mask):
+        p = self.p
+        order = p.orders[color]
+        e = 2 ** t - 1 + subsets(order[:t]).index(mask)
+        piece = p.core * 2 + color
+        blk = xor(p.me, mask)
+        src = self.ins[w].at[piece] if mask == 0 else self.outs[w].at[blk, piece]
+        return remote(src, self.outs[w].at[blk, piece], self.ss.at[w, color, e], self.rs.at[w, color, e],
+                      (p.dp, flip(p.me, order[t])))
+
+    def arrival(self, w, color, t, mask):
+        p = self.p
+        order = p.orders[color]
+        e = 2 ** t - 1 + subsets(order[:t]).index(mask)
+        got = self.outs[w].at[xor(p.me, mask | (1 << order[t])), p.core * 2 + color]
+        return e, got
+
+    def landed(self, w, color, e, got):
+        return remote(got, got, self.ss.at[w, color, e], self.rs.at[w, color, e], (self.p.partner, self.p.me))
+
+    def forward(self, w, color, e, got):
+        return remote(got, got, self.fs.at[w, color, e], self.fr.at[w, color, e], (self.p.partner, self.p.me))
+
+    def own(self, w):
+        p = self.p
+        return remote(self.ins[w], self.outs[w].at[p.me], self.os.at[w], self.orr.at[w], (p.partner, p.me))
+
+    def start(self, w):
+        for t in range(self.p.bits):
+            for color in (0, 1):
+                self.send(w, color, t, 0).start()
+        self.own(w).start()
+
+    def after(self, w, t):
+        for color in (0, 1):
+            order = self.p.orders[color]
+            for mask in subsets(order[:t]):
+                e, got = self.arrival(w, color, t, mask)
+                self.landed(w, color, e, got).wait_recv()
+                for later in range(t + 1, self.p.bits):
+                    self.send(w, color, later, mask | (1 << order[t])).start()
+                self.forward(w, color, e, got).start()
+
+    def finish(self, w):
+        p = self.p
+        for color in (0, 1):
+            order = p.orders[color]
+            for t in range(p.bits):
+                for mask in subsets(order[:t]):
+                    e, got = self.arrival(w, color, t, mask)
+                    other = self.outs[w].at[xor(p.me, mask | (1 << order[t])), (1 - p.core) * 2 + color]
+                    self.forward(w, color, e, other).wait_recv()
+                    self.forward(w, color, e, got).wait_send()
+                    self.send(w, color, t, mask).wait_send()
+        self.own(w).wait()
+
+
+class Direct:
+    def __init__(self, place, src, out, sems):
+        self.p, self.src, self.out = place, src, out
+        self.ss, self.rs = sems
+
+    @staticmethod
+    def scratch(groups):
+        return [pltpu.SemaphoreType.DMA((groups,))] * 2
+
+    def copy(self, m, arrived):
+        p = self.p
+        where = (p.partner, p.me) if m == 0 else (p.dp, xor(p.me, m))
+        slot = xor(p.me, m) if arrived else p.me
+        return remote(self.src, self.out.at[slot], self.ss.at[m], self.rs.at[m], where)
+
+    def start(self):
+        for m in range(self.p.groups):
+            self.copy(m, False).start()
+
+    def finish(self):
+        for m in range(self.p.groups):
+            self.copy(m, True).wait_recv()
+            self.copy(m, False).wait_send()
+
+
+def greet(devices):
+    barrier = pltpu.get_barrier_semaphore()
+    for where in devices:
+        pl.semaphore_signal(barrier, inc=1, device_id=where, device_id_type=MESH)
+    pl.semaphore_wait(barrier, len(devices))
+
+
+def gather_peers(p, everyone):
+    masks = range(1, p.groups) if everyone else [1 << b for b in range(p.bits)]
+    return [(p.partner, p.me)] + [(p.dp, xor(p.me, m)) for m in masks]
+
+
+def quarter(w):
+    return w.reshape(4, w.shape[0] // 4, w.shape[1])
+
+
+def gather_shape(w, groups):
+    return jax.ShapeDtypeStruct((groups, 4, w.shape[0] // 4, w.shape[1]), w.dtype)
+
+
+ANY = pl.BlockSpec(memory_space=pl.ANY)
+
+
+def head_kernel(shape, count, *refs):
+    ins, small, outs, small_out = refs[:count], refs[count], refs[count + 1:2 * count + 1], refs[2 * count + 1]
+    sems = refs[2 * count + 2:]
+    p = Place(shape)
+    g = Gather(p, ins, outs, sems[:6])
+    s = Direct(p, small, small_out, sems[6:])
+    greet(gather_peers(p, True))
+    s.start()
+    for w in range(count):
+        g.start(w)
+    for t in range(p.bits):
+        for w in range(count):
+            g.after(w, t)
+    for w in range(count):
+        g.finish(w)
+    s.finish()
+
+
+def head_call(shape, small, ws):
+    groups = shape["fsdp"]
+    outs = [gather_shape(w, groups) for w in ws] + [jax.ShapeDtypeStruct((groups,) + small.shape, small.dtype)]
+    res = pl.pallas_call(
+        functools.partial(head_kernel, shape, len(ws)), in_specs=[ANY] * (len(ws) + 1), out_specs=[ANY] * len(outs),
+        out_shape=outs, scratch_shapes=Gather.scratch(len(ws), groups) + Direct.scratch(groups),
+        compiler_params=pltpu.CompilerParams(collective_id=1, has_side_effects=True), name="head",
+    )(*[quarter(w) for w in ws], small)
+    return [r.reshape(-1, r.shape[-1]) for r in res[:-1]], res[-1]
+
+
+class Reduce:
+    def __init__(self, place, counts, kinds, srcs, outs, scratch):
+        self.p, self.counts, self.kinds, self.srcs, self.outs = place, counts, kinds, srcs, outs
+        (self.own, self.cb, self.xb, self.zb, self.mb, self.u2, self.fin,
+         self.load, self.cs, self.cr, self.xs, self.xr, self.zs, self.zr, self.ms, self.mr, self.fs, self.fr,
+         self.ps, self.pr, self.st) = scratch
+        p = place
+        self.total = sum(counts)
+        self.n = p.lines // 2
+        self.zi = p.dp // 2
+        left = self.zi // (self.n // 2)
+        self.e = self.zi * (1 - left) + (self.n - 1 - self.zi) * left
+        step = 2 * (1 - 2 * left)
+        self.inner = (p.dp + step, p.me)
+        self.outer = (p.dp - step, p.me)
+        self.last = self.n // 2 - 1
+        self.stages = ([self.begin, self.core_add] + [functools.partial(self.group_add, t) for t in range(p.bits)]
+                       + [functools.partial(self.climb, j) for j in range(1, self.last + 1)] + [self.middle]
+                       + [functools.partial(self.descend, j) for j in range(self.last - 1, -1, -1)])
+        self.ticks = self.total + len(self.stages) - 1
+
+    @staticmethod
+    def scratch(total, groups, rows, cols):
+        sem = pltpu.SemaphoreType.DMA
+        vm = lambda *lead: pltpu.VMEM((total,) + lead + (rows // 2, cols), bf16)
+        one = sem((total,))
+        line = pltpu.VMEM((total, rows, cols), bf16)
+        return [vm(groups, 2), vm(groups, 2), vm(2, groups - 1), line, line, line, line,
+                one, one, one, sem((total, 2, groups - 1)), sem((total, 2, groups - 1)),
+                one, one, one, one, one, one, one, one, one]
+
+    def greet(self):
+        p = self.p
+        barrier = pltpu.get_barrier_semaphore()
+        for where in [(p.partner, p.me)] + [(p.dp, flip(p.me, b)) for b in range(p.bits)] + [self.inner]:
+            pl.semaphore_signal(barrier, inc=1, device_id=where, device_id_type=MESH)
+        @pl.when(self.e > 0)
+        def _():
+            pl.semaphore_signal(barrier, inc=1, device_id=self.outer, device_id_type=MESH)
+        half = self.n // 2
+        pl.semaphore_wait(barrier, 2 + p.bits + (self.e + half - 1) // half)
+
+    def source(self, k, fn):
+        base = 0
+        for i, count in enumerate(self.counts):
+            @pl.when((k >= base) & (k < base + count))
+            def _(i=i, base=base):
+                fn(i, k - base)
+            base += count
+
+    def target(self, i, j, core):
+        rows, cols = self.fin.shape[1:]
+        out = self.outs[i]
+        if self.kinds[i] == "cols":
+            return out.at[:, pl.ds(pl.multiple_of((2 * j + core) * cols, cols), cols)]
+        return out.at[pl.ds(pl.multiple_of(j * rows, rows), rows), pl.ds(pl.multiple_of(core * cols, cols), cols)]
+
+    def load_copy(self, k, src):
+        return pltpu.make_async_copy(src.at[self.p.core], self.own.at[k], self.load.at[k])
+
+    def core_copy(self, k, src):
+        p = self.p
+        return remote(src.at[1 - p.core], self.cb.at[k], self.cs.at[k], self.cr.at[k], (p.partner, p.me))
+
+    def begin(self, k):
+        def go(i, j):
+            self.core_copy(k, self.srcs[i].at[j]).start()
+            self.load_copy(k, self.srcs[i].at[j]).start()
+        self.source(k, go)
+
+    def slot(self, order, t, mask):
+        base = sum(self.p.groups >> (u + 1) for u in range(t))
+        return base + subsets(order[t + 1:]).index(mask)
+
+    def group_copy(self, k, color, t, mask):
+        p = self.p
+        order = p.orders[color]
+        i = self.slot(order, t, mask)
+        return remote(self.own.at[k, xor(p.me, (1 << order[t]) | mask), color], self.xb.at[k, color, i],
+                      self.xs.at[k, color, i], self.xr.at[k, color, i], (p.dp, flip(p.me, order[t])))
+
+    def group_send(self, k, t):
+        for color in (0, 1):
+            for mask in subsets(self.p.orders[color][t + 1:]):
+                self.group_copy(k, color, t, mask).start()
+
+    def core_add(self, k):
+        self.load_copy(k, self.srcs[0].at[0]).wait()
+        self.core_copy(k, self.srcs[0].at[0]).wait_recv()
+        for f in range(self.p.groups):
+            for color in (0, 1):
+                self.own[k, f, color] = (self.own[k, f, color].astype(f32) + self.cb[k, f, color].astype(f32)).astype(bf16)
+        self.group_send(k, 0)
+
+    def group_add(self, t, k):
+        p = self.p
+        for color in (0, 1):
+            order = p.orders[color]
+            for mask in subsets(order[t + 1:]):
+                self.group_copy(k, color, t, mask).wait_recv()
+                blk, i = xor(p.me, mask), self.slot(order, t, mask)
+                total = self.own[k, blk, color].astype(f32) + self.xb[k, color, i].astype(f32)
+                if t == p.bits - 1:
+                    self.u2[k, self.part(color)] = total.astype(bf16)
+                else:
+                    self.own[k, blk, color] = total.astype(bf16)
+        if t < p.bits - 1:
+            self.group_send(k, t + 1)
+        else:
+            @pl.when(self.e == 0)
+            def _():
+                (self.climb_copy(k) if self.last > 0 else self.middle_copy(k)).start()
+
+    def part(self, color):
+        half = self.u2.shape[1] // 2
+        return slice(color * half, (color + 1) * half)
+
+    def climb_copy(self, k):
+        return remote(self.u2.at[k], self.zb.at[k], self.zs.at[k], self.zr.at[k], self.inner)
+
+    def middle_copy(self, k):
+        return remote(self.u2.at[k], self.mb.at[k], self.ms.at[k], self.mr.at[k], self.inner)
+
+    def climb(self, j, k):
+        @pl.when(self.e == j)
+        def _():
+            self.climb_copy(k).wait_recv()
+            for color in (0, 1):
+                total = self.u2[k, self.part(color)].astype(f32) + self.zb[k, self.part(color)].astype(f32)
+                self.u2[k, self.part(color)] = total.astype(bf16)
+            (self.middle_copy(k) if j == self.last else self.climb_copy(k)).start()
+
+    def share_copy(self, k):
+        return remote(self.fin.at[k], self.fin.at[k], self.fs.at[k], self.fr.at[k], self.outer)
+
+    def share_wait(self, k):
+        return remote(self.fin.at[k], self.fin.at[k], self.fs.at[k], self.fr.at[k], self.inner)
+
+    def pass_copy(self, k, dst):
+        p = self.p
+        return remote(self.fin.at[k], dst, self.ps.at[k], self.pr.at[k], (p.partner, p.me))
+
+    def store_copy(self, k, dst):
+        return pltpu.make_async_copy(self.fin.at[k], dst, self.st.at[k])
+
+    def done(self, k):
+        def go(i, j):
+            self.pass_copy(k, self.target(i, j, self.p.core)).start()
+            self.store_copy(k, self.target(i, j, self.p.core)).start()
+        self.source(k, go)
+
+    def middle(self, k):
+        @pl.when(self.e == self.last)
+        def _():
+            self.middle_copy(k).wait_recv()
+            for color in (0, 1):
+                total = self.u2[k, self.part(color)].astype(f32) + self.mb[k, self.part(color)].astype(f32)
+                self.fin[k, self.part(color)] = total.astype(bf16)
+            if self.last > 0:
+                self.share_copy(k).start()
+            self.done(k)
+
+    def descend(self, j, k):
+        @pl.when(self.e == j)
+        def _():
+            self.share_wait(k).wait_recv()
+            if j > 0:
+                self.share_copy(k).start()
+            self.done(k)
+
+    def tick(self, t):
+        for s in range(len(self.stages) - 1, -1, -1):
+            k = t - s
+            @pl.when((k >= 0) & (k < self.total))
+            def _(s=s, k=k):
+                self.stages[s](k)
+
+    def drain(self):
+        p = self.p
+        @pl.loop(0, self.total)
+        def _(k):
+            self.core_copy(k, self.srcs[0].at[0]).wait_send()
+            for color in (0, 1):
+                for t in range(p.bits):
+                    for mask in subsets(p.orders[color][t + 1:]):
+                        self.group_copy(k, color, t, mask).wait_send()
+            @pl.when(self.e == self.last)
+            def _():
+                self.middle_copy(k).wait_send()
+            @pl.when(self.e < self.last)
+            def _():
+                self.climb_copy(k).wait_send()
+            @pl.when(self.e > 0)
+            def _():
+                self.share_copy(k).wait_send()
+            def go(i, j):
+                self.pass_copy(k, self.target(i, j, 1 - p.core)).wait()
+                self.store_copy(k, self.target(i, j, p.core)).wait()
+            self.source(k, go)
+
+
+def reduce_kernel(shape, counts, kinds, *refs):
+    n = len(counts)
+    r = Reduce(Place(shape), counts, kinds, refs[:n], refs[n:2 * n], refs[2 * n:])
+    r.greet()
+    @pl.loop(0, r.ticks)
+    def _(t):
+        r.tick(t)
+    r.drain()
+
+
+def reduced_shapes(grads, kinds):
+    rows, cols = 2 * grads[0].shape[-2], 2 * grads[0].shape[-1]
+    return [jax.ShapeDtypeStruct((rows, g.shape[0] * cols) if kind == "cols" else (g.shape[0] * rows, cols), bf16)
+            for g, kind in zip(grads, kinds)]
+
+
+def reduce_call(shape, grads, kinds, ident):
+    groups = shape["fsdp"]
+    counts = [g.shape[0] for g in grads]
+    rows, cols = 2 * grads[0].shape[-2], grads[0].shape[-1]
+    return pl.pallas_call(
+        functools.partial(reduce_kernel, shape, counts, kinds), in_specs=[ANY] * len(grads),
+        out_specs=[ANY] * len(grads), out_shape=reduced_shapes(grads, kinds),
+        scratch_shapes=Reduce.scratch(sum(counts), groups, rows, cols),
+        compiler_params=pltpu.CompilerParams(collective_id=ident, has_side_effects=True, vmem_limit_bytes=64000 * 1024),
+        name="reduce")(*grads)
+
+
+def wgrad_cols_kernel(a_ref, b_ref, o_ref):
+    y = dot(a_ref[...], b_ref[...], TN).astype(bf16)
+    _, _, g, _, r, c = o_ref.shape
+    for half in (0, 1):
+        o_ref[0, half] = y[:, half * c:(half + 1) * c].reshape(g, 2, r, c)
+
+
+def wgrad_cols(a, b, groups):
+    s, m = a.shape
+    n = b.shape[1]
+    r, c = m // groups // 2, m // 2
+    return pl.pallas_call(
+        wgrad_cols_kernel, grid=(n // m,),
+        in_specs=[pl.BlockSpec((s, m), lambda i: (0, 0)), pl.BlockSpec((s, m), lambda i: (0, i))],
+        out_specs=pl.BlockSpec((1, 2, groups, 2, r, c), lambda i: (i, 0, 0, 0, 0, 0)),
+        out_shape=jax.ShapeDtypeStruct((n // m, 2, groups, 2, r, c), bf16),
+        cost_estimate=pl.CostEstimate(flops=2 * s * m * n, bytes_accessed=2 * (s * (m + n) + m * n),
+                                      transcendentals=0), name="wgrad_cols")(a, b)
+
+
+def wgrad_rows_kernel(a_ref, b_ref, o_ref):
+    y = dot(a_ref[...], b_ref[...], TN).astype(bf16)
+    q, _, _, _, r, c = o_ref.shape
+    for half in (0, 1):
+        o_ref[:, half, 0] = y[:, half * c:(half + 1) * c].reshape(q, 2, r, c)
+
+
+def wgrad_rows(a, b, groups):
+    s, m = a.shape
+    n = b.shape[1]
+    q, r, c = m // n, n // groups // 2, n // 2
+    return pl.pallas_call(
+        wgrad_rows_kernel, grid=(groups,),
+        in_specs=[pl.BlockSpec((s, m // groups), lambda i: (0, i)), pl.BlockSpec((s, n), lambda i: (0, 0))],
+        out_specs=pl.BlockSpec((q, 2, 1, 2, r, c), lambda i: (0, 0, i, 0, 0, 0)),
+        out_shape=jax.ShapeDtypeStruct((q, 2, groups, 2, r, c), bf16),
+        cost_estimate=pl.CostEstimate(flops=2 * s * m * n, bytes_accessed=2 * (s * (m + n) + m * n),
+                                      transcendentals=0), name="wgrad_rows")(a, b)
+
+
+def body_kernel(shape, count, *refs):
+    ins, outs, sems = refs[:count], refs[count:2 * count], refs[2 * count:]
+    p = Place(shape)
+    g = Gather(p, ins, outs, sems)
+    greet(gather_peers(p, False))
+    for w in range(count):
+        g.start(w)
+    for t in range(p.bits):
+        for w in range(count):
+            g.after(w, t)
+    for w in range(count):
+        g.finish(w)
+
+
+def body_call(shape, ws):
+    groups = shape["fsdp"]
+    res = pl.pallas_call(
+        functools.partial(body_kernel, shape, len(ws)), in_specs=[ANY] * len(ws), out_specs=[ANY] * len(ws),
+        out_shape=[gather_shape(w, groups) for w in ws], scratch_shapes=Gather.scratch(len(ws), groups),
+        compiler_params=pltpu.CompilerParams(collective_id=2, has_side_effects=True), name="body",
+    )(*[quarter(w) for w in ws])
+    return [r.reshape(-1, r.shape[-1]) for r in res]
 from jax.sharding import PartitionSpec as P
 
 highest = lax.Precision.HIGHEST
@@ -338,15 +818,16 @@
     groups = shape["fsdp"]
     s, d = tokens.shape[1:]
     ff = b_fc1.shape[0] * groups
-    gather = lambda w: lax.all_gather(w, "fsdp", axis=0, tiled=True)
     tok, cot = tokens[0], cotangent[0]
     flag = hidden_token_indicator.reshape(s, 1)
     sizes = [v.shape[0] for v in (gain_one, gain_two, b_fc2, mask_embed, b_fc1, b_ada)]
-    packed = gather(jnp.concatenate([gain_one, gain_two, b_fc2, mask_embed, b_fc1, b_ada])[None])
+    small = jnp.concatenate([gain_one, gain_two, b_fc2, mask_embed, b_fc1, b_ada])[None]
+    (ada_all, qkv_all), packed = head_call(shape, small, [w_ada, w_qkv])
+    packed = packed[:, 0]
+    out_all, fc1_all, fc2_all = body_call(shape, [w_out, w_fc1, w_fc2])
     cuts = [sum(sizes[:i]) for i in range(len(sizes) + 1)]
     gain1, gain2, b2, emb, b1, bada = (
         packed[:, cuts[i]:cuts[i + 1]].reshape(1, -1).astype(f32) for i in range(len(sizes)))
-    ada_all, qkv_all, out_all, fc1_all, fc2_all = (gather(w) for w in (w_ada, w_qkv, w_out, w_fc1, w_fc2))
     cond_pre = lax.dynamic_slice_in_dim(time_table, time_ids[0], 1, axis=0)
     cond = jax.nn.silu(cond_pre)
     modulation = jnp.dot(cond, ada_all.astype(f32).T, precision=highest) + bada
@@ -359,11 +840,13 @@
     att, lse = attn_fwd_call(lengths, qkv)
     out, gh1, gatt, n2, act, gm, gpre, gap, sums, gb1 = mid_call(
         lengths, att, tok, flag, cot, vec_mid, b1, out_all, fc1_all, fc2_all)
-    g_fc2 = wgrad_call(act, gm)
-    g_fc1 = wgrad_call(n2, gpre)
-    g_out = wgrad_call(att, gap)
+    g_fc2 = wgrad_rows(act, gm, groups)
+    g_fc1 = wgrad_cols(n2, gpre, groups)
+    g_out = wgrad_cols(att, gap, groups)
     dq, dk, dv = attn_bwd_call(lengths, qkv, att, gatt, lse, cos, sin)
-    g_qkv = jnp.concatenate([wgrad_call(n1, x) for x in (dq, dk, dv)], axis=1)
+    g_qkv = [wgrad_cols(n1, x, groups) for x in (dq, dk, dv)]
+    r_fc2, r_fc1, r_out = reduce_call(shape, [g_fc2, g_fc1, g_out], ["rows", "cols", "cols"], 3)
+    r_qkv = reduce_call(shape, g_qkv, ["cols"] * 3, 4)
     igrad, sums1 = post_call(dq, dk, dv, tok, flag, gh1, vec_pre, qkv_all)
     ggm, gb2, a2, s2, gga, st0, st1, st2 = (sums[i:i + 1] for i in range(8))
     a1, s1, gemb = (sums1[i:i + 1] for i in range(3))
@@ -392,11 +875,8 @@
     mods = lax.dynamic_slice_in_dim(rows, width - gmod.shape[1] + me * n_ada, n_ada, axis=1)
     g_ada = lax.dot_general(mods, silu_c, (((0,), (0,)), ((), ())), precision=highest)
 
-    def reduce(g):
-        part = lax.psum_scatter(g, "fsdp", scatter_dimension=0, tiled=True)
-        return lax.psum(part, "dp").astype(f32)
-
-    return (out[None], igrad[None], g1, reduce(g_qkv), reduce(g_out), g2, reduce(g_fc1), gb1, reduce(g_fc2), gb2,
+    return (out[None], igrad[None], g1, jnp.concatenate(r_qkv, axis=1).astype(f32), r_out.astype(f32), g2, r_fc1.astype(f32), gb1,
+            r_fc2.astype(f32), gb2,
             g_ada, gbada, gemb, table, rms)
 
 

time: 657 us -> 411 us (0.63)
  waiting for transfers between devices: 437 us -> 0.02 us
  Pallas kernels: 158 us -> 355 us
  blocking collectives: 9.75 us -> 0 us
    pallas_call x6 -> x10, Pallas kernels: 36.2 us -> 233 us  [the longest x2 121 us: reduce_call(): pl.pallas_call(functools.partial(reduce_kernel, shape, counts, kinds), in...]
    all_gather x5 -> x0, waiting for transfers between devices: 169 us -> none  [per_device(): gather = lambda w: lax.all_gather(w, 'fsdp', axis=0, tiled=True)]
    reduce_scatter x4 -> x0, waiting for transfers between devices: 133 us -> none  [reduce(): part = lax.psum_scatter(g, 'fsdp', scatter_dimension=0, tiled=True)]
    psum x1 -> x0, waiting for transfers between devices: 73.4 us -> none  [reduce(): return lax.psum(part, 'dp').astype(f32)]
    all_gather x1, waiting for transfers between devices: 57.9 us -> 0.01 us  [per_device(): rows = lax.all_gather(row, ('dp', 'fsdp'), axis=0, tiled=True)]
    all_gather x1 -> x0, blocking collectives: 9.75 us -> none  [per_device(): gather = lambda w: lax.all_gather(w, 'fsdp', axis=0, tiled=True)]
  transfers between devices with their start and end apart: 11 -> 1, of which waited for: 9 -> 0; matrix products, arithmetic and copies ran while one was open for 4% -> 2% of each run, Pallas kernels for 18% -> 38%
where the time goes in v2:
time: 411 us; the launch traced here: 409 us
  Pallas kernels  355 us (86%)
  other arithmetic  18.4 us (4%)
  between operations  16.2 us (4%)
  local copies, waits for them, and re-layouts  13.8 us (3%)
  matrix products  6.21 us (2%)
    pallas_call x2, Pallas kernels, reduce_call(): pl.pallas_call(functools.partial(reduce_kernel, shape, counts, kinds), in...  121 us
    pallas_call x1, Pallas kernels, body_call(): pl.pallas_call(functools.partial(body_kernel, shape, len(ws)), in_specs=[...  49 us
    pallas_call x1, Pallas kernels, mid_call(): pl.pallas_call(functools.partial(mid_kernel, cut=cut), grid=(s // rows,),...  37.7 us
    pallas_call x1, Pallas kernels, attn_bwd_call(): pl.pallas_call(functools.partial(attn_bwd_kernel, rows=rows), grid=(np_,)...  37.4 us
    pallas_call x1, Pallas kernels, head_call(): pl.pallas_call(functools.partial(head_kernel, shape, len(ws)), in_specs=[...  27.3 us
    pallas_call x5, Pallas kernels, wgrad_cols(): pl.pallas_call(wgrad_cols_kernel, grid=(n // m,), in_specs=[pl.BlockSpec(...  26.5 us
    pallas_call x1, Pallas kernels, attn_fwd_call(): pl.pallas_call(functools.partial(attn_fwd_kernel, rows=rows), grid=(np_,)...  26.5 us
    pallas_call x1, Pallas kernels, post_call(): pl.pallas_call(post_kernel, grid=(s // rows,), in_specs=[row(d), row(d),...  10.2 us
  transfers between devices with their start and end apart: 1, of which 0 were waited for; matrix products, arithmetic and copies ran while one was open for 2% of the time, Pallas kernels for 38%

profile of v2, /device:TPU:0, one launch (start us, length us, event | category | flops | bytes accessed | tf_op | source)
XLA Modules:
  0.0 409.5 jit_solution(15970549840827343078)
XLA Ops:
  7.2 4.2 %concatenate.21 = bf16[2688]{0:T(1024)(128)(2,1)S(1)} concatenate(bf16[192]{0:T(256)(128)(2,1)} %param.22, bf16[192]{0:T(256)(128)(2,1)} %param.25, bf16[192]{0:T(256)(128)(2,1)} %param.29, bf16[192]{0:T(256)(128)(2,1)} %param.32, bf16[768]{0:T(1024)(128)(2,1)} %param.27, bf16[1152]{0:T(1024)(128)(2,1)} %param.31), dimensions={0} | concatenate | bytes 10752 | tf_op jit(solution)/shard_map/concatenate | solution.py:824
  12.0 27.3 %head.1 = (bf16[4,4,288,128]{3,2,1,0:T(8,128)(2,1)}, bf16[4,4,48,2304]{3,2,1,0:T(8,128)(2,1)}, bf16[4,1,2688]{2,1,0:T(2,128)(2,1)}) custom-call(bf16[4,288,128]{2,1,0:T(8,128)(2,1)} %bitcast.60, bf16[4,48,2304]{2,1,0:T(8,128)(2,1)} %bitcast.59, bf16[1,2688]{1,0:T(2,128)(2,1)} %broadcast_in_dim.26.refs_2_), custom_call_target="tpu_custom_call" | custom-call | tf_op jit(solution)/shard_map/head/pallas_call | solution.py:503
  39.3 0.8 copy.49
  41.0 2.3 convolution_reduce_fusion
  43.8 1.0 copy.35.flag_ref
  45.5 3.0 sine_multiply_fusion
  49.1 9.6 %pre.1 = (bf16[1024,768]{1,0:T(8,128)(2,1)}, bf16[1024,2304]{1,0:T(8,128)(2,1)}) custom-call(bf16[1024,768]{1,0:T(8,128)(2,1)} %bitcast.54, s32[1024,1]{1,0:T(8,128)} %copy.35.flag_ref, f32[8,768]{1,0:T(8,128)} %concatenate.23.vec_ref, bf16[768,2304]{1,0:T(8,128)(2,1)} %bitcast.47, f32[1024,128]{1,0:T(8,128)} %get-tuple-element.87.cos_ref, ...), custom_call_target="tpu_custom_call" | custom-call | flops 3623878656 | bytes 9437184 | tf_op jit(solution)/shard_map/pre/pallas_call | solution.py:50
  58.7 26.5 %attn_fwd.1 = (bf16[1024,768]{1,0:T(8,128)(2,1)}, f32[1024,128]{1,0:T(8,128)}) custom-call(s32[1]{0:T(128)S(6)} %copy.50.len_ref, bf16[1024,2304]{1,0:T(8,128)(2,1)} %get-tuple-element.49.q_ref.k_ref.v_ref, bf16[1024,2304]{1,0:T(8,128)(2,1)} %get-tuple-element.49.q_ref.k_ref.v_ref, bf16[1024,2304]{1,0:T(8,128)(2,1)} %get-tuple-element.49.q_ref.k_ref.v_ref), custom_call_target="tpu_custom_call" | custom-call | flops 6442450944 | bytes 6291456 | tf_op jit(solution)/shard_map/attn_fwd/pallas_call | solution.py:99
  85.8 49.0 %body.1 = (bf16[4,4,48,768]{3,2,1,0:T(8,128)(2,1)}, bf16[4,4,48,3072]{3,2,1,0:T(8,128)(2,1)}, bf16[4,4,192,768]{3,2,1,0:T(8,128)(2,1)}) custom-call(bf16[4,48,768]{2,1,0:T(8,128)(2,1)} %bitcast.61, bf16[4,48,3072]{2,1,0:T(8,128)(2,1)} %bitcast.57, bf16[4,192,768]{2,1,0:T(8,128)(2,1)} %bitcast.58), custom_call_target="tpu_custom_call" | custom-call | tf_op jit(solution)/shard_map/body/pallas_call | solution.py:796
  135.5 37.7 %mid.1 = (bf16[1024,768]{1,0:T(8,128)(2,1)}, f32[1024,768]{1,0:T(8,128)}, bf16[1024,768]{1,0:T(8,128)(2,1)}, bf16[1024,768]{1,0:T(8,128)(2,1)}, bf16[1024,3072]{...) custom-call(s32[1]{0:T(128)S(6)} %copy.50.len_ref, ...), custom_call_target="tpu_custom_call" | custom-call | flops 21743271936 | bytes 23592960 | tf_op jit(solution)/shard_map/mid/pallas_call | solution.py:260
  173.2 37.4 %attn_bwd.1 = (bf16[1024,768]{1,0:T(8,128)(2,1)}, bf16[1024,768]{1,0:T(8,128)(2,1)}, bf16[1024,768]{1,0:T(8,128)(2,1)}) custom-call(s32[1]{0:T(128)S(6)} %copy.50.len_ref, bf16[1024,2304]{1,0:T(8,128)(2,1)} %get-tuple-element.49.q_ref.k_ref.v_ref, bf16[1024,2304]{1,0:T(8,128)(2,1)} %get-tuple-element.49.q_ref.k_ref.v_ref, ...), custom_call_target="tpu_custom_call" | custom-call | flops 16106127360 | bytes 12582912 | tf_op jit(solution)/shard_map/attn_bwd/pallas_call | solution.py:176
  210.7 10.2 %post.1 = (bf16[1024,768]{1,0:T(8,128)(2,1)}, f32[8,768]{1,0:T(8,128)}) custom-call(bf16[1024,768]{1,0:T(8,128)(2,1)} %get-tuple-element.57.dq_ref.b_ref, bf16[1024,768]{1,0:T(8,128)(2,1)} %get-tuple-element.58.dk_ref.b_ref, bf16[1024,768]{1,0:T(8,128)(2,1)} %get-tuple-element.59.dv_ref.b_ref, bf16[1024,768]{1,0:T(8,128)(2,1)} %bitcast.56, ...), custom_call_target="tpu_custom_call" | custom-call | flops 3623878656 | bytes 12582912 | tf_op jit(solution)/shard_map/post/pallas_call | solution.py:300
  220.8 1.5 slice_reduce_fusion.1
  222.3 2.7 concatenate.26
  225.0 4.3 %wgrad_cols.9.refs_2_ = bf16[1,2,4,2,96,384]{5,4,3,2,1,0:T(8,128)(2,1)} custom-call(bf16[1024,768]{1,0:T(8,128)(2,1)} %get-tuple-element.50.att_ref.o_ref.a_ref, bf16[1024,768]{1,0:T(8,128)(2,1)} %get-tuple-element.73.b_ref), custom_call_target="tpu_custom_call" | custom-call | flops 1207959552 | bytes 4325376 | tf_op jit(solution)/shard_map/wgrad_cols/pallas_call | solution.py:751
  229.4 9.2 %wgrad_cols.8.refs_1_ = bf16[4,2,4,2,96,384]{5,4,3,2,1,0:T(8,128)(2,1)} custom-call(bf16[1024,768]{1,0:T(8,128)(2,1)} %get-tuple-element.71.a_ref, bf16[1024,3072]{1,0:T(8,128)(2,1)} %get-tuple-element.72.b_ref), custom_call_target="tpu_custom_call" | custom-call | flops 4831838208 | bytes 12582912 | tf_op jit(solution)/shard_map/wgrad_cols/pallas_call | solution.py:751
  238.6 9.2 %wgrad_rows.1.refs_0_ = bf16[4,2,4,2,96,384]{5,4,3,2,1,0:T(8,128)(2,1)} custom-call(bf16[1024,3072]{1,0:T(8,128)(2,1)} %get-tuple-element.69.a_ref, bf16[1024,768]{1,0:T(8,128)(2,1)} %get-tuple-element.70.b_ref), custom_call_target="tpu_custom_call" | custom-call | flops 4831838208 | bytes 12582912 | tf_op jit(solution)/shard_map/wgrad_rows/pallas_call | solution.py:771
  247.7 82.8 %reduce.13 = (bf16[768,768]{1,0:T(8,128)(2,1)}, bf16[192,3072]{1,0:T(8,128)(2,1)}, bf16[192,768]{1,0:T(8,128)(2,1)}) custom-call(bf16[4,2,4,2,96,384]{5,4,3,2,1,0:T(8,128)(2,1)} %wgrad_rows.1.refs_0_, bf16[4,2,4,2,96,384]{5,4,3,2,1,0:T(8,128)(2,1)} %wgrad_cols.8.refs_1_, bf16[1,2,4,2,96,384]{5,4,3,2,1,0:T(8,128)(2,1)} %wgrad_cols.9.refs_2_), custom_call_target="tpu_custom_call" | custom-call | tf_op jit(solution)/shard_map/reduce/pallas_call | solution.py:732
  330.6 3.0 convert_element_type.115
  333.6 1.6 convert_element_type.116
  335.2 0.9 convert_element_type.114
  336.1 4.3 %wgrad_cols.7.refs_2_ = bf16[1,2,4,2,96,384]{5,4,3,2,1,0:T(8,128)(2,1)} custom-call(bf16[1024,768]{1,0:T(8,128)(2,1)} %get-tuple-element.65.a_ref, bf16[1024,768]{1,0:T(8,128)(2,1)} %get-tuple-element.59.dv_ref.b_ref), custom_call_target="tpu_custom_call" | custom-call | flops 1207959552 | bytes 4325376 | tf_op jit(solution)/shard_map/wgrad_cols/pallas_call | solution.py:751
  340.4 4.3 %wgrad_cols.6.refs_1_ = bf16[1,2,4,2,96,384]{5,4,3,2,1,0:T(8,128)(2,1)} custom-call(bf16[1024,768]{1,0:T(8,128)(2,1)} %get-tuple-element.65.a_ref, bf16[1024,768]{1,0:T(8,128)(2,1)} %get-tuple-element.58.dk_ref.b_ref), custom_call_target="tpu_custom_call" | custom-call | flops 1207959552 | bytes 4325376 | tf_op jit(solution)/shard_map/wgrad_cols/pallas_call | solution.py:751
  344.7 4.4 %wgrad_cols.5.refs_0_ = bf16[1,2,4,2,96,384]{5,4,3,2,1,0:T(8,128)(2,1)} custom-call(bf16[1024,768]{1,0:T(8,128)(2,1)} %get-tuple-element.65.a_ref, bf16[1024,768]{1,0:T(8,128)(2,1)} %get-tuple-element.57.dq_ref.b_ref), custom_call_target="tpu_custom_call" | custom-call | flops 1207959552 | bytes 4325376 | tf_op jit(solution)/shard_map/wgrad_cols/pallas_call | solution.py:751
  349.1 38.5 %reduce.12 = (bf16[192,768]{1,0:T(8,128)(2,1)}, bf16[192,768]{1,0:T(8,128)(2,1)}, bf16[192,768]{1,0:T(8,128)(2,1)}) custom-call(bf16[1,2,4,2,96,384]{5,4,3,2,1,0:T(8,128)(2,1)} %wgrad_cols.5.refs_0_, bf16[1,2,4,2,96,384]{5,4,3,2,1,0:T(8,128)(2,1)} %wgrad_cols.6.refs_1_, bf16[1,2,4,2,96,384]{5,4,3,2,1,0:T(8,128)(2,1)} %wgrad_cols.7.refs_2_), custom_call_target="tpu_custom_call" | custom-call | tf_op jit(solution)/shard_map/reduce/pallas_call | solution.py:732
  387.6 2.5 maximum_convert_fusion
  390.1 1.5 copy.48
  394.4 1.7 fusion.26
  396.0 1.9 fusion.5
  397.9 1.3 fusion.2
  399.3 1.6 dynamic-slice_reduce_fusion
  400.9 1.8 dynamic-slice_reduce_fusion.1
  (46 shorter events, 5.3 us)
Async XLA Ops:
  7.2 33.7 %copy-start = (f32[1000,128]{1,0:T(8,128)S(1)}, f32[1000,128]{1,0:T(8,128)}, u32[]{:S(2)}) copy-start(f32[1000,128]{1,0:T(8,128)} %param.33) | copy-start | bytes 1536004
  7.2 382.9 %all-gather.3.cloned.1.call-start = ((), (), s32[]{:S(2)}) async-start(), calls=%async_computation | async-start | bytes 1453056 | tf_op jit(solution)/shard_map/all_gather | solution.py:858
  12.0 31.8 %copy-start.7 = (s32[1,1024]{1,0:T(1,128)S(1)}, s32[1,1024]{1,0:T(1,128)}, u32[]{:S(2)}) copy-start(s32[1,1024]{1,0:T(1,128)} %param.18) | copy-start | bytes 12292
  210.7 10.2 %copy-start.5 = (f32[8,768]{1,0:T(8,128)S(1)}, f32[8,768]{1,0:T(8,128)}, u32[]{:S(2)}) copy-start(f32[8,768]{1,0:T(8,128)} %get-tuple-element.63) | copy-start | bytes 73732
  210.7 11.7 %copy-start.6 = (f32[1,3072]{1,0:T(1,128)S(1)}, f32[1,3072]{1,0:T(1,128)}, u32[]{:S(2)}) copy-start(f32[1,3072]{1,0:T(1,128)} %get-tuple-element.64) | copy-start | bytes 36868
  330.6 3.0 copy-start.3
  333.6 1.6 copy-start.4
  390.1 1.7 copy-start.2
  391.6 11.0 %copy-start.1 = (f32[1000,128]{1,0:T(8,128)S(1)}, f32[1000,128]{1,0:T(8,128)}, u32[]{:S(2)}) copy-start(f32[1000,128]{1,0:T(8,128)} %param.33) | copy-start | bytes 1536004
Sparse Core Ops, SparseCore 0:
  225.2 56.3 all-gather.2

commit v3 on v2

--- a/solution.py
+++ b/solution.py
@@ -57,7 +57,7 @@
         cost_estimate=pl.CostEstimate(flops=2 * s * d * 3 * d, bytes_accessed=12 * s * d, transcendentals=0),
         name="pre")(tok, flag, vecs, w, cos, sin)
 
-def attn_fwd_kernel(len_ref, q_ref, k_ref, v_ref, o_ref, lse_ref, *, rows):
+def attn_fwd_body(len_ref, q_ref, k_ref, v_ref, o_ref, lse_ref, rows):
     p = pl.program_id(0)
     s = q_ref.shape[0]
     length = len_ref[0]
@@ -92,97 +92,64 @@
         lse_ref[b * rows:(b + 1) * rows, :] = jnp.where(
             lane_q == 2 * p, lses[0], jnp.where(lane_q == 2 * p + 1, lses[1], old))
 
-def attn_fwd_call(length, qkv, rows=256):
-    s, d3 = qkv.shape
-    d = d3 // 3
-    np_ = d // 128
-    return pl.pallas_call(
-        functools.partial(attn_fwd_kernel, rows=rows), grid=(np_,),
-        in_specs=[pl.BlockSpec(memory_space=pltpu.SMEM),
-                  pl.BlockSpec((s, 128), lambda i: (0, i)),
-                  pl.BlockSpec((s, 128), lambda i: (0, np_ + i)),
-                  pl.BlockSpec((s, 128), lambda i: (0, 2 * np_ + i))],
-        out_specs=[pl.BlockSpec((s, 128), lambda i: (0, i)), pl.BlockSpec((s, 128), lambda i: (0, 0))],
-        out_shape=[jax.ShapeDtypeStruct((s, d), bf16), jax.ShapeDtypeStruct((s, 128), f32)],
-        cost_estimate=pl.CostEstimate(flops=8 * s * s * d, bytes_accessed=8 * s * d, transcendentals=s * s * 12),
-        name="attn_fwd")(length, qkv, qkv, qkv)
-
 def split3(x):
     hi = x.astype(bf16).astype(f32)
     r = x - hi
     mid = r.astype(bf16).astype(f32)
     return hi, mid, r - mid
 
-def attn_bwd_kernel(len_ref, q_ref, k_ref, v_ref, o_ref, g_ref, lse_ref, cos_ref, sin_ref,
-                    dq_ref, dk_ref, dv_ref, dqs, *, rows):
-    p = pl.program_id(0)
+def attn_bwd_body(len_ref, q_ref, k_ref, v_ref, o_ref, g_ref, lse_ref, cos_ref, sin_ref,
+                  dq_ref, dk_ref, dv_ref, dqs, dks, dvs, rows):
+    p, h = pl.program_id(0), pl.program_id(1)
     s = q_ref.shape[0]
     length = len_ref[0]
     lane = lax.broadcasted_iota(jnp.int32, (s, 128), 1)
     pos = lax.broadcasted_iota(jnp.int32, (s, 128), 0)
     lane_q = lax.broadcasted_iota(jnp.int32, (rows, 128), 1)
+    e = HD * (1 - h)
+    mine, mine_q = lane // HD == h, lane_q // HD == h
     k = k_ref[...].astype(f32)
     v = v_ref[...].astype(f32)
+    ones = jnp.where((lane >= e) & (lane < e + 3), 1.0, 0.0)
     bias = jnp.where(pos >= length, -1e30, 0.0)
-    dks, dvs = [], []
-    for h in (0, 1):
-        e = HD * (1 - h)
-        mine = (lane >= HD) if h else (lane < HD)
-        mine_q = (lane_q >= HD) if h else (lane_q < HD)
-        ones = jnp.where((lane >= e) & (lane < e + 3), 1.0, 0.0)
-        kx = jnp.where(mine, k, jnp.where(lane == e + 3, bias, ones)).astype(bf16)
-        vx = jnp.where(mine, v, ones).astype(bf16)
-        kt = jnp.where(mine, k, 0.0).T.astype(bf16)
-        dk = jnp.zeros((s, 128), f32)
-        dv = jnp.zeros((s, 128), f32)
-        for b in range(s // rows):
-            sl = slice(b * rows, (b + 1) * rows)
-            qb = q_ref[sl, :]
-            gb = g_ref[sl, :]
-            q = qb.astype(f32)
-            g = gb.astype(f32)
-            lse = jnp.sum(jnp.where(lane_q == 2 * p + h, lse_ref[sl, :], 0.0), axis=1, keepdims=True)
-            dd = jnp.sum(jnp.where(mine_q, g * o_ref[sl, :].astype(f32), 0.0), axis=1, keepdims=True)
-            l0, l1, l2 = split3(-lse)
-            d0, d1, d2 = split3(-dd)
-            qx = jnp.where(mine_q, q, jnp.where(lane_q == e, l0, jnp.where(lane_q == e + 1, l1, jnp.where(
-                lane_q == e + 2, l2, jnp.where(lane_q == e + 3, 1.0, 0.0))))).astype(bf16)
-            gx = jnp.where(mine_q, g, jnp.where(lane_q == e, d0, jnp.where(lane_q == e + 1, d1, jnp.where(
-                lane_q == e + 2, d2, 0.0)))).astype(bf16)
-            pt = jnp.exp2(dot(kx, qx, NT))
-            dst = (pt * dot(vx, gx, NT)).astype(bf16)
-            dv = dv + dot(pt.astype(bf16), gb)
-            dk = dk + dot(dst, qb)
-            dqt = dot(kt, dst)
-            if h == 0:
-                dqs[:, sl] = dqt
-            else:
-                dqs[:, sl] = dqs[:, sl] + dqt
-        dks.append(dk)
-        dvs.append(dv)
-    cos, sin = cos_ref[...], sin_ref[...]
-    dq = dqs[...].T * (HD ** -0.5)
-    dk = jnp.where(lane < HD, dks[0], dks[1]) * (1.0 / LOG2E)
-    dq_ref[...] = (dq * cos - swap_halves(dq) * sin).astype(bf16)
-    dk_ref[...] = (dk * cos - swap_halves(dk) * sin).astype(bf16)
-    dv_ref[...] = jnp.where(lane < HD, dvs[0], dvs[1]).astype(bf16)
-
-def attn_bwd_call(length, qkv, att, gatt, lse, cos, sin, rows=256):
-    s, d3 = qkv.shape
-    d = d3 // 3
-    np_ = d // 128
-    col = pl.BlockSpec((s, 128), lambda i: (0, i))
-    const = pl.BlockSpec((s, 128), lambda i: (0, 0))
-    return pl.pallas_call(
-        functools.partial(attn_bwd_kernel, rows=rows), grid=(np_,),
-        in_specs=[pl.BlockSpec(memory_space=pltpu.SMEM), col,
-                  pl.BlockSpec((s, 128), lambda i: (0, np_ + i)),
-                  pl.BlockSpec((s, 128), lambda i: (0, 2 * np_ + i)), col, col, const, const, const],
-        out_specs=[col, col, col],
-        out_shape=[jax.ShapeDtypeStruct((s, d), bf16)] * 3,
-        scratch_shapes=[pltpu.VMEM((128, s), f32)],
-        cost_estimate=pl.CostEstimate(flops=20 * s * s * d, bytes_accessed=16 * s * d, transcendentals=s * s * 12),
-        name="attn_bwd")(length, qkv, qkv, qkv, att, gatt, lse, cos, sin)
+    kx = jnp.where(mine, k, jnp.where(lane == e + 3, bias, ones)).astype(bf16)
+    vx = jnp.where(mine, v, ones).astype(bf16)
+    kt = jnp.where(mine, k, 0.0).T.astype(bf16)
+    dk = jnp.zeros((s, 128), f32)
+    dv = jnp.zeros((s, 128), f32)
+    for b in range(s // rows):
+        sl = slice(b * rows, (b + 1) * rows)
+        qb = q_ref[sl, :]
+        gb = g_ref[sl, :]
+        q = qb.astype(f32)
+        g = gb.astype(f32)
+        lse = jnp.sum(jnp.where(lane_q == 2 * p + h, lse_ref[sl, :], 0.0), axis=1, keepdims=True)
+        dd = jnp.sum(jnp.where(mine_q, g * o_ref[sl, :].astype(f32), 0.0), axis=1, keepdims=True)
+        l0, l1, l2 = split3(-lse)
+        d0, d1, d2 = split3(-dd)
+        qx = jnp.where(mine_q, q, jnp.where(lane_q == e, l0, jnp.where(lane_q == e + 1, l1, jnp.where(
+            lane_q == e + 2, l2, jnp.where(lane_q == e + 3, 1.0, 0.0))))).astype(bf16)
+        gx = jnp.where(mine_q, g, jnp.where(lane_q == e, d0, jnp.where(lane_q == e + 1, d1, jnp.where(
+            lane_q == e + 2, d2, 0.0)))).astype(bf16)
+        pt = jnp.exp2(dot(kx, qx, NT))
+        dst = (pt * dot(vx, gx, NT)).astype(bf16)
+        dv = dv + dot(pt.astype(bf16), gb)
+        dk = dk + dot(dst, qb)
+        dqt = dot(kt, dst)
+        dqs[:, sl] = jnp.where(h == 0, dqt, dqs[:, sl] + dqt)
+    @pl.when(h == 0)
+    def _():
+        dks[...] = dk
+        dvs[...] = dv
+    @pl.when(h == 1)
+    def _():
+        cos, sin = cos_ref[...], sin_ref[...]
+        dq = dqs[...].T * (HD ** -0.5)
+        dkk = jnp.where(lane < HD, dks[...], dk) * (1.0 / LOG2E)
+        dq_ref[...] = (dq * cos - swap_halves(dq) * sin).astype(bf16)
+        dk_ref[...] = (dkk * cos - swap_halves(dkk) * sin).astype(bf16)
+        dv_ref[...] = jnp.where(lane < HD, dvs[...], dv).astype(bf16)
+
 
 def gelu_both(v):
     a, b = 0.7978845608028654, 0.044715
@@ -271,7 +238,7 @@
                                       transcendentals=s * ff),
         name="mid")(length, att, tok, flag, cot, vec, b1, wo, w1, w2)
 
-def post_kernel(dq_ref, dk_ref, dv_ref, tok_ref, flag_ref, gh1_ref, vec_ref, w_ref, ig_ref, sum_ref):
+def post_body(dq_ref, dk_ref, dv_ref, tok_ref, flag_ref, gh1_ref, vec_ref, w_ref, ig_ref, sum_ref):
     i = pl.program_id(0)
     d = tok_ref.shape[1]
     emb, gain, scale = (vec_ref[r:r + 1, :] for r in range(3))
@@ -292,33 +259,6 @@
     def _():
         sum_ref[...] += new
 
-def post_call(dq, dk, dv, tok, flag, gh1, vec, w, rows=256):
-    s, d = tok.shape
-    row = lambda c: pl.BlockSpec((rows, c), lambda i: (i, 0))
-    whole = lambda a: pl.BlockSpec(a.shape, lambda i: (0, 0))
-    sd = jax.ShapeDtypeStruct
-    return pl.pallas_call(
-        post_kernel, grid=(s // rows,),
-        in_specs=[row(d), row(d), row(d), row(d), row(1), row(d), whole(vec), whole(w)],
-        out_specs=[row(d), pl.BlockSpec((8, d), lambda i: (0, 0))],
-        out_shape=[sd((s, d), bf16), sd((8, d), f32)],
-        cost_estimate=pl.CostEstimate(flops=6 * s * d * d, bytes_accessed=16 * s * d, transcendentals=0),
-        name="post")(dq, dk, dv, tok, flag, gh1, vec, w)
-
-def wgrad_kernel(a_ref, b_ref, o_ref):
-    o_ref[...] = dot(a_ref[...], b_ref[...], TN).astype(bf16)
-
-def wgrad_call(a, b, cols=768, bcols=768):
-    s, m = a.shape
-    n = b.shape[1]
-    return pl.pallas_call(
-        wgrad_kernel, grid=(m // cols, n // bcols),
-        in_specs=[pl.BlockSpec((s, cols), lambda i, j: (0, i)), pl.BlockSpec((s, bcols), lambda i, j: (0, j))],
-        out_specs=pl.BlockSpec((cols, bcols), lambda i, j: (i, j)),
-        out_shape=jax.ShapeDtypeStruct((m, n), bf16),
-        cost_estimate=pl.CostEstimate(flops=2 * s * m * n, bytes_accessed=2 * (s * (m + n) + m * n),
-                                      transcendentals=0),
-        name="wgrad")(a, b)
 
 MESH = pl.DeviceIdType.MESH
 
@@ -509,7 +449,7 @@
 
 
 class Reduce:
-    def __init__(self, place, counts, kinds, srcs, outs, scratch):
+    def __init__(self, place, counts, kinds, srcs, outs, scratch, lag=(1, 2)):
         self.p, self.counts, self.kinds, self.srcs, self.outs = place, counts, kinds, srcs, outs
         (self.own, self.cb, self.xb, self.zb, self.mb, self.u2, self.fin,
          self.load, self.cs, self.cr, self.xs, self.xr, self.zs, self.zr, self.ms, self.mr, self.fs, self.fr,
@@ -527,7 +467,8 @@
         self.stages = ([self.begin, self.core_add] + [functools.partial(self.group_add, t) for t in range(p.bits)]
                        + [functools.partial(self.climb, j) for j in range(1, self.last + 1)] + [self.middle]
                        + [functools.partial(self.descend, j) for j in range(self.last - 1, -1, -1)])
-        self.ticks = self.total + len(self.stages) - 1
+        self.lags = [0, lag[0]] + [lag[0] + lag[1] * (i + 1) for i in range(len(self.stages) - 2)]
+        self.ticks = self.total + self.lags[-1]
 
     @staticmethod
     def scratch(total, groups, rows, cols):
@@ -680,10 +621,24 @@
 
     def tick(self, t):
         for s in range(len(self.stages) - 1, -1, -1):
-            k = t - s
+            k = t - self.lags[s]
             @pl.when((k >= 0) & (k < self.total))
             def _(s=s, k=k):
                 self.stages[s](k)
+
+    def opening(self, step):
+        @pl.when(step == 0)
+        def _():
+            self.greet()
+        self.tick(step)
+
+    def closing(self, step, steps):
+        @pl.when(step == steps - 1)
+        def _():
+            @pl.loop(steps, max(self.ticks, steps))
+            def _(t):
+                self.tick(t)
+            self.drain()
 
     def drain(self):
         p = self.p
@@ -709,32 +664,10 @@
             self.source(k, go)
 
 
-def reduce_kernel(shape, counts, kinds, *refs):
-    n = len(counts)
-    r = Reduce(Place(shape), counts, kinds, refs[:n], refs[n:2 * n], refs[2 * n:])
-    r.greet()
-    @pl.loop(0, r.ticks)
-    def _(t):
-        r.tick(t)
-    r.drain()
-
-
 def reduced_shapes(grads, kinds):
     rows, cols = 2 * grads[0].shape[-2], 2 * grads[0].shape[-1]
     return [jax.ShapeDtypeStruct((rows, g.shape[0] * cols) if kind == "cols" else (g.shape[0] * rows, cols), bf16)
             for g, kind in zip(grads, kinds)]
-
-
-def reduce_call(shape, grads, kinds, ident):
-    groups = shape["fsdp"]
-    counts = [g.shape[0] for g in grads]
-    rows, cols = 2 * grads[0].shape[-2], grads[0].shape[-1]
-    return pl.pallas_call(
-        functools.partial(reduce_kernel, shape, counts, kinds), in_specs=[ANY] * len(grads),
-        out_specs=[ANY] * len(grads), out_shape=reduced_shapes(grads, kinds),
-        scratch_shapes=Reduce.scratch(sum(counts), groups, rows, cols),
-        compiler_params=pltpu.CompilerParams(collective_id=ident, has_side_effects=True, vmem_limit_bytes=64000 * 1024),
-        name="reduce")(*grads)
 
 
 def wgrad_cols_kernel(a_ref, b_ref, o_ref):
@@ -777,28 +710,119 @@
                                       transcendentals=0), name="wgrad_rows")(a, b)
 
 
-def body_kernel(shape, count, *refs):
-    ins, outs, sems = refs[:count], refs[count:2 * count], refs[2 * count:]
+def attn_fwd_kernel(shape, count, rows, *refs):
+    len_ref, q_ref, k_ref, v_ref = refs[:4]
+    ins = refs[4:4 + count]
+    o_ref, lse_ref = refs[4 + count:6 + count]
+    outs = refs[6 + count:6 + 2 * count]
+    step, steps = pl.program_id(0), pl.num_programs(0)
     p = Place(shape)
-    g = Gather(p, ins, outs, sems)
-    greet(gather_peers(p, False))
-    for w in range(count):
-        g.start(w)
-    for t in range(p.bits):
+    g = Gather(p, ins, outs, refs[6 + 2 * count:])
+    @pl.when(step == 0)
+    def _():
+        greet(gather_peers(p, False))
         for w in range(count):
-            g.after(w, t)
-    for w in range(count):
-        g.finish(w)
-
-
-def body_call(shape, ws):
+            g.start(w)
+    for w, at in ((0, 2), (1, 4)):
+        @pl.when(step == at)
+        def _(w=w):
+            g.after(w, 0)
+    attn_fwd_body(len_ref, q_ref, k_ref, v_ref, o_ref, lse_ref, rows)
+    @pl.when(step == steps - 1)
+    def _():
+        for w in range(2, count):
+            g.after(w, 0)
+        for t in range(1, p.bits):
+            for w in range(count):
+                g.after(w, t)
+        for w in range(count):
+            g.finish(w)
+
+
+def attn_fwd_call(shape, length, qkv, ws, rows=256):
     groups = shape["fsdp"]
+    s, d3 = qkv.shape
+    d = d3 // 3
+    np_ = d // 128
+    sd = jax.ShapeDtypeStruct
     res = pl.pallas_call(
-        functools.partial(body_kernel, shape, len(ws)), in_specs=[ANY] * len(ws), out_specs=[ANY] * len(ws),
-        out_shape=[gather_shape(w, groups) for w in ws], scratch_shapes=Gather.scratch(len(ws), groups),
-        compiler_params=pltpu.CompilerParams(collective_id=2, has_side_effects=True), name="body",
-    )(*[quarter(w) for w in ws])
-    return [r.reshape(-1, r.shape[-1]) for r in res]
+        functools.partial(attn_fwd_kernel, shape, len(ws), rows), grid=(np_,),
+        in_specs=[pl.BlockSpec(memory_space=pltpu.SMEM), pl.BlockSpec((s, 128), lambda i: (0, i)),
+                  pl.BlockSpec((s, 128), lambda i: (0, np_ + i)),
+                  pl.BlockSpec((s, 128), lambda i: (0, 2 * np_ + i))] + [ANY] * len(ws),
+        out_specs=[pl.BlockSpec((s, 128), lambda i: (0, i)), pl.BlockSpec((s, 128), lambda i: (0, 0))]
+        + [ANY] * len(ws),
+        out_shape=[sd((s, d), bf16), sd((s, 128), f32)] + [gather_shape(w, groups) for w in ws],
+        scratch_shapes=Gather.scratch(len(ws), groups),
+        compiler_params=pltpu.CompilerParams(collective_id=2, has_side_effects=True),
+        cost_estimate=pl.CostEstimate(flops=8 * s * s * d, bytes_accessed=8 * s * d, transcendentals=s * s * 12),
+        name="attn_fwd")(length, qkv, qkv, qkv, *[quarter(w) for w in ws])
+    return res[0], res[1], [r.reshape(-1, r.shape[-1]) for r in res[2:]]
+
+
+def attn_bwd_kernel(shape, counts, kinds, pairs, rows, *refs):
+    n = len(counts)
+    ins, srcs, grads, outs = refs[:9], refs[9:9 + n], refs[9 + n:12 + n], refs[12 + n:12 + 2 * n]
+    work, scratch = refs[12 + 2 * n:15 + 2 * n], refs[15 + 2 * n:]
+    step = pl.program_id(0) * 2 + pl.program_id(1)
+    r = Reduce(Place(shape), counts, kinds, srcs, outs, scratch)
+    r.opening(step)
+    attn_bwd_body(*ins, *grads, *work, rows)
+    r.closing(step, 2 * pairs)
+
+
+def attn_bwd_call(shape, length, qkv, att, gatt, lse, cos, sin, grads, kinds, rows=256):
+    groups = shape["fsdp"]
+    s, d3 = qkv.shape
+    d = d3 // 3
+    np_ = d // 128
+    counts = [g.shape[0] for g in grads]
+    r, c = 2 * grads[0].shape[-2], grads[0].shape[-1]
+    col = pl.BlockSpec((s, 128), lambda i, h: (0, i))
+    const = pl.BlockSpec((s, 128), lambda i, h: (0, 0))
+    res = pl.pallas_call(
+        functools.partial(attn_bwd_kernel, shape, counts, kinds, np_, rows), grid=(np_, 2),
+        in_specs=[pl.BlockSpec(memory_space=pltpu.SMEM), col,
+                  pl.BlockSpec((s, 128), lambda i, h: (0, np_ + i)),
+                  pl.BlockSpec((s, 128), lambda i, h: (0, 2 * np_ + i)), col, col, const, const, const]
+        + [ANY] * len(grads),
+        out_specs=[col, col, col] + [ANY] * len(grads),
+        out_shape=[jax.ShapeDtypeStruct((s, d), bf16)] * 3 + reduced_shapes(grads, kinds),
+        scratch_shapes=[pltpu.VMEM((128, s), f32), pltpu.VMEM((s, 128), f32), pltpu.VMEM((s, 128), f32)]
+        + Reduce.scratch(sum(counts), groups, r, c),
+        compiler_params=pltpu.CompilerParams(collective_id=3, has_side_effects=True, vmem_limit_bytes=64000 * 1024),
+        cost_estimate=pl.CostEstimate(flops=20 * s * s * d, bytes_accessed=16 * s * d, transcendentals=s * s * 12),
+        name="attn_bwd")(length, qkv, qkv, qkv, att, gatt, lse, cos, sin, *grads)
+    return res[:3], res[3:]
+
+
+def post_kernel(shape, counts, kinds, steps, *refs):
+    n = len(counts)
+    ins, srcs, outs, reduced = refs[:8], refs[8:8 + n], refs[8 + n:10 + n], refs[10 + n:10 + 2 * n]
+    r = Reduce(Place(shape), counts, kinds, srcs, reduced, refs[10 + 2 * n:])
+    step = pl.program_id(0)
+    r.opening(step)
+    post_body(*ins, *outs)
+    r.closing(step, steps)
+
+
+def post_call(shape, dq, dk, dv, tok, flag, gh1, vec, w, grads, kinds, rows=128):
+    s, d = tok.shape
+    row = lambda c: pl.BlockSpec((rows, c), lambda i: (i, 0))
+    whole = lambda a: pl.BlockSpec(a.shape, lambda i: (0, 0))
+    sd = jax.ShapeDtypeStruct
+    counts = [g.shape[0] for g in grads]
+    r, c = 2 * grads[0].shape[-2], grads[0].shape[-1]
+    res = pl.pallas_call(
+        functools.partial(post_kernel, shape, counts, kinds, s // rows), grid=(s // rows,),
+        in_specs=[row(d), row(d), row(d), row(d), row(1), row(d), whole(vec), whole(w)] + [ANY] * len(grads),
+        out_specs=[row(d), pl.BlockSpec((8, d), lambda i: (0, 0))] + [ANY] * len(grads),
+        out_shape=[sd((s, d), bf16), sd((8, d), f32)] + reduced_shapes(grads, kinds),
+        scratch_shapes=Reduce.scratch(sum(counts), shape["fsdp"], r, c),
+        compiler_params=pltpu.CompilerParams(collective_id=4, has_side_effects=True, vmem_limit_bytes=64000 * 1024),
+        cost_estimate=pl.CostEstimate(flops=6 * s * d * d, bytes_accessed=16 * s * d, transcendentals=0),
+        name="post")(dq, dk, dv, tok, flag, gh1, vec, w, *grads)
+    return res[0], res[1], res[2:]
 from jax.sharding import PartitionSpec as P
 
 highest = lax.Precision.HIGHEST
@@ -824,7 +848,6 @@
     small = jnp.concatenate([gain_one, gain_two, b_fc2, mask_embed, b_fc1, b_ada])[None]
     (ada_all, qkv_all), packed = head_call(shape, small, [w_ada, w_qkv])
     packed = packed[:, 0]
-    out_all, fc1_all, fc2_all = body_call(shape, [w_out, w_fc1, w_fc2])
     cuts = [sum(sizes[:i]) for i in range(len(sizes) + 1)]
     gain1, gain2, b2, emb, b1, bada = (
         packed[:, cuts[i]:cuts[i + 1]].reshape(1, -1).astype(f32) for i in range(len(sizes)))
@@ -837,17 +860,16 @@
     vec_pre = jnp.concatenate([emb, gain1, scale_a, shift_a] + [zero] * 4, axis=0)
     vec_mid = jnp.concatenate([emb, gain2, scale_m, shift_m, gate_a, gate_m, b2, zero], axis=0)
     n1, qkv = pre_call(tok, flag, vec_pre, qkv_all, cos, sin)
-    att, lse = attn_fwd_call(lengths, qkv)
+    att, lse, (out_all, fc1_all, fc2_all) = attn_fwd_call(shape, lengths, qkv, [w_out, w_fc1, w_fc2])
     out, gh1, gatt, n2, act, gm, gpre, gap, sums, gb1 = mid_call(
         lengths, att, tok, flag, cot, vec_mid, b1, out_all, fc1_all, fc2_all)
     g_fc2 = wgrad_rows(act, gm, groups)
     g_fc1 = wgrad_cols(n2, gpre, groups)
     g_out = wgrad_cols(att, gap, groups)
-    dq, dk, dv = attn_bwd_call(lengths, qkv, att, gatt, lse, cos, sin)
+    (dq, dk, dv), (r_fc2, r_fc1, r_out) = attn_bwd_call(
+        shape, lengths, qkv, att, gatt, lse, cos, sin, [g_fc2, g_fc1, g_out], ["rows", "cols", "cols"])
     g_qkv = [wgrad_cols(n1, x, groups) for x in (dq, dk, dv)]
-    r_fc2, r_fc1, r_out = reduce_call(shape, [g_fc2, g_fc1, g_out], ["rows", "cols", "cols"], 3)
-    r_qkv = reduce_call(shape, g_qkv, ["cols"] * 3, 4)
-    igrad, sums1 = post_call(dq, dk, dv, tok, flag, gh1, vec_pre, qkv_all)
+    igrad, sums1, r_qkv = post_call(shape, dq, dk, dv, tok, flag, gh1, vec_pre, qkv_all, g_qkv, ["cols"] * 3)
     ggm, gb2, a2, s2, gga, st0, st1, st2 = (sums[i:i + 1] for i in range(8))
     a1, s1, gemb = (sums1[i:i + 1] for i in range(3))
     gmod = jnp.concatenate([s1, a1 * gain1, gga, s2, a2 * gain2, ggm], axis=1)

time: 411 us -> 384 us (0.934)
  Pallas kernels: 355 us -> 283 us
  waiting for transfers between devices: 0.02 us -> 45.9 us
    pallas_call x6 -> x3, Pallas kernels: 244 us -> 172 us  [the longest x1 78.6 us: attn_bwd_call(): pl.pallas_call(functools.partial(attn_bwd_kernel, shape, counts, kinds, n...]
    all_gather x1, waiting for transfers between devices: 0.01 us -> 45.9 us  [per_device(): rows = lax.all_gather(row, ('dp', 'fsdp'), axis=0, tiled=True)]
  transfers between devices with their start and end apart: 1 -> 1, of which waited for: 0 -> 1; matrix products, arithmetic and copies ran while one was open for 2% -> 2% of each run, Pallas kernels for 38% -> 0%
where the time goes in v3:
time: 384 us; the launch traced here: 383 us
  Pallas kernels  283 us (74%)
  waiting for transfers between devices  45.9 us (12%)
  other arithmetic  17.2 us (4%)
  between operations  16.2 us (4%)
  local copies, waits for them, and re-layouts  15 us (4%)
  matrix products  6.21 us (2%)
    pallas_call x1, Pallas kernels, attn_bwd_call(): pl.pallas_call(functools.partial(attn_bwd_kernel, shape, counts, kinds, n...  78.6 us
    pallas_call x1, Pallas kernels, attn_fwd_call(): pl.pallas_call(functools.partial(attn_fwd_kernel, shape, len(ws), rows),...  51.1 us
    all_gather x1, waiting for transfers between devices, per_device(): rows = lax.all_gather(row, ('dp', 'fsdp'), axis=0, tiled=True)  45.9 us
    pallas_call x1, Pallas kernels, post_call(): pl.pallas_call(functools.partial(post_kernel, shape, counts, kinds, s //...  42.5 us
    pallas_call x1, Pallas kernels, mid_call(): pl.pallas_call(functools.partial(mid_kernel, cut=cut), grid=(s // rows,),...  37.7 us
    pallas_call x1, Pallas kernels, head_call(): pl.pallas_call(functools.partial(head_kernel, shape, len(ws)), in_specs=[...  27.3 us
    pallas_call x5, Pallas kernels, wgrad_cols(): pl.pallas_call(wgrad_cols_kernel, grid=(n // m,), in_specs=[pl.BlockSpec(...  26.6 us
    pallas_call x1, Pallas kernels, pre_call(): pl.pallas_call(pre_kernel, grid=(s // rows,), in_specs=[pl.BlockSpec((row...  9.62 us
  transfers between devices with their start and end apart: 1, of which 1 were waited for; matrix products, arithmetic and copies ran while one was open for 2% of the time, Pallas kernels for 0%

profile of v3, /device:TPU:0, one launch (start us, length us, event | category | flops | bytes accessed | tf_op | source)
XLA Modules:
  0.0 383.1 jit_solution(15528812583359780785)
XLA Ops:
  7.2 4.2 %concatenate.21 = bf16[2688]{0:T(1024)(128)(2,1)S(1)} concatenate(bf16[192]{0:T(256)(128)(2,1)} %param.22, bf16[192]{0:T(256)(128)(2,1)} %param.25, bf16[192]{0:T(256)(128)(2,1)} %param.29, bf16[192]{0:T(256)(128)(2,1)} %param.32, bf16[768]{0:T(1024)(128)(2,1)} %param.27, bf16[1152]{0:T(1024)(128)(2,1)} %param.31), dimensions={0} | concatenate | bytes 10752 | tf_op jit(solution)/shard_map/concatenate | solution.py:848
  12.0 27.3 %head.1 = (bf16[4,4,288,128]{3,2,1,0:T(8,128)(2,1)}, bf16[4,4,48,2304]{3,2,1,0:T(8,128)(2,1)}, bf16[4,1,2688]{2,1,0:T(2,128)(2,1)}) custom-call(bf16[4,288,128]{2,1,0:T(8,128)(2,1)} %bitcast.59, bf16[4,48,2304]{2,1,0:T(8,128)(2,1)} %bitcast.58, bf16[1,2688]{1,0:T(2,128)(2,1)} %broadcast_in_dim.26.refs_2_), custom_call_target="tpu_custom_call" | custom-call | tf_op jit(solution)/shard_map/head/pallas_call | solution.py:443
  39.3 0.8 copy.49
  41.0 2.3 convolution_reduce_fusion
  43.8 1.0 copy.35.flag_ref.refs_4_
  46.1 3.0 sine_multiply_fusion
  49.7 9.6 %pre.1 = (bf16[1024,768]{1,0:T(8,128)(2,1)}, bf16[1024,2304]{1,0:T(8,128)(2,1)}) custom-call(bf16[1024,768]{1,0:T(8,128)(2,1)} %bitcast.54, s32[1024,1]{1,0:T(8,128)} %copy.35.flag_ref.refs_4_, f32[8,768]{1,0:T(8,128)} %concatenate.23.vec_ref.refs_6_, bf16[768,2304]{1,0:T(8,128)(2,1)} %bitcast.47, f32[1024,128]{1,0:T(8,128)} %get-tuple-element.87.cos_ref.refs_7_, ...), custom_call_target="tpu_custom_call" | custom-call | flops 3623878656 | bytes 9437184 | tf_op jit(solution)/shard_map/pre/pallas_call | solution.py:50
  59.3 51.1 %attn_fwd.1 = (bf16[1024,768]{1,0:T(8,128)(2,1)}, f32[1024,128]{1,0:T(8,128)}, bf16[4,4,48,768]{3,2,1,0:T(8,128)(2,1)}, bf16[4,4,48,3072]{3,2,1,0:T(8,128)(2,1)}, bf16[4,4,192,768]{3,2,1,0:T(8,128)(2,1)}) custom-call(s32[1]{0:T(128)S(6)} %copy.51.refs_0_.len_ref, bf16[1024,2304]{1,0:T(8,128)(2,1)} %get-tuple-element.49.refs_1_.refs_2_.refs_3_, ...), custom_call_target="tpu_custom_call" | custom-call | flops 6442450944 | bytes 6291456 | tf_op jit(solution)/shard_map/attn_fwd/pallas_call | solution.py:748
  110.5 0.6 concatenate.25.vec_ref
  111.1 37.7 %mid.1 = (bf16[1024,768]{1,0:T(8,128)(2,1)}, f32[1024,768]{1,0:T(8,128)}, bf16[1024,768]{1,0:T(8,128)(2,1)}, bf16[1024,768]{1,0:T(8,128)(2,1)}, bf16[1024,3072]{...) custom-call(s32[1]{0:T(128)S(6)} %copy.51.refs_0_.len_ref, ...), custom_call_target="tpu_custom_call" | custom-call | flops 21743271936 | bytes 23592960 | tf_op jit(solution)/shard_map/mid/pallas_call | solution.py:227
  148.8 4.4 %wgrad_cols.6.refs_11_ = bf16[1,2,4,2,96,384]{5,4,3,2,1,0:T(8,128)(2,1)} custom-call(bf16[1024,768]{1,0:T(8,128)(2,1)} %get-tuple-element.50.att_ref.a_ref.refs_4_, bf16[1024,768]{1,0:T(8,128)(2,1)} %get-tuple-element.61.b_ref), custom_call_target="tpu_custom_call" | custom-call | flops 1207959552 | bytes 4325376 | tf_op jit(solution)/shard_map/wgrad_cols/pallas_call | solution.py:684
  153.2 9.2 %wgrad_cols.5.refs_10_ = bf16[4,2,4,2,96,384]{5,4,3,2,1,0:T(8,128)(2,1)} custom-call(bf16[1024,768]{1,0:T(8,128)(2,1)} %get-tuple-element.59.a_ref, bf16[1024,3072]{1,0:T(8,128)(2,1)} %get-tuple-element.60.b_ref), custom_call_target="tpu_custom_call" | custom-call | flops 4831838208 | bytes 12582912 | tf_op jit(solution)/shard_map/wgrad_cols/pallas_call | solution.py:684
  162.4 9.2 %wgrad_rows.1.refs_9_ = bf16[4,2,4,2,96,384]{5,4,3,2,1,0:T(8,128)(2,1)} custom-call(bf16[1024,3072]{1,0:T(8,128)(2,1)} %get-tuple-element.57.a_ref, bf16[1024,768]{1,0:T(8,128)(2,1)} %get-tuple-element.58.b_ref), custom_call_target="tpu_custom_call" | custom-call | flops 4831838208 | bytes 12582912 | tf_op jit(solution)/shard_map/wgrad_rows/pallas_call | solution.py:704
  171.6 78.6 %attn_bwd.1 = (bf16[1024,768]{1,0:T(8,128)(2,1)}, bf16[1024,768]{1,0:T(8,128)(2,1)}, bf16[1024,768]{1,0:T(8,128)(2,1)}, bf16[768,768]{1,0:T(8,128)(2,1)}, bf16[1...) custom-call(s32[1]{0:T(128)S(6)} %copy.51.refs_0_.len_ref, bf16[1024,2304]{1,0:T(8,128)(2,1)} %get-tuple-element.49.refs_1_.refs_2_.refs_3_, ...), custom_call_target="tpu_custom_call" | custom-call | flops 16106127360 | bytes 12582912 | tf_op jit(solution)/shard_map/attn_bwd/pallas_call | solution.py:783
  250.2 4.3 %wgrad_cols.9.refs_10_ = bf16[1,2,4,2,96,384]{5,4,3,2,1,0:T(8,128)(2,1)} custom-call(bf16[1024,768]{1,0:T(8,128)(2,1)} %get-tuple-element.66.a_ref, bf16[1024,768]{1,0:T(8,128)(2,1)} %get-tuple-element.64.b_ref.refs_2_), custom_call_target="tpu_custom_call" | custom-call | flops 1207959552 | bytes 4325376 | tf_op jit(solution)/shard_map/wgrad_cols/pallas_call | solution.py:684
  254.5 4.3 %wgrad_cols.8.refs_9_ = bf16[1,2,4,2,96,384]{5,4,3,2,1,0:T(8,128)(2,1)} custom-call(bf16[1024,768]{1,0:T(8,128)(2,1)} %get-tuple-element.66.a_ref, bf16[1024,768]{1,0:T(8,128)(2,1)} %get-tuple-element.63.b_ref.refs_1_), custom_call_target="tpu_custom_call" | custom-call | flops 1207959552 | bytes 4325376 | tf_op jit(solution)/shard_map/wgrad_cols/pallas_call | solution.py:684
  258.8 4.3 %wgrad_cols.7.refs_8_ = bf16[1,2,4,2,96,384]{5,4,3,2,1,0:T(8,128)(2,1)} custom-call(bf16[1024,768]{1,0:T(8,128)(2,1)} %get-tuple-element.66.a_ref, bf16[1024,768]{1,0:T(8,128)(2,1)} %get-tuple-element.62.b_ref.refs_0_), custom_call_target="tpu_custom_call" | custom-call | flops 1207959552 | bytes 4325376 | tf_op jit(solution)/shard_map/wgrad_cols/pallas_call | solution.py:684
  263.2 42.5 %post.1 = (bf16[1024,768]{1,0:T(8,128)(2,1)}, f32[8,768]{1,0:T(8,128)}, bf16[192,768]{1,0:T(8,128)(2,1)}, bf16[192,768]{1,0:T(8,128)(2,1)}, bf16[192,768]{1,0:T(8,128)(2,1)}) custom-call(bf16[1024,768]{1,0:T(8,128)(2,1)} %get-tuple-element.62.b_ref.refs_0_, bf16[1024,768]{1,0:T(8,128)(2,1)} %get-tuple-element.63.b_ref.refs_1_, ...), custom_call_target="tpu_custom_call" | custom-call | flops 3623878656 | bytes 12582912 | tf_op jit(solution)/shard_map/post/pallas_call | solution.py:816
  305.7 1.5 slice_reduce_fusion.1
  307.2 2.7 concatenate.26
  309.9 3.0 convert_element_type.115
  312.9 1.6 convert_element_type.116
  314.5 0.9 convert_element_type.114
  315.4 1.3 maximum_convert_fusion
  316.7 45.9 %all-gather.3.cloned.1.call-done = f32[32,1,11008]{2,1,0:T(1,128)} async-done(((f32[1,1,11008]{2,1,0:T(1,128)}), f32[32,1,11008]{2,1,0:T(1,128)}) %all-gather.3.cloned.1.call-update) | async-done | bytes 1409040 | tf_op jit(solution)/shard_map/all_gather | solution.py:880
  362.5 1.4 copy.48
  366.6 1.7 fusion.26
  368.3 1.9 fusion.5
  370.2 1.3 fusion.2
  371.5 1.6 dynamic-slice_reduce_fusion
  373.1 1.8 dynamic-slice_reduce_fusion.1
  374.9 1.1 copy.53
  (52 shorter events, 4.8 us)
Async XLA Ops:
  7.2 33.7 %copy-start = (f32[1000,128]{1,0:T(8,128)S(1)}, f32[1000,128]{1,0:T(8,128)}, u32[]{:S(2)}) copy-start(f32[1000,128]{1,0:T(8,128)} %param.33) | copy-start | bytes 1536004
  7.2 355.3 %all-gather.3.cloned.1.call-start = ((), (), s32[]{:S(2)}) async-start(), calls=%async_computation | async-start | bytes 1453056 | tf_op jit(solution)/shard_map/all_gather | solution.py:880
  12.0 31.8 %copy-start.11 = (s32[1,1024]{1,0:T(1,128)S(1)}, s32[1,1024]{1,0:T(1,128)}, u32[]{:S(2)}) copy-start(s32[1,1024]{1,0:T(1,128)} %param.18) | copy-start | bytes 12292
  263.2 42.5 %copy-start.9 = (f32[8,768]{1,0:T(8,128)S(1)}, f32[8,768]{1,0:T(8,128)}, u32[]{:S(2)}) copy-start(f32[8,768]{1,0:T(8,128)} %get-tuple-element.69) | copy-start | bytes 73732
  263.2 44.0 %copy-start.10 = (f32[1,3072]{1,0:T(1,128)S(1)}, f32[1,3072]{1,0:T(1,128)}, u32[]{:S(2)}) copy-start(f32[1,3072]{1,0:T(1,128)} %get-tuple-element.70) | copy-start | bytes 36868
  309.9 3.0 copy-start.4
  312.9 1.6 copy-start.5
  312.9 2.5 copy-start.6
  312.9 2.5 copy-start.7
  312.9 2.5 copy-start.8
  316.7 47.3 %copy-start.2 = (bf16[4,4,288,128]{3,2,1,0:T(8,128)(2,1)S(1)}, bf16[4,4,288,128]{3,2,1,0:T(8,128)(2,1)}, u32[]{:S(2)}) copy-start(bf16[4,4,288,128]{3,2,1,0:T(8,128)(2,1)} %get-tuple-element.47) | copy-start | bytes 3538948
  364.0 10.9 %copy-start.3 = (bf16[1024,768]{1,0:T(8,128)(2,1)S(1)}, bf16[1024,768]{1,0:T(8,128)(2,1)}, u32[]{:S(2)}) copy-start(bf16[1024,768]{1,0:T(8,128)(2,1)} %get-tuple-element.67) | copy-start | bytes 4718596
  374.9 1.4 copy-start.1
Sparse Core Ops, SparseCore 0:
  310.0 52.5 all-gather.2

commit v4 on v3

--- a/solution.py
+++ b/solution.py
@@ -823,6 +823,160 @@
         cost_estimate=pl.CostEstimate(flops=6 * s * d * d, bytes_accessed=16 * s * d, transcendentals=0),
         name="post")(dq, dk, dv, tok, flag, gh1, vec, w, *grads)
     return res[0], res[1], res[2:]
+
+def f32_rows_dot(row, weights):
+    parts = split3(row)
+    stack = jnp.concatenate(list(parts) + [jnp.zeros((5, row.shape[1]), f32)], axis=0).astype(bf16)
+    return colsum(dot(stack, weights))
+
+
+class Small:
+    def __init__(self, place, scratch):
+        self.p = place
+        (self.ag, self.rows, self.ab, self.bs, self.bm, self.bb, self.bg, self.s1, self.r1, self.s2, self.r2) = scratch
+
+    @staticmethod
+    def widths(shape, d, ff, n_mod):
+        groups = shape["fsdp"]
+        part = n_mod // groups
+        return -(-(d // groups) // 128) * 128, ff // groups, part if part % 128 == 0 else n_mod
+
+    @staticmethod
+    def scratch(shape, d, ff, n_mod):
+        groups, lines = shape["fsdp"], shape["dp"]
+        wide, fpart, gpart = Small.widths(shape, d, ff, n_mod)
+        vm = lambda *dims: pltpu.VMEM(dims, f32)
+        sem = pltpu.SemaphoreType.DMA
+        return [vm(groups, 1, n_mod), vm(groups, 8, d), vm(groups, 1, ff), vm(lines, 8, wide), vm(lines, groups, 384),
+                vm(lines, 1, fpart), vm(lines, groups, gpart), sem((groups, 3)), sem((groups, 3)), sem((lines, 4)),
+                sem((lines, 4))]
+
+    def peers(self):
+        p = self.p
+        return [(p.dp, xor(p.me, m)) for m in range(1, p.groups)] + [(xor(p.dp, m), p.me) for m in range(1, p.lines)]
+
+    def copies(self, stage, m, arrived):
+        p = self.p
+        if stage == 1:
+            bufs, ss, rs = (self.ag, self.rows, self.ab), self.s1, self.r1
+            where, slot = (p.dp, xor(p.me, m)), xor(p.me, m) if arrived else p.me
+        else:
+            bufs, ss, rs = (self.bs, self.bm, self.bb, self.bg), self.s2, self.r2
+            where, slot = (xor(p.dp, m), p.me), xor(p.dp, m) if arrived else p.dp
+        return [remote(b.at[slot], b.at[slot], ss.at[m, i], rs.at[m, i], where) for i, b in enumerate(bufs)]
+
+    def spread(self, stage):
+        for m in range(1, self.p.groups if stage == 1 else self.p.lines):
+            for c in self.copies(stage, m, False):
+                c.start()
+
+    def collect(self, stage):
+        for m in range(1, self.p.groups if stage == 1 else self.p.lines):
+            for c in self.copies(stage, m, True):
+                c.wait_recv()
+
+    def settle(self):
+        for stage in (1, 2):
+            for m in range(1, self.p.groups if stage == 1 else self.p.lines):
+                for c in self.copies(stage, m, False):
+                    c.wait_send()
+
+    def first(self, sums, sb1, sums1, vec_pre, vec_mid, condp, meta, ada):
+        me = self.p.me
+        d = sums.shape[1]
+        ggm, gb2, a2, s2, gga, st0, st1, st2 = (sums[i:i + 1] for i in range(8))
+        a1, s1, gemb = (sums1[i:i + 1] for i in range(3))
+        gain1, scale_a, gain2, scale_m = vec_pre[1:2], vec_pre[2:3], vec_mid[1:2], vec_mid[2:3]
+        gm = jnp.concatenate([s1, a1 * gain1, gga, s2, a2 * gain2, ggm], axis=1)
+        sig = 1.0 / (1.0 + jnp.exp(-condp))
+        gc = f32_rows_dot(gm, ada) * (sig * (1.0 + condp * (1.0 - sig)))
+        lane = lax.broadcasted_iota(jnp.int32, (1, 128), 1)
+        total = lambda x: jnp.sum(x, axis=1, keepdims=True)
+        stat = jnp.where(lane == 0, total(st0), jnp.where(lane == 1, total(st1), jnp.where(lane == 2, total(st2), meta)))
+        tail = jnp.concatenate([gc, condp * sig, stat, jnp.zeros((1, d - 384), f32)], axis=1)
+        self.ag[me] = gm
+        self.ab[me] = sb1
+        self.rows[me] = jnp.concatenate([(1.0 + scale_a) * a1, (1.0 + scale_m) * a2, gb2, gemb, tail,
+                                         jnp.zeros((3, d), f32)], axis=0)
+        self.spread(1)
+
+    def second(self):
+        p = self.p
+        self.collect(1)
+        d = self.rows.shape[2]
+        wide, fpart, gpart = self.bs.shape[2], self.bb.shape[2], self.bg.shape[2]
+        total = self.rows[0]
+        for f in range(1, p.groups):
+            total = total + self.rows[f]
+        self.bs[p.dp] = pltpu.roll(total, (d - p.me * (d // p.groups)) % d, 1)[:, :wide]
+        self.bm[p.dp] = jnp.concatenate([self.rows[f, 4:5, :384] for f in range(p.groups)], axis=0)
+        cut = pl.ds(pl.multiple_of(p.me * fpart, 128), fpart)
+        part = self.ab[0, :, cut]
+        for f in range(1, p.groups):
+            part = part + self.ab[f, :, cut]
+        self.bb[p.dp] = part
+        n_mod = self.ag.shape[2]
+        cut = slice(None) if gpart == n_mod else pl.ds(pl.multiple_of(p.me * gpart, 128), gpart)
+        self.bg[p.dp] = jnp.concatenate([self.ag[f, :, cut] for f in range(p.groups)], axis=0)
+        self.spread(2)
+
+    def third(self, norms_ref, gb1_ref, gada_ref, gbada_ref, table_ref, rms_ref, d):
+        p = self.p
+        self.collect(2)
+        total, part = self.bs[0], self.bb[0]
+        for z in range(1, p.lines):
+            total = total + self.bs[z]
+            part = part + self.bb[z]
+        norms_ref[...] = total
+        gb1_ref[...] = part
+        mods = jnp.concatenate([self.bg[z] for z in range(p.lines)], axis=0)
+        info = jnp.concatenate([self.bm[z] for z in range(p.lines)], axis=0)
+        gcs, conds, stat = info[:, :128], info[:, 128:256], info[:, 256:384]
+        highest = lax.Precision.HIGHEST
+        gada_ref[...] = lax.dot_general(mods, conds, TN, precision=highest, preferred_element_type=f32)
+        gbada_ref[...] = colsum(mods)
+        ids = stat[:, 4:5].astype(jnp.int32)
+        hot = (lax.broadcasted_iota(jnp.int32, (ids.shape[0], table_ref.shape[0]), 1) == ids).astype(f32)
+        table_ref[...] = lax.dot_general(hot, gcs, TN, precision=highest, preferred_element_type=f32)
+        stat = colsum(stat)
+        rms_ref[...] = jnp.sqrt(stat / (stat[:, 3:4] * d))
+
+
+def small_kernel(shape, sums, sb1, sums1, vec_pre, vec_mid, condp, meta, ada, norms, gb1, gada, gbada, table, rms,
+                 *scratch):
+    s = Small(Place(shape), scratch)
+    greet(s.peers())
+    s.first(sums[...], sb1[...], sums1[...], vec_pre[...], vec_mid[...], condp[...], meta[...], ada[...])
+    s.second()
+    s.third(norms, gb1, gada, gbada, table, rms, sums.shape[1])
+    s.settle()
+
+
+def small_shapes(shape, d, ff, n_mod, table_rows):
+    wide, fpart, gpart = Small.widths(shape, d, ff, n_mod)
+    sd = lambda *dims: jax.ShapeDtypeStruct(dims, f32)
+    return [sd(8, wide), sd(1, fpart), sd(gpart, 128), sd(1, gpart), sd(table_rows, 128), sd(1, 128)]
+
+
+def small_call(shape, sums, sb1, sums1, vec_pre, vec_mid, condp, meta, ada, table_rows):
+    d, ff, n_mod = sums.shape[1], sb1.shape[1], ada.shape[0]
+    vm = pl.BlockSpec(memory_space=pltpu.VMEM)
+    return pl.pallas_call(
+        functools.partial(small_kernel, shape), in_specs=[vm] * 8, out_specs=[vm] * 6,
+        out_shape=small_shapes(shape, d, ff, n_mod, table_rows), scratch_shapes=Small.scratch(shape, d, ff, n_mod),
+        compiler_params=pltpu.CompilerParams(collective_id=5, has_side_effects=True), name="small",
+    )(sums, sb1, sums1, vec_pre, vec_mid, condp, meta, ada)
+
+
+def small_results(shape, res, sizes):
+    norms, gb1, gada, gbada, table, rms = res
+    n_ada = sizes[5]
+    if gada.shape[0] != n_ada:
+        me = lax.axis_index("fsdp")
+        gada = lax.dynamic_slice_in_dim(gada, me * n_ada, n_ada, axis=0)
+        gbada = lax.dynamic_slice_in_dim(gbada, me * n_ada, n_ada, axis=1)
+    g1, g2, gb2, gemb = (norms[i, :sizes[i]] for i in range(4))
+    return g1, g2, gb2, gemb, gb1[0], gada, gbada[0], table, rms[0, :3]
 from jax.sharding import PartitionSpec as P
 
 highest = lax.Precision.HIGHEST
@@ -870,33 +1024,9 @@
         shape, lengths, qkv, att, gatt, lse, cos, sin, [g_fc2, g_fc1, g_out], ["rows", "cols", "cols"])
     g_qkv = [wgrad_cols(n1, x, groups) for x in (dq, dk, dv)]
     igrad, sums1, r_qkv = post_call(shape, dq, dk, dv, tok, flag, gh1, vec_pre, qkv_all, g_qkv, ["cols"] * 3)
-    ggm, gb2, a2, s2, gga, st0, st1, st2 = (sums[i:i + 1] for i in range(8))
-    a1, s1, gemb = (sums1[i:i + 1] for i in range(3))
-    gmod = jnp.concatenate([s1, a1 * gain1, gga, s2, a2 * gain2, ggm], axis=1)
-    small = jnp.concatenate([(1.0 + scale_a) * a1, (1.0 + scale_m) * a2, gb2, gemb, gb1, gmod], axis=1)
-    stats = jnp.concatenate([jnp.sum(st0).reshape(1, 1), jnp.sum(st1).reshape(1, 1), jnp.sum(st2).reshape(1, 1),
-                             lengths.astype(f32).reshape(1, 1), time_ids.astype(f32).reshape(1, 1)], axis=1)
-    row = jnp.concatenate([small, cond_pre, stats, jnp.zeros((1, 123), f32)], axis=1)
-    rows = lax.all_gather(row, ("dp", "fsdp"), axis=0, tiled=True)
-    width = small.shape[1]
-    conds, tail = rows[:, width:width + cond.shape[1]], rows[:, width + cond.shape[1]:]
-    gmods = rows[:, width - gmod.shape[1]:width]
-    silu_c, pull = jax.vjp(jax.nn.silu, conds)
-    grad_cond = pull(jnp.dot(gmods, ada_all.astype(f32), precision=highest))[0]
-    hot = (jnp.arange(time_table.shape[0])[:, None] == tail[:, 4].astype(jnp.int32)[None, :]).astype(f32)
-    table = jnp.dot(hot, grad_cond, precision=highest)
-    totals = jnp.sum(tail[:, :4], axis=0)
-    rms = jnp.sqrt(totals[:3] / (totals[3] * d))
-    me = lax.axis_index("fsdp")
-    parts, base = [], 0
-    for size in sizes:
-        parts.append(jnp.sum(lax.dynamic_slice_in_dim(rows, base + me * size, size, axis=1), axis=0))
-        base += size * groups
-    g1, g2, gb2, gemb, gb1, gbada = parts
-    n_ada = w_ada.shape[0]
-    mods = lax.dynamic_slice_in_dim(rows, width - gmod.shape[1] + me * n_ada, n_ada, axis=1)
-    g_ada = lax.dot_general(mods, silu_c, (((0,), (0,)), ((), ())), precision=highest)
-
+    meta = jnp.concatenate([jnp.zeros((3,), f32), lengths.astype(f32), time_ids.astype(f32), jnp.zeros((123,), f32)])[None]
+    g1, g2, gb2, gemb, gb1, g_ada, gbada, table, rms = small_results(
+        shape, small_call(shape, sums, gb1, sums1, vec_pre, vec_mid, cond_pre, meta, ada_all, time_table.shape[0]), sizes)
     return (out[None], igrad[None], g1, jnp.concatenate(r_qkv, axis=1).astype(f32), r_out.astype(f32), g2, r_fc1.astype(f32), gb1,
             r_fc2.astype(f32), gb2,
             g_ada, gbada, gemb, table, rms)

time: 384 us -> 335 us (0.87)
  waiting for transfers between devices: 45.9 us -> 0 us
  Pallas kernels: 283 us -> 301 us
  between operations: 16.2 us -> 2.19 us
  matrix products: 6.21 us -> 2.3 us
    all_gather x1 -> x0, waiting for transfers between devices: 45.9 us -> none  [per_device(): rows = lax.all_gather(row, ('dp', 'fsdp'), axis=0, tiled=True)]
    pallas_call x0 -> x1, Pallas kernels: none -> 18.5 us  [small_call(): pl.pallas_call(functools.partial(small_kernel, shape), in_specs=[vm] * 8,...]
    reduce_sum x5 -> x0, other arithmetic: 6.53 us -> none  [the longest x3 5.01 us: per_device(): jnp.sum(lax.dynamic_slice_in_dim(rows, base + me * size, size, axis=1), a...]
    dot_general x3 -> x0, matrix products: 3.9 us -> none  [the longest x1 1.91 us: per_device(): lax.dot_general(mods, silu_c, (((0,), (0,)), ((), ())), precision=highest)]
  transfers between devices with their start and end apart: 1 -> 0, of which waited for: 1 -> 0; matrix products, arithmetic and copies ran while one was open for 2% -> 0% of each run, Pallas kernels for 0% -> 0%
where the time goes in v4:
time: 335 us; the launch traced here: 334 us
  Pallas kernels  301 us (90%)
  local copies, waits for them, and re-layouts  15 us (4%)
  other arithmetic  13.9 us (4%)
    pallas_call x1, Pallas kernels, attn_bwd_call(): pl.pallas_call(functools.partial(attn_bwd_kernel, shape, counts, kinds, n...  78.5 us
    pallas_call x1, Pallas kernels, attn_fwd_call(): pl.pallas_call(functools.partial(attn_fwd_kernel, shape, len(ws), rows),...  51.1 us
    pallas_call x1, Pallas kernels, post_call(): pl.pallas_call(functools.partial(post_kernel, shape, counts, kinds, s //...  42.4 us
    pallas_call x1, Pallas kernels, mid_call(): pl.pallas_call(functools.partial(mid_kernel, cut=cut), grid=(s // rows,),...  37.7 us
    pallas_call x1, Pallas kernels, head_call(): pl.pallas_call(functools.partial(head_kernel, shape, len(ws)), in_specs=[...  27.3 us
    pallas_call x5, Pallas kernels, wgrad_cols(): pl.pallas_call(wgrad_cols_kernel, grid=(n // m,), in_specs=[pl.BlockSpec(...  26.5 us
    pallas_call x1, Pallas kernels, small_call(): pl.pallas_call(functools.partial(small_kernel, shape), in_specs=[vm] * 8,...  18.5 us
    pallas_call x1, Pallas kernels, pre_call(): pl.pallas_call(pre_kernel, grid=(s // rows,), in_specs=[pl.BlockSpec((row...  9.61 us

profile of v4, /device:TPU:0, one launch (start us, length us, event | category | flops | bytes accessed | tf_op | source)
XLA Modules:
  0.0 334.1 jit_solution(6688467695500171658)
XLA Ops:
  2.7 4.1 %concatenate.21 = bf16[2688]{0:T(1024)(128)(2,1)S(1)} concatenate(bf16[192]{0:T(256)(128)(2,1)} %param.22, bf16[192]{0:T(256)(128)(2,1)} %param.25, bf16[192]{0:T(256)(128)(2,1)} %param.29, bf16[192]{0:T(256)(128)(2,1)} %param.32, bf16[768]{0:T(1024)(128)(2,1)} %param.27, bf16[1152]{0:T(1024)(128)(2,1)} %param.31), dimensions={0} | concatenate | bytes 10752 | tf_op jit(solution)/shard_map/concatenate | solution.py:1002
  6.8 0.6 broadcast_in_dim.27.refs_2_
  7.6 3.0 sine_multiply_fusion
  10.6 1.0 copy.32.flag_ref.refs_4_
  11.6 27.3 %head.1 = (bf16[4,4,288,128]{3,2,1,0:T(8,128)(2,1)}, bf16[4,4,48,2304]{3,2,1,0:T(8,128)(2,1)}, bf16[4,1,2688]{2,1,0:T(2,128)(2,1)}) custom-call(bf16[4,288,128]{2,1,0:T(8,128)(2,1)} %bitcast.48, bf16[4,48,2304]{2,1,0:T(8,128)(2,1)} %bitcast.47, bf16[1,2688]{1,0:T(2,128)(2,1)} %broadcast_in_dim.27.refs_2_), custom_call_target="tpu_custom_call" | custom-call | tf_op jit(solution)/shard_map/head/pallas_call | solution.py:443
  38.9 0.8 copy.38
  40.7 2.3 convolution_reduce_fusion
  43.1 0.6 concatenate.25.vec_ref.vec_mid
  43.7 0.6 concatenate.23.vec_ref.refs_6_.vec_pre
  44.4 9.6 %pre.1 = (bf16[1024,768]{1,0:T(8,128)(2,1)}, bf16[1024,2304]{1,0:T(8,128)(2,1)}) custom-call(bf16[1024,768]{1,0:T(8,128)(2,1)} %bitcast.43, s32[1024,1]{1,0:T(8,128)} %copy.32.flag_ref.refs_4_, f32[8,768]{1,0:T(8,128)} %concatenate.23.vec_ref.refs_6_.vec_pre, bf16[768,2304]{1,0:T(8,128)(2,1)} %bitcast.41, f32[1024,128]{1,0:T(8,128)} %get-tuple-element.90.cos_ref.refs_7_, ...), custom_call_target="tpu_custom_call" | custom-call | flops 3623878656 | bytes 9437184 | tf_op jit(solution)/shard_map/pre/pallas_call | solution.py:50
  54.0 51.1 %attn_fwd.1 = (bf16[1024,768]{1,0:T(8,128)(2,1)}, f32[1024,128]{1,0:T(8,128)}, bf16[4,4,48,768]{3,2,1,0:T(8,128)(2,1)}, bf16[4,4,48,3072]{3,2,1,0:T(8,128)(2,1)}, bf16[4,4,192,768]{3,2,1,0:T(8,128)(2,1)}) custom-call(s32[1]{0:T(128)S(6)} %copy.42.refs_0_.len_ref, bf16[1024,2304]{1,0:T(8,128)(2,1)} %get-tuple-element.55.refs_1_.refs_2_.refs_3_, ...), custom_call_target="tpu_custom_call" | custom-call | flops 6442450944 | bytes 6291456 | tf_op jit(solution)/shard_map/attn_fwd/pallas_call | solution.py:748
  105.1 37.7 %mid.1 = (bf16[1024,768]{1,0:T(8,128)(2,1)}, f32[1024,768]{1,0:T(8,128)}, bf16[1024,768]{1,0:T(8,128)(2,1)}, bf16[1024,768]{1,0:T(8,128)(2,1)}, bf16[1024,3072]{...) custom-call(s32[1]{0:T(128)S(6)} %copy.42.refs_0_.len_ref, ...), custom_call_target="tpu_custom_call" | custom-call | flops 21743271936 | bytes 23592960 | tf_op jit(solution)/shard_map/mid/pallas_call | solution.py:227
  142.8 4.4 %wgrad_cols.6.refs_11_ = bf16[1,2,4,2,96,384]{5,4,3,2,1,0:T(8,128)(2,1)} custom-call(bf16[1024,768]{1,0:T(8,128)(2,1)} %get-tuple-element.56.att_ref.a_ref.refs_4_, bf16[1024,768]{1,0:T(8,128)(2,1)} %get-tuple-element.67.b_ref), custom_call_target="tpu_custom_call" | custom-call | flops 1207959552 | bytes 4325376 | tf_op jit(solution)/shard_map/wgrad_cols/pallas_call | solution.py:684
  147.2 9.2 %wgrad_rows.1.refs_9_ = bf16[4,2,4,2,96,384]{5,4,3,2,1,0:T(8,128)(2,1)} custom-call(bf16[1024,3072]{1,0:T(8,128)(2,1)} %get-tuple-element.63.a_ref, bf16[1024,768]{1,0:T(8,128)(2,1)} %get-tuple-element.64.b_ref), custom_call_target="tpu_custom_call" | custom-call | flops 4831838208 | bytes 12582912 | tf_op jit(solution)/shard_map/wgrad_rows/pallas_call | solution.py:704
  156.4 9.2 %wgrad_cols.5.refs_10_ = bf16[4,2,4,2,96,384]{5,4,3,2,1,0:T(8,128)(2,1)} custom-call(bf16[1024,768]{1,0:T(8,128)(2,1)} %get-tuple-element.65.a_ref, bf16[1024,3072]{1,0:T(8,128)(2,1)} %get-tuple-element.66.b_ref), custom_call_target="tpu_custom_call" | custom-call | flops 4831838208 | bytes 12582912 | tf_op jit(solution)/shard_map/wgrad_cols/pallas_call | solution.py:684
  165.5 78.5 %attn_bwd.1 = (bf16[1024,768]{1,0:T(8,128)(2,1)}, bf16[1024,768]{1,0:T(8,128)(2,1)}, bf16[1024,768]{1,0:T(8,128)(2,1)}, bf16[768,768]{1,0:T(8,128)(2,1)}, bf16[1...) custom-call(s32[1]{0:T(128)S(6)} %copy.42.refs_0_.len_ref, bf16[1024,2304]{1,0:T(8,128)(2,1)} %get-tuple-element.55.refs_1_.refs_2_.refs_3_, ...), custom_call_target="tpu_custom_call" | custom-call | flops 16106127360 | bytes 12582912 | tf_op jit(solution)/shard_map/attn_bwd/pallas_call | solution.py:783
  244.0 1.8 convert_element_type.102
  245.8 4.3 %wgrad_cols.7.refs_8_ = bf16[1,2,4,2,96,384]{5,4,3,2,1,0:T(8,128)(2,1)} custom-call(bf16[1024,768]{1,0:T(8,128)(2,1)} %get-tuple-element.72.a_ref, bf16[1024,768]{1,0:T(8,128)(2,1)} %get-tuple-element.68.b_ref.refs_0_), custom_call_target="tpu_custom_call" | custom-call | flops 1207959552 | bytes 4325376 | tf_op jit(solution)/shard_map/wgrad_cols/pallas_call | solution.py:684
  250.1 4.3 %wgrad_cols.8.refs_9_ = bf16[1,2,4,2,96,384]{5,4,3,2,1,0:T(8,128)(2,1)} custom-call(bf16[1024,768]{1,0:T(8,128)(2,1)} %get-tuple-element.72.a_ref, bf16[1024,768]{1,0:T(8,128)(2,1)} %get-tuple-element.69.b_ref.refs_1_), custom_call_target="tpu_custom_call" | custom-call | flops 1207959552 | bytes 4325376 | tf_op jit(solution)/shard_map/wgrad_cols/pallas_call | solution.py:684
  254.5 4.3 %wgrad_cols.9.refs_10_ = bf16[1,2,4,2,96,384]{5,4,3,2,1,0:T(8,128)(2,1)} custom-call(bf16[1024,768]{1,0:T(8,128)(2,1)} %get-tuple-element.72.a_ref, bf16[1024,768]{1,0:T(8,128)(2,1)} %get-tuple-element.70.b_ref.refs_2_), custom_call_target="tpu_custom_call" | custom-call | flops 1207959552 | bytes 4325376 | tf_op jit(solution)/shard_map/wgrad_cols/pallas_call | solution.py:684
  258.8 42.4 %post.1 = (bf16[1024,768]{1,0:T(8,128)(2,1)}, f32[8,768]{1,0:T(8,128)}, bf16[192,768]{1,0:T(8,128)(2,1)}, bf16[192,768]{1,0:T(8,128)(2,1)}, bf16[192,768]{1,0:T(8,128)(2,1)}) custom-call(bf16[1024,768]{1,0:T(8,128)(2,1)} %get-tuple-element.68.b_ref.refs_0_, bf16[1024,768]{1,0:T(8,128)(2,1)} %get-tuple-element.69.b_ref.refs_1_, ...), custom_call_target="tpu_custom_call" | custom-call | flops 3623878656 | bytes 12582912 | tf_op jit(solution)/shard_map/post/pallas_call | solution.py:816
  301.2 18.5 %small.1 = (f32[8,256]{1,0:T(8,128)}, f32[1,768]{1,0:T(1,128)}, f32[1152,128]{1,0:T(8,128)}, f32[1,1152]{1,0:T(1,128)}, f32[1000,128]{1,0:T(8,128)}, /*index=5*/f32[1,128]{1,0:T(1,128)}) custom-call(f32[8,768]{1,0:T(8,128)} %get-tuple-element.74.sums, f32[1,3072]{1,0:T(1,128)} %get-tuple-element.75.sb1, f32[8,768]{1,0:T(8,128)} %get-tuple-element.76.sums1, ...), custom_call_target="tpu_custom_call" | custom-call | tf_op jit(solution)/shard_map/small/pallas_call | solution.py:964
  319.7 1.4 fusion.7
  321.1 1.1 slice_bitcast_fusion
  322.2 1.3 reduce.1
  323.5 1.3 reduce.2
  324.8 2.5 maximum_convert_fusion
  327.3 1.7 convert_element_type.103
  329.0 1.6 convert_element_type.104
  331.1 1.1 copy.44
  332.5 0.8 copy.45
  333.3 0.8 copy.46
  (39 shorter events, 2.7 us)
Async XLA Ops:
  0.6 1.4 copy-start
  0.7 9.9 %copy-start.7 = (s32[1,1024]{1,0:T(1,128)S(1)}, s32[1,1024]{1,0:T(1,128)}, u32[]{:S(2)}) copy-start(s32[1,1024]{1,0:T(1,128)} %param.18) | copy-start | bytes 12292
  2.1 38.7 %copy-start.8 = (f32[1,128]{1,0:T(1,128)}, f32[1,128]{1,0:T(1,128)S(1)}, u32[]{:S(2)}) copy-start(f32[1,128]{1,0:T(1,128)S(1)} %constant_dynamic-slice_fusion.condp) | copy-start | bytes 1540
  319.7 7.6 %copy-start.4 = (bf16[192,3072]{1,0:T(8,128)(2,1)S(1)}, bf16[192,3072]{1,0:T(8,128)(2,1)}, u32[]{:S(2)}) copy-start(bf16[192,3072]{1,0:T(8,128)(2,1)} %get-tuple-element.82) | copy-start | bytes 3538948
  327.3 1.7 copy-start.3
  329.0 2.1 copy-start.2
  331.1 1.4 copy-start.5
  331.1 2.3 copy-start.6
  331.1 3.0 copy-start.1

commit v5 on v4

--- a/solution.py
+++ b/solution.py
@@ -31,7 +31,7 @@
     h0 = jnp.where(flag_ref[...] == 1, emb, tok_ref[...].astype(f32))
     n, _ = norm_parts(h0)
     n1 = (n * gain * (1.0 + scale) + shift).astype(bf16)
-    n1_ref[...] = n1
+    n1_ref[...] = n1.astype(f32).T.astype(bf16)
     d = n1.shape[1]
     cos, sin = cos_ref[...], sin_ref[...]
     for part in range(3):
@@ -52,8 +52,8 @@
         in_specs=[pl.BlockSpec((rows, d), lambda i: (i, 0)), pl.BlockSpec((rows, 1), lambda i: (i, 0)),
                   pl.BlockSpec((8, d), lambda i: (0, 0)), pl.BlockSpec((d, 3 * d), lambda i: (0, 0)),
                   pl.BlockSpec((rows, 128), lambda i: (i, 0)), pl.BlockSpec((rows, 128), lambda i: (i, 0))],
-        out_specs=[pl.BlockSpec((rows, d), lambda i: (i, 0)), pl.BlockSpec((rows, 3 * d), lambda i: (i, 0))],
-        out_shape=[jax.ShapeDtypeStruct((s, d), bf16), jax.ShapeDtypeStruct((s, 3 * d), bf16)],
+        out_specs=[pl.BlockSpec((d, rows), lambda i: (0, i)), pl.BlockSpec((rows, 3 * d), lambda i: (i, 0))],
+        out_shape=[jax.ShapeDtypeStruct((d, s), bf16), jax.ShapeDtypeStruct((s, 3 * d), bf16)],
         cost_estimate=pl.CostEstimate(flops=2 * s * d * 3 * d, bytes_accessed=12 * s * d, transcendentals=0),
         name="pre")(tok, flag, vecs, w, cos, sin)
 
@@ -99,8 +99,7 @@
     return hi, mid, r - mid
 
 def attn_bwd_body(len_ref, q_ref, k_ref, v_ref, o_ref, g_ref, lse_ref, cos_ref, sin_ref,
-                  dq_ref, dk_ref, dv_ref, dqs, dks, dvs, rows):
-    p, h = pl.program_id(0), pl.program_id(1)
+                  dqs, dks, dvs, rows, p, h, emit):
     s = q_ref.shape[0]
     length = len_ref[0]
     lane = lax.broadcasted_iota(jnp.int32, (s, 128), 1)
@@ -146,9 +145,8 @@
         cos, sin = cos_ref[...], sin_ref[...]
         dq = dqs[...].T * (HD ** -0.5)
         dkk = jnp.where(lane < HD, dks[...], dk) * (1.0 / LOG2E)
-        dq_ref[...] = (dq * cos - swap_halves(dq) * sin).astype(bf16)
-        dk_ref[...] = (dkk * cos - swap_halves(dkk) * sin).astype(bf16)
-        dv_ref[...] = jnp.where(lane < HD, dvs[...], dv).astype(bf16)
+        emit((dq * cos - swap_halves(dq) * sin).astype(bf16), (dkk * cos - swap_halves(dkk) * sin).astype(bf16),
+             jnp.where(lane < HD, dvs[...], dv).astype(bf16))
 
 
 def gelu_both(v):
@@ -238,27 +236,15 @@
                                       transcendentals=s * ff),
         name="mid")(length, att, tok, flag, cot, vec, b1, wo, w1, w2)
 
-def post_body(dq_ref, dk_ref, dv_ref, tok_ref, flag_ref, gh1_ref, vec_ref, w_ref, ig_ref, sum_ref):
-    i = pl.program_id(0)
-    d = tok_ref.shape[1]
-    emb, gain, scale = (vec_ref[r:r + 1, :] for r in range(3))
-    masked = flag_ref[...] == 1
-    h0 = jnp.where(masked, emb, tok_ref[...].astype(f32))
+def post_rows(grads, h0, masked, gh1, gain, scale, w_ref):
+    d = h0.shape[1]
     n, rs = norm_parts(h0)
-    gn1 = dot(dq_ref[...], w_ref[:, :d], NT) + dot(dk_ref[...], w_ref[:, d:2 * d], NT) + dot(
-        dv_ref[...], w_ref[:, 2 * d:], NT)
+    gn1 = sum(dot(g, w_ref[:, i * d:(i + 1) * d], NT) for i, g in enumerate(grads))
     e = gn1 * (gain * (1.0 + scale))
-    gh0 = gh1_ref[...] + rs * (e - jnp.mean(e, axis=1, keepdims=True) - n * jnp.mean(e * n, axis=1, keepdims=True))
-    ig_ref[...] = jnp.where(masked, 0.0, gh0).astype(bf16)
-    zero = jnp.zeros((5, d), f32)
-    new = jnp.concatenate([colsum(gn1 * n), colsum(gn1), colsum(jnp.where(masked, gh0, 0.0)), zero], axis=0)
-    @pl.when(i == 0)
-    def _():
-        sum_ref[...] = new
-    @pl.when(i > 0)
-    def _():
-        sum_ref[...] += new
-
+    gh0 = gh1 + rs * (e - jnp.mean(e, axis=1, keepdims=True) - n * jnp.mean(e * n, axis=1, keepdims=True))
+    sums = jnp.concatenate([colsum(gn1 * n), colsum(gn1), colsum(jnp.where(masked, gh0, 0.0)),
+                            jnp.zeros((5, d), f32)], axis=0)
+    return jnp.where(masked, 0.0, gh0).astype(bf16), sums
 
 MESH = pl.DeviceIdType.MESH
 
@@ -449,7 +435,7 @@
 
 
 class Reduce:
-    def __init__(self, place, counts, kinds, srcs, outs, scratch, lag=(1, 2)):
+    def __init__(self, place, counts, kinds, srcs, outs, scratch, lag, gap):
         self.p, self.counts, self.kinds, self.srcs, self.outs = place, counts, kinds, srcs, outs
         (self.own, self.cb, self.xb, self.zb, self.mb, self.u2, self.fin,
          self.load, self.cs, self.cr, self.xs, self.xr, self.zs, self.zr, self.ms, self.mr, self.fs, self.fr,
@@ -467,8 +453,9 @@
         self.stages = ([self.begin, self.core_add] + [functools.partial(self.group_add, t) for t in range(p.bits)]
                        + [functools.partial(self.climb, j) for j in range(1, self.last + 1)] + [self.middle]
                        + [functools.partial(self.descend, j) for j in range(self.last - 1, -1, -1)])
-        self.lags = [0, lag[0]] + [lag[0] + lag[1] * (i + 1) for i in range(len(self.stages) - 2)]
-        self.ticks = self.total + self.lags[-1]
+        self.lags = [lag * i for i in range(len(self.stages))]
+        self.gap = gap
+        self.ticks = self.total + gap + self.lags[-1]
 
     @staticmethod
     def scratch(total, groups, rows, cols):
@@ -478,18 +465,14 @@
         line = pltpu.VMEM((total, rows, cols), bf16)
         return [vm(groups, 2), vm(groups, 2), vm(2, groups - 1), line, line, line, line,
                 one, one, one, sem((total, 2, groups - 1)), sem((total, 2, groups - 1)),
-                one, one, one, one, one, one, one, one, one]
-
-    def greet(self):
+                one, one, one, one, one, one, sem((total, 3)), sem((total, 3)), sem((total, 3))]
+
+    def greet(self, peers):
         p = self.p
         barrier = pltpu.get_barrier_semaphore()
-        for where in [(p.partner, p.me)] + [(p.dp, flip(p.me, b)) for b in range(p.bits)] + [self.inner]:
+        for where in peers:
             pl.semaphore_signal(barrier, inc=1, device_id=where, device_id_type=MESH)
-        @pl.when(self.e > 0)
-        def _():
-            pl.semaphore_signal(barrier, inc=1, device_id=self.outer, device_id_type=MESH)
-        half = self.n // 2
-        pl.semaphore_wait(barrier, 2 + p.bits + (self.e + half - 1) // half)
+        pl.semaphore_wait(barrier, len(peers))
 
     def source(self, k, fn):
         base = 0
@@ -499,12 +482,19 @@
                 fn(i, k - base)
             base += count
 
-    def target(self, i, j, core):
+    def targets(self, k, i, j, core):
         rows, cols = self.fin.shape[1:]
-        out = self.outs[i]
+        out, fin = self.outs[i], self.fin.at[k]
+        if self.kinds[i] == "rows":
+            cut = pl.ds(pl.multiple_of(core * cols, cols), cols)
+            return [(fin, out.at[pl.ds(pl.multiple_of(j * rows, rows), rows), cut])]
+        down = pl.ds(pl.multiple_of((j % 2) * rows, rows), rows)
         if self.kinds[i] == "cols":
-            return out.at[:, pl.ds(pl.multiple_of((2 * j + core) * cols, cols), cols)]
-        return out.at[pl.ds(pl.multiple_of(j * rows, rows), rows), pl.ds(pl.multiple_of(core * cols, cols), cols)]
+            return [(fin, out.at[down, pl.ds(pl.multiple_of((2 * (j // 2) + core) * cols, cols), cols)])]
+        width = out.shape[1] // 3
+        pair = 2 * (j // 2) + core
+        return [(fin.at[:, part * 128:(part + 1) * 128],
+                 out.at[down, pl.ds(pl.multiple_of(part * width + pair * 128, 128), 128)]) for part in range(3)]
 
     def load_copy(self, k, src):
         return pltpu.make_async_copy(src.at[self.p.core], self.own.at[k], self.load.at[k])
@@ -587,17 +577,30 @@
     def share_wait(self, k):
         return remote(self.fin.at[k], self.fin.at[k], self.fs.at[k], self.fr.at[k], self.inner)
 
-    def pass_copy(self, k, dst):
-        p = self.p
-        return remote(self.fin.at[k], dst, self.ps.at[k], self.pr.at[k], (p.partner, p.me))
-
-    def store_copy(self, k, dst):
-        return pltpu.make_async_copy(self.fin.at[k], dst, self.st.at[k])
+    def out_copies(self, k, i, j):
+        p = self.p
+        mine, other = self.targets(k, i, j, p.core), self.targets(k, i, j, 1 - p.core)
+        sent = [remote(s, d, self.ps.at[k, n], self.pr.at[k, n], (p.partner, p.me)) for n, (s, d) in enumerate(mine)]
+        kept = [pltpu.make_async_copy(s, d, self.st.at[k, n]) for n, (s, d) in enumerate(mine)]
+        return sent, kept, other
 
     def done(self, k):
         def go(i, j):
-            self.pass_copy(k, self.target(i, j, self.p.core)).start()
-            self.store_copy(k, self.target(i, j, self.p.core)).start()
+            sent, kept, _ = self.out_copies(k, i, j)
+            for c in sent + kept:
+                c.start()
+        self.source(k, go)
+
+    def retire(self, k):
+        p = self.p
+        def go(i, j):
+            sent, kept, other = self.out_copies(k, i, j)
+            for n, c in enumerate(sent):
+                c.wait_send()
+                s, d = other[n]
+                remote(s, d, self.ps.at[k, n], self.pr.at[k, n], (p.partner, p.me)).wait_recv()
+            for c in kept:
+                c.wait()
         self.source(k, go)
 
     def middle(self, k):
@@ -622,23 +625,9 @@
     def tick(self, t):
         for s in range(len(self.stages) - 1, -1, -1):
             k = t - self.lags[s]
-            @pl.when((k >= 0) & (k < self.total))
+            @pl.when((k >= 0) & (k < self.total + self.gap) & ((k < self.total - self.gap) | (k >= self.total)))
             def _(s=s, k=k):
-                self.stages[s](k)
-
-    def opening(self, step):
-        @pl.when(step == 0)
-        def _():
-            self.greet()
-        self.tick(step)
-
-    def closing(self, step, steps):
-        @pl.when(step == steps - 1)
-        def _():
-            @pl.loop(steps, max(self.ticks, steps))
-            def _(t):
-                self.tick(t)
-            self.drain()
+                self.stages[s](k - self.gap * (k // self.total))
 
     def drain(self):
         p = self.p
@@ -658,34 +647,27 @@
             @pl.when(self.e > 0)
             def _():
                 self.share_copy(k).wait_send()
-            def go(i, j):
-                self.pass_copy(k, self.target(i, j, 1 - p.core)).wait()
-                self.store_copy(k, self.target(i, j, p.core)).wait()
-            self.source(k, go)
-
-
-def reduced_shapes(grads, kinds):
-    rows, cols = 2 * grads[0].shape[-2], 2 * grads[0].shape[-1]
-    return [jax.ShapeDtypeStruct((rows, g.shape[0] * cols) if kind == "cols" else (g.shape[0] * rows, cols), bf16)
-            for g, kind in zip(grads, kinds)]
+            self.retire(k)
 
 
 def wgrad_cols_kernel(a_ref, b_ref, o_ref):
     y = dot(a_ref[...], b_ref[...], TN).astype(bf16)
     _, _, g, _, r, c = o_ref.shape
-    for half in (0, 1):
-        o_ref[0, half] = y[:, half * c:(half + 1) * c].reshape(g, 2, r, c)
+    for core in (0, 1):
+        z = y[:, core * c:(core + 1) * c].reshape(g, 2, 2, r, c)
+        for half in (0, 1):
+            o_ref[half, core] = z[:, half]
 
 
 def wgrad_cols(a, b, groups):
     s, m = a.shape
     n = b.shape[1]
-    r, c = m // groups // 2, m // 2
+    r, c = m // groups // 4, m // 2
     return pl.pallas_call(
         wgrad_cols_kernel, grid=(n // m,),
         in_specs=[pl.BlockSpec((s, m), lambda i: (0, 0)), pl.BlockSpec((s, m), lambda i: (0, i))],
-        out_specs=pl.BlockSpec((1, 2, groups, 2, r, c), lambda i: (i, 0, 0, 0, 0, 0)),
-        out_shape=jax.ShapeDtypeStruct((n // m, 2, groups, 2, r, c), bf16),
+        out_specs=pl.BlockSpec((2, 2, groups, 2, r, c), lambda i: (i, 0, 0, 0, 0, 0)),
+        out_shape=jax.ShapeDtypeStruct((2 * n // m, 2, groups, 2, r, c), bf16),
         cost_estimate=pl.CostEstimate(flops=2 * s * m * n, bytes_accessed=2 * (s * (m + n) + m * n),
                                       transcendentals=0), name="wgrad_cols")(a, b)
 
@@ -693,14 +675,14 @@
 def wgrad_rows_kernel(a_ref, b_ref, o_ref):
     y = dot(a_ref[...], b_ref[...], TN).astype(bf16)
     q, _, _, _, r, c = o_ref.shape
-    for half in (0, 1):
-        o_ref[:, half, 0] = y[:, half * c:(half + 1) * c].reshape(q, 2, r, c)
+    for core in (0, 1):
+        o_ref[:, core, 0] = y[:, core * c:(core + 1) * c].reshape(q, 2, r, c)
 
 
 def wgrad_rows(a, b, groups):
     s, m = a.shape
     n = b.shape[1]
-    q, r, c = m // n, n // groups // 2, n // 2
+    q, r, c = 2 * m // n, n // groups // 4, n // 2
     return pl.pallas_call(
         wgrad_rows_kernel, grid=(groups,),
         in_specs=[pl.BlockSpec((s, m // groups), lambda i: (0, i)), pl.BlockSpec((s, n), lambda i: (0, 0))],
@@ -760,70 +742,6 @@
     return res[0], res[1], [r.reshape(-1, r.shape[-1]) for r in res[2:]]
 
 
-def attn_bwd_kernel(shape, counts, kinds, pairs, rows, *refs):
-    n = len(counts)
-    ins, srcs, grads, outs = refs[:9], refs[9:9 + n], refs[9 + n:12 + n], refs[12 + n:12 + 2 * n]
-    work, scratch = refs[12 + 2 * n:15 + 2 * n], refs[15 + 2 * n:]
-    step = pl.program_id(0) * 2 + pl.program_id(1)
-    r = Reduce(Place(shape), counts, kinds, srcs, outs, scratch)
-    r.opening(step)
-    attn_bwd_body(*ins, *grads, *work, rows)
-    r.closing(step, 2 * pairs)
-
-
-def attn_bwd_call(shape, length, qkv, att, gatt, lse, cos, sin, grads, kinds, rows=256):
-    groups = shape["fsdp"]
-    s, d3 = qkv.shape
-    d = d3 // 3
-    np_ = d // 128
-    counts = [g.shape[0] for g in grads]
-    r, c = 2 * grads[0].shape[-2], grads[0].shape[-1]
-    col = pl.BlockSpec((s, 128), lambda i, h: (0, i))
-    const = pl.BlockSpec((s, 128), lambda i, h: (0, 0))
-    res = pl.pallas_call(
-        functools.partial(attn_bwd_kernel, shape, counts, kinds, np_, rows), grid=(np_, 2),
-        in_specs=[pl.BlockSpec(memory_space=pltpu.SMEM), col,
-                  pl.BlockSpec((s, 128), lambda i, h: (0, np_ + i)),
-                  pl.BlockSpec((s, 128), lambda i, h: (0, 2 * np_ + i)), col, col, const, const, const]
-        + [ANY] * len(grads),
-        out_specs=[col, col, col] + [ANY] * len(grads),
-        out_shape=[jax.ShapeDtypeStruct((s, d), bf16)] * 3 + reduced_shapes(grads, kinds),
-        scratch_shapes=[pltpu.VMEM((128, s), f32), pltpu.VMEM((s, 128), f32), pltpu.VMEM((s, 128), f32)]
-        + Reduce.scratch(sum(counts), groups, r, c),
-        compiler_params=pltpu.CompilerParams(collective_id=3, has_side_effects=True, vmem_limit_bytes=64000 * 1024),
-        cost_estimate=pl.CostEstimate(flops=20 * s * s * d, bytes_accessed=16 * s * d, transcendentals=s * s * 12),
-        name="attn_bwd")(length, qkv, qkv, qkv, att, gatt, lse, cos, sin, *grads)
-    return res[:3], res[3:]
-
-
-def post_kernel(shape, counts, kinds, steps, *refs):
-    n = len(counts)
-    ins, srcs, outs, reduced = refs[:8], refs[8:8 + n], refs[8 + n:10 + n], refs[10 + n:10 + 2 * n]
-    r = Reduce(Place(shape), counts, kinds, srcs, reduced, refs[10 + 2 * n:])
-    step = pl.program_id(0)
-    r.opening(step)
-    post_body(*ins, *outs)
-    r.closing(step, steps)
-
-
-def post_call(shape, dq, dk, dv, tok, flag, gh1, vec, w, grads, kinds, rows=128):
-    s, d = tok.shape
-    row = lambda c: pl.BlockSpec((rows, c), lambda i: (i, 0))
-    whole = lambda a: pl.BlockSpec(a.shape, lambda i: (0, 0))
-    sd = jax.ShapeDtypeStruct
-    counts = [g.shape[0] for g in grads]
-    r, c = 2 * grads[0].shape[-2], grads[0].shape[-1]
-    res = pl.pallas_call(
-        functools.partial(post_kernel, shape, counts, kinds, s // rows), grid=(s // rows,),
-        in_specs=[row(d), row(d), row(d), row(d), row(1), row(d), whole(vec), whole(w)] + [ANY] * len(grads),
-        out_specs=[row(d), pl.BlockSpec((8, d), lambda i: (0, 0))] + [ANY] * len(grads),
-        out_shape=[sd((s, d), bf16), sd((8, d), f32)] + reduced_shapes(grads, kinds),
-        scratch_shapes=Reduce.scratch(sum(counts), shape["fsdp"], r, c),
-        compiler_params=pltpu.CompilerParams(collective_id=4, has_side_effects=True, vmem_limit_bytes=64000 * 1024),
-        cost_estimate=pl.CostEstimate(flops=6 * s * d * d, bytes_accessed=16 * s * d, transcendentals=0),
-        name="post")(dq, dk, dv, tok, flag, gh1, vec, w, *grads)
-    return res[0], res[1], res[2:]
-
 def f32_rows_dot(row, weights):
     parts = split3(row)
     stack = jnp.concatenate(list(parts) + [jnp.zeros((5, row.shape[1]), f32)], axis=0).astype(bf16)
@@ -942,30 +860,10 @@
         rms_ref[...] = jnp.sqrt(stat / (stat[:, 3:4] * d))
 
 
-def small_kernel(shape, sums, sb1, sums1, vec_pre, vec_mid, condp, meta, ada, norms, gb1, gada, gbada, table, rms,
-                 *scratch):
-    s = Small(Place(shape), scratch)
-    greet(s.peers())
-    s.first(sums[...], sb1[...], sums1[...], vec_pre[...], vec_mid[...], condp[...], meta[...], ada[...])
-    s.second()
-    s.third(norms, gb1, gada, gbada, table, rms, sums.shape[1])
-    s.settle()
-
-
 def small_shapes(shape, d, ff, n_mod, table_rows):
     wide, fpart, gpart = Small.widths(shape, d, ff, n_mod)
     sd = lambda *dims: jax.ShapeDtypeStruct(dims, f32)
     return [sd(8, wide), sd(1, fpart), sd(gpart, 128), sd(1, gpart), sd(table_rows, 128), sd(1, 128)]
-
-
-def small_call(shape, sums, sb1, sums1, vec_pre, vec_mid, condp, meta, ada, table_rows):
-    d, ff, n_mod = sums.shape[1], sb1.shape[1], ada.shape[0]
-    vm = pl.BlockSpec(memory_space=pltpu.VMEM)
-    return pl.pallas_call(
-        functools.partial(small_kernel, shape), in_specs=[vm] * 8, out_specs=[vm] * 6,
-        out_shape=small_shapes(shape, d, ff, n_mod, table_rows), scratch_shapes=Small.scratch(shape, d, ff, n_mod),
-        compiler_params=pltpu.CompilerParams(collective_id=5, has_side_effects=True), name="small",
-    )(sums, sb1, sums1, vec_pre, vec_mid, condp, meta, ada)
 
 
 def small_results(shape, res, sizes):
@@ -977,6 +875,109 @@
         gbada = lax.dynamic_slice_in_dim(gbada, me * n_ada, n_ada, axis=1)
     g1, g2, gb2, gemb = (norms[i, :sizes[i]] for i in range(4))
     return g1, g2, gb2, gemb, gb1[0], gada, gbada[0], table, rms[0, :3]
+
+
+def tail_kernel(shape, counts, rows, post, pairs, *refs):
+    n = len(counts)
+    (len_ref, q_ref, k_ref, v_ref, o_ref, g_ref, lse_ref, cos_ref, sin_ref, n1_ref, w_ref, tok_ref, flag_ref, gh1_ref,
+     vpre_ref, vmid_ref, sums_ref, sb1_ref, condp_ref, meta_ref, ada_ref) = refs[:21]
+    srcs = refs[21:20 + n]
+    outs = refs[20 + n:21 + 2 * n]
+    igrad_ref, reduced, small_out = outs[0], outs[1:1 + n], refs[21 + 2 * n:27 + 2 * n]
+    dqs, dks, dvs, dqkv, gq, sums1 = refs[27 + 2 * n:33 + 2 * n]
+    rscratch, sscratch = refs[33 + 2 * n:54 + 2 * n], refs[54 + 2 * n:]
+    step, steps = pl.program_id(0), 2 * pairs + post
+    p = Place(shape)
+    r = Reduce(p, counts, ["rows"] + ["cols"] * (n - 2) + ["qkv"], list(srcs) + [gq], reduced, rscratch, 2, 2)
+    small = Small(p, sscratch)
+
+    @pl.when(step == 0)
+    def _():
+        r.greet(small.peers())
+
+    @pl.loop(2 * step, 2 * step + 2)
+    def _(t):
+        r.tick(t)
+
+    @pl.when(step < 2 * pairs)
+    def _():
+        pair, head = step // 2, step % 2
+
+        def emit(*parts):
+            for i, x in enumerate(parts):
+                dqkv[i, pair] = x
+            y = dot(n1_ref[...], jnp.concatenate(parts, axis=1)).astype(bf16)
+            _, _, g, _, rr, c = gq.shape
+            y = y.reshape(g, 2, 2, rr, c)
+            for half in (0, 1):
+                gq[2 * (pair // 2) + half, pair % 2] = y[:, half]
+
+        attn_bwd_body(len_ref, q_ref, k_ref, v_ref, o_ref, g_ref, lse_ref, cos_ref, sin_ref, dqs, dks, dvs, rows,
+                      pair, head, emit)
+
+    @pl.when(step >= 2 * pairs)
+    def _():
+        i = step - 2 * pairs
+        m = tok_ref.shape[0]
+        cut = pl.ds(pl.multiple_of(i * m, m), m)
+        grads = [jnp.concatenate([dqkv[a, b, cut, :] for b in range(pairs)], axis=1) for a in range(3)]
+        masked = flag_ref[...] == 1
+        h0 = jnp.where(masked, vpre_ref[0:1, :], tok_ref[...].astype(f32))
+        igrad_ref[...], new = post_rows(grads, h0, masked, gh1_ref[...], vpre_ref[1:2, :], vpre_ref[2:3, :], w_ref)
+        sums1[...] = jnp.where(i == 0, new, sums1[...] + new)
+
+    @pl.when(step == steps - 1)
+    def _():
+        small.first(sums_ref[...], sb1_ref[...], sums1[...], vpre_ref[...], vmid_ref[...], condp_ref[...], meta_ref[...],
+                    ada_ref[...])
+        small.second()
+        @pl.loop(2 * steps, max(r.ticks, 2 * steps))
+        def _(t):
+            r.tick(t)
+        small.third(*small_out, sums1.shape[1])
+        r.drain()
+        small.settle()
+
+
+def tail_call(shape, length, qkv, att, gatt, lse, cos, sin, n1t, w, tok, flag, gh1, vpre, vmid, sums, sb1, condp, meta,
+              ada, grads, table_rows, rows=256, post=128):
+    groups = shape["fsdp"]
+    s, d3 = qkv.shape
+    d = d3 // 3
+    pairs = d // 128
+    blocks = s // post
+    steps = 2 * pairs + blocks
+    ff, n_mod = sb1.shape[1], ada.shape[0]
+    r, c = 2 * grads[0].shape[-2], grads[0].shape[-1]
+    counts = [g.shape[0] for g in grads] + [pairs]
+    pair = lambda i: jnp.minimum(i // 2, pairs - 1)
+    blk = lambda i: jnp.maximum(i - 2 * pairs, 0)
+    once = pl.Buffered(1)
+    col = lambda base: pl.BlockSpec((s, 128), lambda i: (0, base + pair(i)))
+    whole = lambda a: pl.BlockSpec(a.shape, lambda i: (0,) * a.ndim, pipeline_mode=once)
+    row = lambda cc: pl.BlockSpec((post, cc), lambda i: (blk(i), 0))
+    sd = jax.ShapeDtypeStruct
+    shard = d // groups
+    red = [sd((shard * (g.shape[0] // 2), d), bf16) if i == 0 else sd((shard, d * (g.shape[0] // 2)), bf16)
+           for i, g in enumerate(grads)] + [sd((shard, d3), bf16)]
+    smalls = small_shapes(shape, d, ff, n_mod, table_rows)
+    const = lambda x: pl.BlockSpec(x.shape, lambda i: (0, 0), pipeline_mode=once)
+    res = pl.pallas_call(
+        functools.partial(tail_kernel, shape, counts, rows, blocks, pairs), grid=(steps,),
+        in_specs=[pl.BlockSpec(memory_space=pltpu.SMEM), col(0), col(pairs), col(2 * pairs), col(0), col(0), whole(lse),
+                  whole(cos), whole(sin), whole(n1t), whole(w), row(d), row(1), row(d)]
+        + [whole(x) for x in (vpre, vmid, sums, sb1, condp, meta, ada)] + [ANY] * len(grads),
+        out_specs=[row(d)] + [ANY] * len(red) + [const(x) for x in smalls],
+        out_shape=[sd((s, d), bf16)] + red + smalls,
+        scratch_shapes=[pltpu.VMEM((128, s), f32), pltpu.VMEM((s, 128), f32), pltpu.VMEM((s, 128), f32),
+                        pltpu.VMEM((3, pairs, s, 128), bf16), pltpu.VMEM((pairs, 2, groups, 2, r // 2, c), bf16),
+                        pltpu.VMEM((8, d), f32)]
+        + Reduce.scratch(sum(counts), groups, r, c) + Small.scratch(shape, d, ff, n_mod),
+        compiler_params=pltpu.CompilerParams(collective_id=3, has_side_effects=True, vmem_limit_bytes=65000 * 1024),
+        cost_estimate=pl.CostEstimate(flops=30 * s * s * d, bytes_accessed=40 * s * d, transcendentals=s * s * 12),
+        name="tail")(length, qkv, qkv, qkv, att, gatt, lse, cos, sin, n1t, w, tok, flag, gh1, vpre, vmid, sums, sb1, condp,
+                     meta, ada, *grads)
+    return res[0], res[1:1 + len(red)], res[1 + len(red):]
 from jax.sharding import PartitionSpec as P
 
 highest = lax.Precision.HIGHEST
@@ -1020,14 +1021,12 @@
     g_fc2 = wgrad_rows(act, gm, groups)
     g_fc1 = wgrad_cols(n2, gpre, groups)
     g_out = wgrad_cols(att, gap, groups)
-    (dq, dk, dv), (r_fc2, r_fc1, r_out) = attn_bwd_call(
-        shape, lengths, qkv, att, gatt, lse, cos, sin, [g_fc2, g_fc1, g_out], ["rows", "cols", "cols"])
-    g_qkv = [wgrad_cols(n1, x, groups) for x in (dq, dk, dv)]
-    igrad, sums1, r_qkv = post_call(shape, dq, dk, dv, tok, flag, gh1, vec_pre, qkv_all, g_qkv, ["cols"] * 3)
     meta = jnp.concatenate([jnp.zeros((3,), f32), lengths.astype(f32), time_ids.astype(f32), jnp.zeros((123,), f32)])[None]
-    g1, g2, gb2, gemb, gb1, g_ada, gbada, table, rms = small_results(
-        shape, small_call(shape, sums, gb1, sums1, vec_pre, vec_mid, cond_pre, meta, ada_all, time_table.shape[0]), sizes)
-    return (out[None], igrad[None], g1, jnp.concatenate(r_qkv, axis=1).astype(f32), r_out.astype(f32), g2, r_fc1.astype(f32), gb1,
+    igrad, (r_fc2, r_fc1, r_out, r_qkv), smalls = tail_call(
+        shape, lengths, qkv, att, gatt, lse, cos, sin, n1, qkv_all, tok, flag, gh1, vec_pre, vec_mid, sums, gb1, cond_pre,
+        meta, ada_all, [g_fc2, g_fc1, g_out], time_table.shape[0])
+    g1, g2, gb2, gemb, gb1, g_ada, gbada, table, rms = small_results(shape, smalls, sizes)
+    return (out[None], igrad[None], g1, r_qkv.astype(f32), r_out.astype(f32), g2, r_fc1.astype(f32), gb1,
             r_fc2.astype(f32), gb2,
             g_ada, gbada, gemb, table, rms)
 

time: 335 us -> 303 us (0.904)
  Pallas kernels: 301 us -> 269 us
    pallas_call x3 -> x1, Pallas kernels: 139 us -> 120 us  [tail_call(): pl.pallas_call(functools.partial(tail_kernel, shape, counts, rows, blocks...]
    pallas_call x5 -> x2, Pallas kernels: 26.5 us -> 13.5 us  [wgrad_cols(): pl.pallas_call(wgrad_cols_kernel, grid=(n // m,), in_specs=[pl.BlockSpec(...]
where the time goes in v5:
time: 303 us
  Pallas kernels  269 us (89%)
  local copies, waits for them, and re-layouts  15.7 us (5%)
  other arithmetic  14.1 us (5%)
    pallas_call x1, Pallas kernels, tail_call(): pl.pallas_call(functools.partial(tail_kernel, shape, counts, rows, blocks...  120 us
    pallas_call x1, Pallas kernels, attn_fwd_call(): pl.pallas_call(functools.partial(attn_fwd_kernel, shape, len(ws), rows),...  51.1 us
    pallas_call x1, Pallas kernels, mid_call(): pl.pallas_call(functools.partial(mid_kernel, cut=cut), grid=(s // rows,),...  37.7 us
    pallas_call x1, Pallas kernels, head_call(): pl.pallas_call(functools.partial(head_kernel, shape, len(ws)), in_specs=[...  27.3 us
    pallas_call x2, Pallas kernels, wgrad_cols(): pl.pallas_call(wgrad_cols_kernel, grid=(n // m,), in_specs=[pl.BlockSpec(...  13.5 us
    pallas_call x1, Pallas kernels, pre_call(): pl.pallas_call(pre_kernel, grid=(s // rows,), in_specs=[pl.BlockSpec((row...  9.44 us
    pallas_call x1, Pallas kernels, wgrad_rows(): pl.pallas_call(wgrad_rows_kernel, grid=(groups,), in_specs=[pl.BlockSpec(...  9.2 us

profile of v5, /device:TPU:0, one launch (start us, length us, event | category | flops | bytes accessed | tf_op | source)
XLA Modules:
  0.0 302.6 jit_solution(13518562865643705832)
XLA Ops:
  2.0 0.7 constant_dynamic-slice_fusion.refs_18_
  2.7 0.6 maximum_bitcast_fusion.refs_19_
  3.3 4.1 %concatenate.18 = bf16[2688]{0:T(1024)(128)(2,1)S(1)} concatenate(bf16[192]{0:T(256)(128)(2,1)} %param.22, bf16[192]{0:T(256)(128)(2,1)} %param.25, bf16[192]{0:T(256)(128)(2,1)} %param.29, bf16[192]{0:T(256)(128)(2,1)} %param.32, bf16[768]{0:T(1024)(128)(2,1)} %param.27, bf16[1152]{0:T(1024)(128)(2,1)} %param.31), dimensions={0} | concatenate | bytes 10752 | tf_op jit(solution)/shard_map/concatenate | solution.py:1003
  7.4 0.6 broadcast_in_dim.27.refs_2_
  8.2 3.0 sine_multiply_fusion
  11.1 1.0 copy.32.flag_ref.refs_12_
  12.2 27.3 %head.1 = (bf16[4,4,288,128]{3,2,1,0:T(8,128)(2,1)}, bf16[4,4,48,2304]{3,2,1,0:T(8,128)(2,1)}, bf16[4,1,2688]{2,1,0:T(2,128)(2,1)}) custom-call(bf16[4,288,128]{2,1,0:T(8,128)(2,1)} %bitcast.43, bf16[4,48,2304]{2,1,0:T(8,128)(2,1)} %bitcast.42, bf16[1,2688]{1,0:T(2,128)(2,1)} %broadcast_in_dim.27.refs_2_), custom_call_target="tpu_custom_call" | custom-call | tf_op jit(solution)/shard_map/head/pallas_call | solution.py:429
  39.5 0.8 copy.38
  40.3 0.6 copy.36
  41.3 2.3 convolution_reduce_fusion
  43.7 0.6 concatenate.22.vec_ref.refs_15_
  44.3 0.6 concatenate.20.vec_ref.refs_14_
  45.0 9.4 %pre.1 = (bf16[768,1024]{1,0:T(8,128)(2,1)}, bf16[1024,2304]{1,0:T(8,128)(2,1)}) custom-call(bf16[1024,768]{1,0:T(8,128)(2,1)} %bitcast.56, s32[1024,1]{1,0:T(8,128)} %copy.32.flag_ref.refs_12_, f32[8,768]{1,0:T(8,128)} %concatenate.20.vec_ref.refs_14_, bf16[768,2304]{1,0:T(8,128)(2,1)} %bitcast.53, f32[1024,128]{1,0:T(8,128)} %get-tuple-element.78.cos_ref.refs_7_, ...), custom_call_target="tpu_custom_call" | custom-call | flops 3623878656 | bytes 9437184 | tf_op jit(solution)/shard_map/pre/pallas_call | solution.py:50
  54.4 51.1 %attn_fwd.1 = (bf16[1024,768]{1,0:T(8,128)(2,1)}, f32[1024,128]{1,0:T(8,128)}, bf16[4,4,48,768]{3,2,1,0:T(8,128)(2,1)}, bf16[4,4,48,3072]{3,2,1,0:T(8,128)(2,1)}, bf16[4,4,192,768]{3,2,1,0:T(8,128)(2,1)}) custom-call(s32[1]{0:T(128)S(6)} %copy.42.refs_0_.len_ref, bf16[1024,2304]{1,0:T(8,128)(2,1)} %get-tuple-element.49.refs_1_.refs_2_.refs_3_, ...), custom_call_target="tpu_custom_call" | custom-call | flops 6442450944 | bytes 6291456 | tf_op jit(solution)/shard_map/attn_fwd/pallas_call | solution.py:730
  105.5 37.7 %mid.1 = (bf16[1024,768]{1,0:T(8,128)(2,1)}, f32[1024,768]{1,0:T(8,128)}, bf16[1024,768]{1,0:T(8,128)(2,1)}, bf16[1024,768]{1,0:T(8,128)(2,1)}, bf16[1024,3072]{...) custom-call(s32[1]{0:T(128)S(6)} %copy.42.refs_0_.len_ref, ...), custom_call_target="tpu_custom_call" | custom-call | flops 21743271936 | bytes 23592960 | tf_op jit(solution)/shard_map/mid/pallas_call | solution.py:225
  143.3 4.4 %wgrad_cols.3.refs_23_ = bf16[2,2,4,2,48,384]{5,4,3,2,1,0:T(8,128)(2,1)} custom-call(bf16[1024,768]{1,0:T(8,128)(2,1)} %get-tuple-element.50.att_ref.a_ref.refs_4_, bf16[1024,768]{1,0:T(8,128)(2,1)} %get-tuple-element.65.b_ref), custom_call_target="tpu_custom_call" | custom-call | flops 1207959552 | bytes 4325376 | tf_op jit(solution)/shard_map/wgrad_cols/pallas_call | solution.py:666
  147.6 9.2 %wgrad_rows.1.refs_21_ = bf16[8,2,4,2,48,384]{5,4,3,2,1,0:T(8,128)(2,1)} custom-call(bf16[1024,3072]{1,0:T(8,128)(2,1)} %get-tuple-element.61.a_ref, bf16[1024,768]{1,0:T(8,128)(2,1)} %get-tuple-element.62.b_ref), custom_call_target="tpu_custom_call" | custom-call | flops 4831838208 | bytes 12582912 | tf_op jit(solution)/shard_map/wgrad_rows/pallas_call | solution.py:686
  156.8 9.2 %wgrad_cols.2.refs_22_ = bf16[8,2,4,2,48,384]{5,4,3,2,1,0:T(8,128)(2,1)} custom-call(bf16[1024,768]{1,0:T(8,128)(2,1)} %get-tuple-element.63.a_ref, bf16[1024,3072]{1,0:T(8,128)(2,1)} %get-tuple-element.64.b_ref), custom_call_target="tpu_custom_call" | custom-call | flops 4831838208 | bytes 12582912 | tf_op jit(solution)/shard_map/wgrad_cols/pallas_call | solution.py:666
  166.0 120.2 %tail.1 = (bf16[1024,768]{1,0:T(8,128)(2,1)}, bf16[768,768]{1,0:T(8,128)(2,1)}, bf16[192,3072]{1,0:T(8,128)(2,1)}, bf16[192,768]{1,0:T(8,128)(2,1)}, bf16[192,23...) custom-call(s32[1]{0:T(128)S(6)} %copy.42.refs_0_.len_ref, ...), custom_call_target="tpu_custom_call" | custom-call | flops 24159191040 | bytes 31457280 | tf_op jit(solution)/shard_map/tail/pallas_call | solution.py:965
  286.2 1.1 slice_bitcast_fusion
  287.4 1.3 reduce.1
  288.7 1.3 reduce.2
  290.0 1.4 fusion.7
  291.4 1.9 convert_element_type.102
  293.3 2.5 convert_element_type.101
  295.8 1.7 convert_element_type.103
  297.5 1.6 convert_element_type.104
  299.0 0.5 copy-done
  299.6 1.1 copy.44
  300.7 0.3 copy-done.3
  301.0 0.8 copy.45
  301.8 0.8 copy.46
  (30 shorter events, 0.6 us)
Async XLA Ops:
  0.6 10.5 %copy-start.5 = (s32[1,1024]{1,0:T(1,128)S(1)}, s32[1,1024]{1,0:T(1,128)}, u32[]{:S(2)}) copy-start(s32[1,1024]{1,0:T(1,128)} %param.18) | copy-start | bytes 12292
  2.7 38.7 %copy-start.6 = (f32[1,128]{1,0:T(1,128)}, f32[1,128]{1,0:T(1,128)S(1)}, u32[]{:S(2)}) copy-start(f32[1,128]{1,0:T(1,128)S(1)} %constant_dynamic-slice_fusion.refs_18_) | copy-start | bytes 1540
  291.4 4.4 %copy-start.2 = (bf16[192,3072]{1,0:T(8,128)(2,1)S(1)}, bf16[192,3072]{1,0:T(8,128)(2,1)}, u32[]{:S(2)}) copy-start(bf16[192,3072]{1,0:T(8,128)(2,1)} %get-tuple-element.70) | copy-start | bytes 3538948
  295.8 1.7 copy-start.1
  297.5 2.1 copy-start
  299.6 1.4 copy-start.3
  299.6 2.3 copy-start.4

commit v6 on v5

--- a/solution.py
+++ b/solution.py
@@ -453,7 +453,8 @@
         self.stages = ([self.begin, self.core_add] + [functools.partial(self.group_add, t) for t in range(p.bits)]
                        + [functools.partial(self.climb, j) for j in range(1, self.last + 1)] + [self.middle]
                        + [functools.partial(self.descend, j) for j in range(self.last - 1, -1, -1)])
-        self.lags = [lag * i for i in range(len(self.stages))]
+        self.lags = [0, 1] + [1 + lag * (i + 1) for i in range(len(self.stages) - 2)]
+        self.early = self.total - counts[-1]
         self.gap = gap
         self.ticks = self.total + gap + self.lags[-1]
 
@@ -623,11 +624,17 @@
             self.done(k)
 
     def tick(self, t):
-        for s in range(len(self.stages) - 1, -1, -1):
+        for s in range(len(self.stages) - 1, 0, -1):
             k = t - self.lags[s]
             @pl.when((k >= 0) & (k < self.total + self.gap) & ((k < self.total - self.gap) | (k >= self.total)))
             def _(s=s, k=k):
                 self.stages[s](k - self.gap * (k // self.total))
+        @pl.when(t + 1 < self.early)
+        def _():
+            self.begin(t + 1)
+        @pl.when((t >= self.early) & (t < self.total + self.gap) & ((t < self.total - self.gap) | (t >= self.total)))
+        def _():
+            self.begin(t - self.gap * (t // self.total))
 
     def drain(self):
         p = self.p
@@ -888,12 +895,13 @@
     rscratch, sscratch = refs[33 + 2 * n:54 + 2 * n], refs[54 + 2 * n:]
     step, steps = pl.program_id(0), 2 * pairs + post
     p = Place(shape)
-    r = Reduce(p, counts, ["rows"] + ["cols"] * (n - 2) + ["qkv"], list(srcs) + [gq], reduced, rscratch, 2, 2)
+    r = Reduce(p, counts, ["rows"] + ["cols"] * (n - 2) + ["qkv"], list(srcs) + [gq], reduced, rscratch, 3, 2)
     small = Small(p, sscratch)
 
     @pl.when(step == 0)
     def _():
         r.greet(small.peers())
+        r.begin(0)
 
     @pl.loop(2 * step, 2 * step + 2)
     def _(t):
@@ -930,25 +938,34 @@
     def _():
         small.first(sums_ref[...], sb1_ref[...], sums1[...], vpre_ref[...], vmid_ref[...], condp_ref[...], meta_ref[...],
                     ada_ref[...])
-        small.second()
-        @pl.loop(2 * steps, max(r.ticks, 2 * steps))
-        def _(t):
-            r.tick(t)
-        small.third(*small_out, sums1.shape[1])
+        last = max(r.ticks, 2 * steps)
+        marks = [2 * steps, min(2 * steps + SPLIT[0], last), min(2 * steps + SPLIT[1], last), last]
+        for n in range(3):
+            @pl.loop(marks[n], marks[n + 1])
+            def _(t):
+                r.tick(t)
+            if n == 0:
+                small.second()
+            if n == 1:
+                small.third(*small_out, sums1.shape[1])
         r.drain()
         small.settle()
 
 
+SPLIT = (3, 8)
+
+
 def tail_call(shape, length, qkv, att, gatt, lse, cos, sin, n1t, w, tok, flag, gh1, vpre, vmid, sums, sb1, condp, meta,
-              ada, grads, table_rows, rows=256, post=128):
+              ada, grads, table_rows, rows=256):
     groups = shape["fsdp"]
     s, d3 = qkv.shape
     d = d3 // 3
     pairs = d // 128
+    r, c = 2 * grads[0].shape[-2], grads[0].shape[-1]
+    post = 256 if r % 32 == 0 else 128
     blocks = s // post
     steps = 2 * pairs + blocks
     ff, n_mod = sb1.shape[1], ada.shape[0]
-    r, c = 2 * grads[0].shape[-2], grads[0].shape[-1]
     counts = [g.shape[0] for g in grads] + [pairs]
     pair = lambda i: jnp.minimum(i // 2, pairs - 1)
     blk = lambda i: jnp.maximum(i - 2 * pairs, 0)
@@ -1000,12 +1017,12 @@
     tok, cot = tokens[0], cotangent[0]
     flag = hidden_token_indicator.reshape(s, 1)
     sizes = [v.shape[0] for v in (gain_one, gain_two, b_fc2, mask_embed, b_fc1, b_ada)]
-    small = jnp.concatenate([gain_one, gain_two, b_fc2, mask_embed, b_fc1, b_ada])[None]
+    small = jnp.concatenate([v[None].astype(f32) for v in (gain_one, gain_two, b_fc2, mask_embed, b_fc1, b_ada)], axis=1)
     (ada_all, qkv_all), packed = head_call(shape, small, [w_ada, w_qkv])
     packed = packed[:, 0]
     cuts = [sum(sizes[:i]) for i in range(len(sizes) + 1)]
     gain1, gain2, b2, emb, b1, bada = (
-        packed[:, cuts[i]:cuts[i + 1]].reshape(1, -1).astype(f32) for i in range(len(sizes)))
+        packed[:, cuts[i]:cuts[i + 1]].reshape(1, -1) for i in range(len(sizes)))
     cond_pre = lax.dynamic_slice_in_dim(time_table, time_ids[0], 1, axis=0)
     cond = jax.nn.silu(cond_pre)
     modulation = jnp.dot(cond, ada_all.astype(f32).T, precision=highest) + bada

time: 303 us -> 290 us (0.957)
  Pallas kernels: 269 us -> 255 us
    pallas_call x1, Pallas kernels: 120 us -> 107 us  [tail_call(): pl.pallas_call(functools.partial(tail_kernel, shape, counts, rows, blocks...]
    concatenate x1, local copies, waits for them, and re-layouts: 4.12 us -> 0.1 us  [per_device(): jnp.concatenate([v[None].astype(f32) for v in (gain_one, gain_two, b_fc2,...]
    convert_element_type x5 -> x6, local copies, waits for them, and re-layouts: 0.35 us -> 4.01 us  [per_device(): v[None].astype(f32)]
where the time goes in v6:
time: 290 us; the launch traced here: 289 us
  Pallas kernels  255 us (88%)
  local copies, waits for them, and re-layouts  15.1 us (5%)
  other arithmetic  14.6 us (5%)
    pallas_call x1, Pallas kernels, tail_call(): pl.pallas_call(functools.partial(tail_kernel, shape, counts, rows, blocks...  107 us
    pallas_call x1, Pallas kernels, attn_fwd_call(): pl.pallas_call(functools.partial(attn_fwd_kernel, shape, len(ws), rows),...  51.1 us
    pallas_call x1, Pallas kernels, mid_call(): pl.pallas_call(functools.partial(mid_kernel, cut=cut), grid=(s // rows,),...  37.7 us
    pallas_call x1, Pallas kernels, head_call(): pl.pallas_call(functools.partial(head_kernel, shape, len(ws)), in_specs=[...  27.3 us
    pallas_call x2, Pallas kernels, wgrad_cols(): pl.pallas_call(wgrad_cols_kernel, grid=(n // m,), in_specs=[pl.BlockSpec(...  13.5 us
    pallas_call x1, Pallas kernels, pre_call(): pl.pallas_call(pre_kernel, grid=(s // rows,), in_specs=[pl.BlockSpec((row...  9.44 us
    pallas_call x1, Pallas kernels, wgrad_rows(): pl.pallas_call(wgrad_rows_kernel, grid=(groups,), in_specs=[pl.BlockSpec(...  9.2 us

profile of v6, /device:TPU:0, one launch (start us, length us, event | category | flops | bytes accessed | tf_op | source)
XLA Modules:
  0.0 289.3 jit_solution(15195368452636904622)
XLA Ops:
  2.0 0.7 constant_dynamic-slice_fusion.refs_18_
  3.3 0.7 convert_element_type.43
  3.9 0.7 convert_element_type.44
  4.6 0.7 convert_element_type.45
  5.3 0.7 convert_element_type.46
  5.9 0.7 convert_element_type.47
  6.6 0.7 convert_element_type.48
  8.2 3.0 %sine_multiply_fusion = (f32[1024,128]{1,0:T(8,128)}, f32[1024,128]{1,0:T(8,128)}) fusion(f32[1024,32]{1,0:T(8,128)S(1)} %iota_multiply_fusion, f32[128]{0:T(128)S(1)} %compare_select_fusion), kind=kLoop, calls=%fused_computation.2 | loop fusion | flops 524288 | bytes 1180160 | tf_op jit(solution)/shard_map/mul | solution.py:1009
  11.1 1.0 copy.32.flag_ref.refs_12_
  12.2 27.3 %head.1 = (bf16[4,4,288,128]{3,2,1,0:T(8,128)(2,1)}, bf16[4,4,48,2304]{3,2,1,0:T(8,128)(2,1)}, f32[4,1,2688]{2,1,0:T(1,128)}) custom-call(bf16[4,288,128]{2,1,0:T(8,128)(2,1)} %bitcast.43, bf16[4,48,2304]{2,1,0:T(8,128)(2,1)} %bitcast.42, f32[1,2688]{1,0:T(1,128)} %concatenate.21.refs_2_), custom_call_target="tpu_custom_call" | custom-call | tf_op jit(solution)/shard_map/head/pallas_call | solution.py:429
  39.5 0.8 copy.38
  41.3 2.3 convolution_reduce_fusion
  43.7 0.6 concatenate.25.vec_ref.refs_15_
  44.3 0.6 concatenate.23.vec_ref.refs_14_
  45.0 9.4 %pre.1 = (bf16[768,1024]{1,0:T(8,128)(2,1)}, bf16[1024,2304]{1,0:T(8,128)(2,1)}) custom-call(bf16[1024,768]{1,0:T(8,128)(2,1)} %bitcast.56, s32[1024,1]{1,0:T(8,128)} %copy.32.flag_ref.refs_12_, f32[8,768]{1,0:T(8,128)} %concatenate.23.vec_ref.refs_14_, bf16[768,2304]{1,0:T(8,128)(2,1)} %bitcast.53, f32[1024,128]{1,0:T(8,128)} %get-tuple-element.78.cos_ref.refs_7_, ...), custom_call_target="tpu_custom_call" | custom-call | flops 3623878656 | bytes 9437184 | tf_op jit(solution)/shard_map/pre/pallas_call | solution.py:50
  54.4 51.1 %attn_fwd.1 = (bf16[1024,768]{1,0:T(8,128)(2,1)}, f32[1024,128]{1,0:T(8,128)}, bf16[4,4,48,768]{3,2,1,0:T(8,128)(2,1)}, bf16[4,4,48,3072]{3,2,1,0:T(8,128)(2,1)}, bf16[4,4,192,768]{3,2,1,0:T(8,128)(2,1)}) custom-call(s32[1]{0:T(128)S(6)} %copy.42.refs_0_.len_ref, bf16[1024,2304]{1,0:T(8,128)(2,1)} %get-tuple-element.49.refs_1_.refs_2_.refs_3_, ...), custom_call_target="tpu_custom_call" | custom-call | flops 6442450944 | bytes 6291456 | tf_op jit(solution)/shard_map/attn_fwd/pallas_call | solution.py:737
  105.5 37.7 %mid.1 = (bf16[1024,768]{1,0:T(8,128)(2,1)}, f32[1024,768]{1,0:T(8,128)}, bf16[1024,768]{1,0:T(8,128)(2,1)}, bf16[1024,768]{1,0:T(8,128)(2,1)}, bf16[1024,3072]{...) custom-call(s32[1]{0:T(128)S(6)} %copy.42.refs_0_.len_ref, ...), custom_call_target="tpu_custom_call" | custom-call | flops 21743271936 | bytes 23592960 | tf_op jit(solution)/shard_map/mid/pallas_call | solution.py:225
  143.3 4.4 %wgrad_cols.3.refs_23_ = bf16[2,2,4,2,48,384]{5,4,3,2,1,0:T(8,128)(2,1)} custom-call(bf16[1024,768]{1,0:T(8,128)(2,1)} %get-tuple-element.50.att_ref.a_ref.refs_4_, bf16[1024,768]{1,0:T(8,128)(2,1)} %get-tuple-element.65.b_ref), custom_call_target="tpu_custom_call" | custom-call | flops 1207959552 | bytes 4325376 | tf_op jit(solution)/shard_map/wgrad_cols/pallas_call | solution.py:673
  147.6 9.2 %wgrad_rows.1.refs_21_ = bf16[8,2,4,2,48,384]{5,4,3,2,1,0:T(8,128)(2,1)} custom-call(bf16[1024,3072]{1,0:T(8,128)(2,1)} %get-tuple-element.61.a_ref, bf16[1024,768]{1,0:T(8,128)(2,1)} %get-tuple-element.62.b_ref), custom_call_target="tpu_custom_call" | custom-call | flops 4831838208 | bytes 12582912 | tf_op jit(solution)/shard_map/wgrad_rows/pallas_call | solution.py:693
  156.8 9.2 %wgrad_cols.2.refs_22_ = bf16[8,2,4,2,48,384]{5,4,3,2,1,0:T(8,128)(2,1)} custom-call(bf16[1024,768]{1,0:T(8,128)(2,1)} %get-tuple-element.63.a_ref, bf16[1024,3072]{1,0:T(8,128)(2,1)} %get-tuple-element.64.b_ref), custom_call_target="tpu_custom_call" | custom-call | flops 4831838208 | bytes 12582912 | tf_op jit(solution)/shard_map/wgrad_cols/pallas_call | solution.py:673
  166.0 106.9 %tail.1 = (bf16[1024,768]{1,0:T(8,128)(2,1)}, bf16[768,768]{1,0:T(8,128)(2,1)}, bf16[192,3072]{1,0:T(8,128)(2,1)}, bf16[192,768]{1,0:T(8,128)(2,1)}, bf16[192,23...) custom-call(s32[1]{0:T(128)S(6)} %copy.42.refs_0_.len_ref, ...), custom_call_target="tpu_custom_call" | custom-call | flops 24159191040 | bytes 31457280 | tf_op jit(solution)/shard_map/tail/pallas_call | solution.py:982
  273.0 1.1 slice_bitcast_fusion.1
  274.1 1.3 reduce.1
  275.4 1.3 reduce.2
  276.7 1.4 fusion.8
  278.1 1.9 convert_element_type.52
  280.0 2.5 convert_element_type.51
  282.5 1.7 convert_element_type.53
  284.2 1.6 convert_element_type.54
  286.3 1.1 copy.44
  287.7 0.8 copy.45
  288.5 0.8 copy.46
  (36 shorter events, 3.4 us)
Async XLA Ops:
  0.6 10.5 %copy-start.5 = (s32[1,1024]{1,0:T(1,128)S(1)}, s32[1,1024]{1,0:T(1,128)}, u32[]{:S(2)}) copy-start(s32[1,1024]{1,0:T(1,128)} %param.18) | copy-start | bytes 12292
  2.7 38.7 %copy-start.6 = (f32[1,128]{1,0:T(1,128)}, f32[1,128]{1,0:T(1,128)S(1)}, u32[]{:S(2)}) copy-start(f32[1,128]{1,0:T(1,128)S(1)} %constant_dynamic-slice_fusion.refs_18_) | copy-start | bytes 1540
  278.1 4.4 %copy-start.2 = (bf16[192,3072]{1,0:T(8,128)(2,1)S(1)}, bf16[192,3072]{1,0:T(8,128)(2,1)}, u32[]{:S(2)}) copy-start(bf16[192,3072]{1,0:T(8,128)(2,1)} %get-tuple-element.70) | copy-start | bytes 3538948
  282.5 1.7 copy-start.1
  284.2 2.1 copy-start
  286.3 1.4 copy-start.3
  286.3 2.3 copy-start.4

commit v7 on v6

--- a/solution.py
+++ b/solution.py
@@ -26,39 +26,7 @@
     lane = lax.broadcasted_iota(jnp.int32, u.shape, 1)
     return jnp.where(lane % HD < HD // 2, pltpu.roll(u, 96, 1), pltpu.roll(u, 32, 1))
 
-def pre_kernel(tok_ref, flag_ref, vec_ref, w_ref, cos_ref, sin_ref, n1_ref, qkv_ref):
-    emb, gain, scale, shift = (vec_ref[i:i + 1, :] for i in range(4))
-    h0 = jnp.where(flag_ref[...] == 1, emb, tok_ref[...].astype(f32))
-    n, _ = norm_parts(h0)
-    n1 = (n * gain * (1.0 + scale) + shift).astype(bf16)
-    n1_ref[...] = n1.astype(f32).T.astype(bf16)
-    d = n1.shape[1]
-    cos, sin = cos_ref[...], sin_ref[...]
-    for part in range(3):
-        y = dot(n1, w_ref[:, part * d:(part + 1) * d])
-        for c in range(d // 128):
-            lo = part * d + c * 128
-            u = y[:, c * 128:(c + 1) * 128]
-            if part < 2:
-                u = u * cos + swap_halves(u) * sin
-                if part == 0:
-                    u = u * QSCALE
-            qkv_ref[:, lo:lo + 128] = u.astype(bf16)
-
-def pre_call(tok, flag, vecs, w, cos, sin, rows=256):
-    s, d = tok.shape
-    return pl.pallas_call(
-        pre_kernel, grid=(s // rows,),
-        in_specs=[pl.BlockSpec((rows, d), lambda i: (i, 0)), pl.BlockSpec((rows, 1), lambda i: (i, 0)),
-                  pl.BlockSpec((8, d), lambda i: (0, 0)), pl.BlockSpec((d, 3 * d), lambda i: (0, 0)),
-                  pl.BlockSpec((rows, 128), lambda i: (i, 0)), pl.BlockSpec((rows, 128), lambda i: (i, 0))],
-        out_specs=[pl.BlockSpec((d, rows), lambda i: (0, i)), pl.BlockSpec((rows, 3 * d), lambda i: (i, 0))],
-        out_shape=[jax.ShapeDtypeStruct((d, s), bf16), jax.ShapeDtypeStruct((s, 3 * d), bf16)],
-        cost_estimate=pl.CostEstimate(flops=2 * s * d * 3 * d, bytes_accessed=12 * s * d, transcendentals=0),
-        name="pre")(tok, flag, vecs, w, cos, sin)
-
-def attn_fwd_body(len_ref, q_ref, k_ref, v_ref, o_ref, lse_ref, rows):
-    p = pl.program_id(0)
+def attn_fwd_body(len_ref, q_ref, k_ref, v_ref, o_ref, lse_ref, rows, p):
     s = q_ref.shape[0]
     length = len_ref[0]
     lane = lax.broadcasted_iota(jnp.int32, (s, 128), 1)
@@ -405,35 +373,6 @@
 ANY = pl.BlockSpec(memory_space=pl.ANY)
 
 
-def head_kernel(shape, count, *refs):
-    ins, small, outs, small_out = refs[:count], refs[count], refs[count + 1:2 * count + 1], refs[2 * count + 1]
-    sems = refs[2 * count + 2:]
-    p = Place(shape)
-    g = Gather(p, ins, outs, sems[:6])
-    s = Direct(p, small, small_out, sems[6:])
-    greet(gather_peers(p, True))
-    s.start()
-    for w in range(count):
-        g.start(w)
-    for t in range(p.bits):
-        for w in range(count):
-            g.after(w, t)
-    for w in range(count):
-        g.finish(w)
-    s.finish()
-
-
-def head_call(shape, small, ws):
-    groups = shape["fsdp"]
-    outs = [gather_shape(w, groups) for w in ws] + [jax.ShapeDtypeStruct((groups,) + small.shape, small.dtype)]
-    res = pl.pallas_call(
-        functools.partial(head_kernel, shape, len(ws)), in_specs=[ANY] * (len(ws) + 1), out_specs=[ANY] * len(outs),
-        out_shape=outs, scratch_shapes=Gather.scratch(len(ws), groups) + Direct.scratch(groups),
-        compiler_params=pltpu.CompilerParams(collective_id=1, has_side_effects=True), name="head",
-    )(*[quarter(w) for w in ws], small)
-    return [r.reshape(-1, r.shape[-1]) for r in res[:-1]], res[-1]
-
-
 class Reduce:
     def __init__(self, place, counts, kinds, srcs, outs, scratch, lag, gap):
         self.p, self.counts, self.kinds, self.srcs, self.outs = place, counts, kinds, srcs, outs
@@ -699,55 +638,170 @@
                                       transcendentals=0), name="wgrad_rows")(a, b)
 
 
-def attn_fwd_kernel(shape, count, rows, *refs):
-    len_ref, q_ref, k_ref, v_ref = refs[:4]
-    ins = refs[4:4 + count]
-    o_ref, lse_ref = refs[4 + count:6 + count]
-    outs = refs[6 + count:6 + 2 * count]
+def pad128(n):
+    return -(-n // 128) * 128
+
+
+def small_row(vectors):
+    wide = [jnp.pad(v.astype(f32), (0, pad128(v.shape[0]) - v.shape[0])) for v in vectors]
+    return jnp.concatenate([v[None] for v in wide], axis=1)
+
+
+def unpack(ref, sizes, groups):
+    out, base = [], 0
+    for size in sizes:
+        wide, full = pad128(size), size * groups
+        total = None
+        for f in range(groups):
+            x = ref[f, :, base:base + wide]
+            if full > wide:
+                x = jnp.concatenate([x, jnp.zeros((1, full - wide), f32)], axis=1)
+            if f > 0:
+                x = pltpu.roll(jnp.broadcast_to(x, (8, full)), f * size, 1)[0:1]
+            total = x if total is None else total + x
+        out.append(total)
+        base += wide
+    return out
+
+
+def flat(ref, lo, hi):
+    groups, _, rows, _ = ref.shape
+    if rows % 16 == 0:
+        return ref[:, :, :, lo:hi].reshape(groups * 4 * rows, hi - lo)
+    parts = [jnp.concatenate([ref[f, i, :, lo:hi].astype(f32) for i in range(4)], axis=0).astype(bf16) for f in range(groups)]
+    return jnp.concatenate(parts, axis=0)
+
+
+def front_kernel(shape, sizes, rows, *refs):
+    len_ref, tok_ref, flag_ref, cos_ref, sin_ref, condp_ref, small_ref = refs[:7]
+    ins = refs[7:12]
+    att_ref, lse_ref, vpre_ref, vmid_ref, b1_ref, n1t_hbm, qkv_hbm = refs[12:19]
+    outs = refs[19:24]
+    n1, n1t, qkv, wq, ada, smalls, loads, stores = refs[24:32]
+    gsems, dsems = refs[32:38], refs[38:40]
     step, steps = pl.program_id(0), pl.num_programs(0)
+    s, d = tok_ref.shape
     p = Place(shape)
-    g = Gather(p, ins, outs, refs[6 + 2 * count:])
+    g = Gather(p, ins, outs, gsems)
+    direct = Direct(p, small_ref, smalls, dsems)
+    save = [pltpu.make_async_copy(n1t, n1t_hbm, stores.at[0]), pltpu.make_async_copy(qkv, qkv_hbm, stores.at[1])]
+
     @pl.when(step == 0)
     def _():
-        greet(gather_peers(p, False))
-        for w in range(count):
+        greet(gather_peers(p, True))
+        direct.start()
+        g.start(0)
+        g.start(1)
+        g.after(0, 0)
+        g.after(1, 0)
+        for w in (2, 3, 4):
             g.start(w)
-    for w, at in ((0, 2), (1, 4)):
-        @pl.when(step == at)
-        def _(w=w):
-            g.after(w, 0)
-    attn_fwd_body(len_ref, q_ref, k_ref, v_ref, o_ref, lse_ref, rows)
+        for t in range(1, p.bits):
+            g.after(0, t)
+        g.finish(0)
+        direct.finish()
+        fetch = pltpu.make_async_copy(outs[0], ada, loads.at[0])
+        fetch.start()
+        gain1, gain2, b2, emb, b1, bada = unpack(smalls, sizes, p.groups)
+        fetch.wait()
+        condp = condp_ref[...]
+        cond = condp / (1.0 + jnp.exp(-condp))
+        stack = jnp.concatenate(list(split3(cond)) + [jnp.zeros((5, cond.shape[1]), f32)], axis=0).astype(bf16)
+        mod = colsum(dot(stack, flat(ada, 0, 128), NT)) + bada
+        shift_a, scale_a, gate_a, shift_m, scale_m, gate_m = (mod[:, i * d:(i + 1) * d] for i in range(6))
+        vpre_ref[...] = jnp.concatenate([emb, gain1, scale_a, shift_a, jnp.zeros((4, d), f32)], axis=0)
+        vmid_ref[...] = jnp.concatenate([emb, gain2, scale_m, shift_m, gate_a, gate_m, b2, jnp.zeros((1, d), f32)], axis=0)
+        b1_ref[...] = b1
+        amp = gain1 * (1.0 + scale_a)
+
+        @pl.loop(0, s // rows)
+        def _(i):
+            cut = pl.ds(pl.multiple_of(i * rows, rows), rows)
+            h0 = jnp.where(flag_ref[cut, :] == 1, emb, tok_ref[cut, :].astype(f32))
+            x = norm_parts(h0)[0] * amp + shift_a
+            n1[cut, :] = x.astype(bf16)
+            n1t[:, cut] = x.T.astype(bf16)
+
+        for t in range(1, p.bits):
+            g.after(1, t)
+        g.finish(1)
+        fetch = pltpu.make_async_copy(outs[1], wq, loads.at[1])
+        fetch.start()
+        fetch.wait()
+
+        @pl.loop(0, s // rows)
+        def _(i):
+            cut = pl.ds(pl.multiple_of(i * rows, rows), rows)
+            x = n1[cut, :]
+            cos, sin = cos_ref[cut, :], sin_ref[cut, :]
+            for part in range(3):
+                y = dot(x, flat(wq, part * d, (part + 1) * d))
+                for c in range(d // 128):
+                    lo = part * d + c * 128
+                    u = y[:, c * 128:(c + 1) * 128]
+                    if part < 2:
+                        u = u * cos + swap_halves(u) * sin
+                        if part == 0:
+                            u = u * QSCALE
+                    qkv[cut, lo:lo + 128] = u.astype(bf16)
+
+        for c in save:
+            c.start()
+
+    @pl.when(step == 1)
+    def _():
+        g.after(2, 0)
+        g.after(3, 0)
+
+    @pl.when(step == 4)
+    def _():
+        g.after(4, 0)
+
+    @pl.when(step > 0)
+    def _():
+        pair = step - 1
+        col = lambda base: qkv.at[:, pl.ds(pl.multiple_of(base + pair * 128, 128), 128)]
+        attn_fwd_body(len_ref, col(0), col(d), col(2 * d), att_ref, lse_ref, rows, pair)
+
     @pl.when(step == steps - 1)
     def _():
-        for w in range(2, count):
-            g.after(w, 0)
         for t in range(1, p.bits):
-            for w in range(count):
+            for w in (2, 3, 4):
                 g.after(w, t)
-        for w in range(count):
+        for w in (2, 3, 4):
             g.finish(w)
-
-
-def attn_fwd_call(shape, length, qkv, ws, rows=256):
+        for c in save:
+            c.wait()
+
+
+def front_call(shape, length, tok, flag, cos, sin, condp, small, ws, sizes, rows=256):
     groups = shape["fsdp"]
-    s, d3 = qkv.shape
-    d = d3 // 3
-    np_ = d // 128
+    s, d = tok.shape
+    pairs = d // 128
     sd = jax.ShapeDtypeStruct
+    once = pl.Buffered(1)
+    whole = lambda dims: pl.BlockSpec(dims, lambda i: (0, 0), pipeline_mode=once)
+    sem = pltpu.SemaphoreType.DMA
+    gathered = [gather_shape(w, groups) for w in ws]
+    ff = sizes[4] * groups
     res = pl.pallas_call(
-        functools.partial(attn_fwd_kernel, shape, len(ws), rows), grid=(np_,),
-        in_specs=[pl.BlockSpec(memory_space=pltpu.SMEM), pl.BlockSpec((s, 128), lambda i: (0, i)),
-                  pl.BlockSpec((s, 128), lambda i: (0, np_ + i)),
-                  pl.BlockSpec((s, 128), lambda i: (0, 2 * np_ + i))] + [ANY] * len(ws),
-        out_specs=[pl.BlockSpec((s, 128), lambda i: (0, i)), pl.BlockSpec((s, 128), lambda i: (0, 0))]
-        + [ANY] * len(ws),
-        out_shape=[sd((s, d), bf16), sd((s, 128), f32)] + [gather_shape(w, groups) for w in ws],
-        scratch_shapes=Gather.scratch(len(ws), groups),
-        compiler_params=pltpu.CompilerParams(collective_id=2, has_side_effects=True),
-        cost_estimate=pl.CostEstimate(flops=8 * s * s * d, bytes_accessed=8 * s * d, transcendentals=s * s * 12),
-        name="attn_fwd")(length, qkv, qkv, qkv, *[quarter(w) for w in ws])
-    return res[0], res[1], [r.reshape(-1, r.shape[-1]) for r in res[2:]]
-
+        functools.partial(front_kernel, shape, sizes, rows), grid=(pairs + 1,),
+        in_specs=[pl.BlockSpec(memory_space=pltpu.SMEM), whole((s, d)), whole((s, 1)), whole((s, 128)), whole((s, 128)),
+                  whole((1, 128))] + [ANY] * (1 + len(ws)),
+        out_specs=[pl.BlockSpec((s, 128), lambda i: (0, jnp.maximum(i - 1, 0))), whole((s, 128)), whole((8, d)),
+                   whole((8, d)), whole((1, ff))] + [ANY] * (2 + len(ws)),
+        out_shape=[sd((s, d), bf16), sd((s, 128), f32), sd((8, d), f32), sd((8, d), f32), sd((1, ff), f32),
+                   sd((d, s), bf16), sd((s, 3 * d), bf16)] + gathered,
+        scratch_shapes=[pltpu.VMEM((s, d), bf16), pltpu.VMEM((d, s), bf16), pltpu.VMEM((s, 3 * d), bf16),
+                        pltpu.VMEM(gathered[1].shape, bf16), pltpu.VMEM(gathered[0].shape, bf16),
+                        pltpu.VMEM((groups,) + small.shape, f32), sem((2,)), sem((2,))]
+        + Gather.scratch(len(ws), groups) + Direct.scratch(groups),
+        compiler_params=pltpu.CompilerParams(collective_id=1, has_side_effects=True, vmem_limit_bytes=60000 * 1024),
+        cost_estimate=pl.CostEstimate(flops=8 * s * s * d + 6 * s * d * d, bytes_accessed=20 * s * d,
+                                      transcendentals=s * s * 12),
+        name="front")(length, tok, flag, cos, sin, condp, small, *[quarter(w) for w in ws])
+    att, lse, vpre, vmid, b1, n1t, qkv = res[:7]
+    return att, lse, vpre, vmid, b1, n1t, qkv, [r.reshape(-1, r.shape[-1]) for r in res[7:]]
 
 def f32_rows_dot(row, weights):
     parts = split3(row)
@@ -1017,22 +1071,11 @@
     tok, cot = tokens[0], cotangent[0]
     flag = hidden_token_indicator.reshape(s, 1)
     sizes = [v.shape[0] for v in (gain_one, gain_two, b_fc2, mask_embed, b_fc1, b_ada)]
-    small = jnp.concatenate([v[None].astype(f32) for v in (gain_one, gain_two, b_fc2, mask_embed, b_fc1, b_ada)], axis=1)
-    (ada_all, qkv_all), packed = head_call(shape, small, [w_ada, w_qkv])
-    packed = packed[:, 0]
-    cuts = [sum(sizes[:i]) for i in range(len(sizes) + 1)]
-    gain1, gain2, b2, emb, b1, bada = (
-        packed[:, cuts[i]:cuts[i + 1]].reshape(1, -1) for i in range(len(sizes)))
     cond_pre = lax.dynamic_slice_in_dim(time_table, time_ids[0], 1, axis=0)
-    cond = jax.nn.silu(cond_pre)
-    modulation = jnp.dot(cond, ada_all.astype(f32).T, precision=highest) + bada
-    shift_a, scale_a, gate_a, shift_m, scale_m, gate_m = (modulation[:, i * d:(i + 1) * d] for i in range(6))
     cos, sin = rotary_tables(s)
-    zero = jnp.zeros((1, d), f32)
-    vec_pre = jnp.concatenate([emb, gain1, scale_a, shift_a] + [zero] * 4, axis=0)
-    vec_mid = jnp.concatenate([emb, gain2, scale_m, shift_m, gate_a, gate_m, b2, zero], axis=0)
-    n1, qkv = pre_call(tok, flag, vec_pre, qkv_all, cos, sin)
-    att, lse, (out_all, fc1_all, fc2_all) = attn_fwd_call(shape, lengths, qkv, [w_out, w_fc1, w_fc2])
+    att, lse, vec_pre, vec_mid, b1, n1, qkv, (ada_all, qkv_all, out_all, fc1_all, fc2_all) = front_call(
+        shape, lengths, tok, flag, cos, sin, cond_pre, small_row((gain_one, gain_two, b_fc2, mask_embed, b_fc1, b_ada)),
+        [w_ada, w_qkv, w_out, w_fc1, w_fc2], sizes)
     out, gh1, gatt, n2, act, gm, gpre, gap, sums, gb1 = mid_call(
         lengths, att, tok, flag, cot, vec_mid, b1, out_all, fc1_all, fc2_all)
     g_fc2 = wgrad_rows(act, gm, groups)

time: 290 us -> 271 us (0.934)
  Pallas kernels: 255 us -> 241 us
    pallas_call x3 -> x1, Pallas kernels: 87.8 us -> 73.8 us  [front_call(): pl.pallas_call(functools.partial(front_kernel, shape, sizes, rows), grid=...]
    convert_element_type x6 -> x0, local copies, waits for them, and re-layouts: 4.01 us -> none  [per_device(): v[None].astype(f32)]
where the time goes in v7:
time: 271 us; the launch traced here: 270 us
  Pallas kernels  241 us (89%)
  other arithmetic  14.6 us (5%)
  local copies, waits for them, and re-layouts  12.5 us (5%)
    pallas_call x1, Pallas kernels, tail_call(): pl.pallas_call(functools.partial(tail_kernel, shape, counts, rows, blocks...  107 us
    pallas_call x1, Pallas kernels, front_call(): pl.pallas_call(functools.partial(front_kernel, shape, sizes, rows), grid=...  73.8 us
    pallas_call x1, Pallas kernels, mid_call(): pl.pallas_call(functools.partial(mid_kernel, cut=cut), grid=(s // rows,),...  37.7 us
    pallas_call x2, Pallas kernels, wgrad_cols(): pl.pallas_call(wgrad_cols_kernel, grid=(n // m,), in_specs=[pl.BlockSpec(...  13.5 us
    pallas_call x1, Pallas kernels, wgrad_rows(): pl.pallas_call(wgrad_rows_kernel, grid=(groups,), in_specs=[pl.BlockSpec(...  9.19 us

profile of v7, /device:TPU:0, one launch (start us, length us, event | category | flops | bytes accessed | tf_op | source)
XLA Modules:
  0.0 270.2 jit_solution(10584724881482265059)
XLA Ops:
  0.6 0.0 copy-start.5
  2.0 1.2 constant_dynamic-slice_fusion.refs_5_.refs_18_
  3.2 0.7 pad.17
  3.8 0.7 pad.18
  4.5 0.7 pad.19
  5.2 0.7 pad.20
  5.8 0.6 maximum_bitcast_fusion.refs_19_
  6.5 0.7 constant_dynamic-update-slice_fusion.1
  7.2 0.7 constant_dynamic-update-slice_fusion
  7.9 0.6 concatenate.13.refs_6_
  8.5 0.1 iota_multiply_fusion
  8.6 3.0 %sine_multiply_fusion = (f32[1024,128]{1,0:T(8,128)}, f32[1024,128]{1,0:T(8,128)}) fusion(f32[1024,32]{1,0:T(8,128)S(1)} %iota_multiply_fusion, f32[128]{0:T(128)S(1)} %compare_select_fusion), kind=kLoop, calls=%fused_computation.1 | loop fusion | flops 524288 | bytes 1180160 | tf_op jit(solution)/shard_map/mul | solution.py:1063
  11.6 1.0 copy.32.refs_2_.flag_ref.refs_12_
  12.6 73.8 %front.1 = (bf16[1024,768]{1,0:T(8,128)(2,1)}, f32[1024,128]{1,0:T(8,128)}, f32[8,768]{1,0:T(8,128)}, f32[8,768]{1,0:T(8,128)}, f32[1,3072]{1,0:T(1,128)}, /*ind...) custom-call(s32[1]{0:T(128)S(6)} %copy.43.refs_0_.len_ref, ...), custom_call_target="tpu_custom_call" | custom-call | flops 10066329600 | bytes 15728640 | tf_op jit(solution)/shard_map/front/pallas_call | solution.py:787
  86.5 37.7 %mid.1 = (bf16[1024,768]{1,0:T(8,128)(2,1)}, f32[1024,768]{1,0:T(8,128)}, bf16[1024,768]{1,0:T(8,128)(2,1)}, bf16[1024,768]{1,0:T(8,128)(2,1)}, bf16[1024,3072]{...) custom-call(s32[1]{0:T(128)S(6)} %copy.43.refs_0_.len_ref, ...), custom_call_target="tpu_custom_call" | custom-call | flops 21743271936 | bytes 23592960 | tf_op jit(solution)/shard_map/mid/pallas_call | solution.py:193
  124.2 4.4 %wgrad_cols.3.refs_23_ = bf16[2,2,4,2,48,384]{5,4,3,2,1,0:T(8,128)(2,1)} custom-call(bf16[1024,768]{1,0:T(8,128)(2,1)} %get-tuple-element.48.att_ref.a_ref.refs_4_, bf16[1024,768]{1,0:T(8,128)(2,1)} %get-tuple-element.69.b_ref), custom_call_target="tpu_custom_call" | custom-call | flops 1207959552 | bytes 4325376 | tf_op jit(solution)/shard_map/wgrad_cols/pallas_call | solution.py:612
  128.6 9.2 %wgrad_rows.1.refs_21_ = bf16[8,2,4,2,48,384]{5,4,3,2,1,0:T(8,128)(2,1)} custom-call(bf16[1024,3072]{1,0:T(8,128)(2,1)} %get-tuple-element.65.a_ref, bf16[1024,768]{1,0:T(8,128)(2,1)} %get-tuple-element.66.b_ref), custom_call_target="tpu_custom_call" | custom-call | flops 4831838208 | bytes 12582912 | tf_op jit(solution)/shard_map/wgrad_rows/pallas_call | solution.py:632
  137.7 9.2 %wgrad_cols.2.refs_22_ = bf16[8,2,4,2,48,384]{5,4,3,2,1,0:T(8,128)(2,1)} custom-call(bf16[1024,768]{1,0:T(8,128)(2,1)} %get-tuple-element.67.a_ref, bf16[1024,3072]{1,0:T(8,128)(2,1)} %get-tuple-element.68.b_ref), custom_call_target="tpu_custom_call" | custom-call | flops 4831838208 | bytes 12582912 | tf_op jit(solution)/shard_map/wgrad_cols/pallas_call | solution.py:612
  146.9 106.9 %tail.1 = (bf16[1024,768]{1,0:T(8,128)(2,1)}, bf16[768,768]{1,0:T(8,128)(2,1)}, bf16[192,3072]{1,0:T(8,128)(2,1)}, bf16[192,768]{1,0:T(8,128)(2,1)}, bf16[192,23...) custom-call(s32[1]{0:T(128)S(6)} %copy.43.refs_0_.len_ref, ...), custom_call_target="tpu_custom_call" | custom-call | flops 24159191040 | bytes 31457280 | tf_op jit(solution)/shard_map/tail/pallas_call | solution.py:1036
  253.8 1.1 slice_bitcast_fusion
  255.0 1.3 reduce
  256.3 1.3 reduce.1
  257.6 1.4 fusion.1
  259.0 1.9 convert_element_type.32
  260.9 2.5 convert_element_type.31
  263.4 1.7 convert_element_type.33
  265.1 1.6 convert_element_type.34
  266.7 0.5 copy-done
  267.2 1.1 copy.45
  268.3 0.3 copy-done.3
  268.6 0.8 copy.46
  269.5 0.8 copy.47
  (17 shorter events, 0.1 us)
Async XLA Ops:
  0.6 11.0 %copy-start.5 = (s32[1,1024]{1,0:T(1,128)S(1)}, s32[1,1024]{1,0:T(1,128)}, u32[]{:S(2)}) copy-start(s32[1,1024]{1,0:T(1,128)} %param.18) | copy-start | bytes 12292
  259.0 4.4 %copy-start.2 = (bf16[192,3072]{1,0:T(8,128)(2,1)S(1)}, bf16[192,3072]{1,0:T(8,128)(2,1)}, u32[]{:S(2)}) copy-start(bf16[192,3072]{1,0:T(8,128)(2,1)} %get-tuple-element.74) | copy-start | bytes 3538948
  263.4 1.7 copy-start.1
  265.1 2.1 copy-start
  267.2 1.4 copy-start.3
  267.2 2.3 copy-start.4

commit v8 on v7

--- a/solution.py
+++ b/solution.py
@@ -67,7 +67,7 @@
     return hi, mid, r - mid
 
 def attn_bwd_body(len_ref, q_ref, k_ref, v_ref, o_ref, g_ref, lse_ref, cos_ref, sin_ref,
-                  dqs, dks, dvs, rows, p, h, emit):
+                  dqs, dks, dvs, rows, p, h, emit, pause):
     s = q_ref.shape[0]
     length = len_ref[0]
     lane = lax.broadcasted_iota(jnp.int32, (s, 128), 1)
@@ -104,6 +104,8 @@
         dk = dk + dot(dst, qb)
         dqt = dot(kt, dst)
         dqs[:, sl] = jnp.where(h == 0, dqt, dqs[:, sl] + dqt)
+        if b == s // rows // 2 - 1:
+            pause()
     @pl.when(h == 0)
     def _():
         dks[...] = dk
@@ -949,7 +951,7 @@
     rscratch, sscratch = refs[33 + 2 * n:54 + 2 * n], refs[54 + 2 * n:]
     step, steps = pl.program_id(0), 2 * pairs + post
     p = Place(shape)
-    r = Reduce(p, counts, ["rows"] + ["cols"] * (n - 2) + ["qkv"], list(srcs) + [gq], reduced, rscratch, 3, 2)
+    r = Reduce(p, counts, ["rows"] + ["cols"] * (n - 2) + ["qkv"], list(srcs) + [gq], reduced, rscratch, 2, 2)
     small = Small(p, sscratch)
 
     @pl.when(step == 0)
@@ -957,9 +959,7 @@
         r.greet(small.peers())
         r.begin(0)
 
-    @pl.loop(2 * step, 2 * step + 2)
-    def _(t):
-        r.tick(t)
+    r.tick(2 * step)
 
     @pl.when(step < 2 * pairs)
     def _():
@@ -975,7 +975,7 @@
                 gq[2 * (pair // 2) + half, pair % 2] = y[:, half]
 
         attn_bwd_body(len_ref, q_ref, k_ref, v_ref, o_ref, g_ref, lse_ref, cos_ref, sin_ref, dqs, dks, dvs, rows,
-                      pair, head, emit)
+                      pair, head, emit, lambda: r.tick(2 * step + 1))
 
     @pl.when(step >= 2 * pairs)
     def _():
@@ -987,6 +987,7 @@
         h0 = jnp.where(masked, vpre_ref[0:1, :], tok_ref[...].astype(f32))
         igrad_ref[...], new = post_rows(grads, h0, masked, gh1_ref[...], vpre_ref[1:2, :], vpre_ref[2:3, :], w_ref)
         sums1[...] = jnp.where(i == 0, new, sums1[...] + new)
+        r.tick(2 * step + 1)
 
     @pl.when(step == steps - 1)
     def _():
@@ -1049,6 +1050,21 @@
         name="tail")(length, qkv, qkv, qkv, att, gatt, lse, cos, sin, n1t, w, tok, flag, gh1, vpre, vmid, sums, sb1, condp,
                      meta, ada, *grads)
     return res[0], res[1:1 + len(red)], res[1 + len(red):]
+
+
+def widen_kernel(*refs):
+    n = len(refs) // 2
+    for x, y in zip(refs[:n], refs[n:]):
+        y[...] = x[...].astype(f32)
+
+
+def widen(arrays, pieces):
+    specs = [pl.BlockSpec((a.shape[0], a.shape[1] // pieces), lambda i: (0, i)) for a in arrays]
+    return pl.pallas_call(
+        widen_kernel, grid=(pieces,), in_specs=specs, out_specs=specs,
+        out_shape=[jax.ShapeDtypeStruct(a.shape, f32) for a in arrays],
+        cost_estimate=pl.CostEstimate(flops=0, bytes_accessed=6 * sum(a.size for a in arrays), transcendentals=0),
+        name="widen")(*arrays)
 from jax.sharding import PartitionSpec as P
 
 highest = lax.Precision.HIGHEST
@@ -1086,9 +1102,8 @@
         shape, lengths, qkv, att, gatt, lse, cos, sin, n1, qkv_all, tok, flag, gh1, vec_pre, vec_mid, sums, gb1, cond_pre,
         meta, ada_all, [g_fc2, g_fc1, g_out], time_table.shape[0])
     g1, g2, gb2, gemb, gb1, g_ada, gbada, table, rms = small_results(shape, smalls, sizes)
-    return (out[None], igrad[None], g1, r_qkv.astype(f32), r_out.astype(f32), g2, r_fc1.astype(f32), gb1,
-            r_fc2.astype(f32), gb2,
-            g_ada, gbada, gemb, table, rms)
+    r_fc2, r_fc1, r_out, r_qkv = widen([r_fc2, r_fc1, r_out, r_qkv], d // 256)
+    return (out[None], igrad[None], g1, r_qkv, r_out, g2, r_fc1, gb1, r_fc2, gb2, g_ada, gbada, gemb, table, rms)
 
 
 def solution(mesh):

time: 271 us -> 265 us (0.978)
  other arithmetic: 14.6 us -> 6.93 us
  Pallas kernels: 241 us -> 244 us
    convert_element_type x4 -> x0, other arithmetic: 7.64 us -> none  [the longest x1 2.49 us: per_device(): r_qkv.astype(f32)]
    pallas_call x0 -> x1, Pallas kernels: none -> 5.23 us  [widen(): pl.pallas_call(widen_kernel, grid=(pieces,), in_specs=specs, out_specs=sp...]
    pallas_call x1, Pallas kernels: 107 us -> 104 us  [tail_call(): pl.pallas_call(functools.partial(tail_kernel, shape, counts, rows, blocks...]
where the time goes in v8:
time: 265 us
  Pallas kernels  244 us (92%)
  local copies, waits for them, and re-layouts  11.9 us (4%)
  other arithmetic  6.93 us (3%)
    pallas_call x1, Pallas kernels, tail_call(): pl.pallas_call(functools.partial(tail_kernel, shape, counts, rows, blocks...  104 us
    pallas_call x1, Pallas kernels, front_call(): pl.pallas_call(functools.partial(front_kernel, shape, sizes, rows), grid=...  73.8 us
    pallas_call x1, Pallas kernels, mid_call(): pl.pallas_call(functools.partial(mid_kernel, cut=cut), grid=(s // rows,),...  37.7 us
    pallas_call x2, Pallas kernels, wgrad_cols(): pl.pallas_call(wgrad_cols_kernel, grid=(n // m,), in_specs=[pl.BlockSpec(...  13.5 us
    pallas_call x1, Pallas kernels, wgrad_rows(): pl.pallas_call(wgrad_rows_kernel, grid=(groups,), in_specs=[pl.BlockSpec(...  9.22 us

profile of v8, /device:TPU:0, one launch (start us, length us, event | category | flops | bytes accessed | tf_op | source)
XLA Modules:
  0.0 264.6 jit_solution(14169858318275015823)
XLA Ops:
  0.6 0.0 copy-start.3
  2.0 1.2 constant_dynamic-slice_fusion.refs_5_.refs_18_
  3.2 0.7 pad.17
  3.8 0.7 pad.18
  4.5 0.7 pad.19
  5.2 0.7 pad.20
  5.8 0.6 maximum_bitcast_fusion.refs_19_
  6.5 0.7 constant_dynamic-update-slice_fusion.1
  7.2 0.7 constant_dynamic-update-slice_fusion
  7.9 0.6 concatenate.13.refs_6_
  8.5 0.1 iota_multiply_fusion
  8.6 3.0 %sine_multiply_fusion = (f32[1024,128]{1,0:T(8,128)}, f32[1024,128]{1,0:T(8,128)}) fusion(f32[1024,32]{1,0:T(8,128)S(1)} %iota_multiply_fusion, f32[128]{0:T(128)S(1)} %compare_select_fusion), kind=kLoop, calls=%fused_computation.1 | loop fusion | flops 524288 | bytes 1180160 | tf_op jit(solution)/shard_map/mul | solution.py:1079
  11.6 0.0 copy-done.3
  11.6 1.0 copy.32.refs_2_.flag_ref.refs_12_
  12.6 73.8 %front.1 = (bf16[1024,768]{1,0:T(8,128)(2,1)}, f32[1024,128]{1,0:T(8,128)}, f32[8,768]{1,0:T(8,128)}, f32[8,768]{1,0:T(8,128)}, f32[1,3072]{1,0:T(1,128)}, /*ind...) custom-call(s32[1]{0:T(128)S(6)} %copy.43.refs_0_.len_ref, ...), custom_call_target="tpu_custom_call" | custom-call | flops 10066329600 | bytes 15728640 | tf_op jit(solution)/shard_map/front/pallas_call | solution.py:789
  86.4 37.7 %mid.1 = (bf16[1024,768]{1,0:T(8,128)(2,1)}, f32[1024,768]{1,0:T(8,128)}, bf16[1024,768]{1,0:T(8,128)(2,1)}, bf16[1024,768]{1,0:T(8,128)(2,1)}, bf16[1024,3072]{...) custom-call(s32[1]{0:T(128)S(6)} %copy.43.refs_0_.len_ref, ...), custom_call_target="tpu_custom_call" | custom-call | flops 21743271936 | bytes 23592960 | tf_op jit(solution)/shard_map/mid/pallas_call | solution.py:195
  124.2 4.3 %wgrad_cols.3.refs_23_ = bf16[2,2,4,2,48,384]{5,4,3,2,1,0:T(8,128)(2,1)} custom-call(bf16[1024,768]{1,0:T(8,128)(2,1)} %get-tuple-element.52.att_ref.a_ref.refs_4_, bf16[1024,768]{1,0:T(8,128)(2,1)} %get-tuple-element.73.b_ref), custom_call_target="tpu_custom_call" | custom-call | flops 1207959552 | bytes 4325376 | tf_op jit(solution)/shard_map/wgrad_cols/pallas_call | solution.py:614
  128.5 9.2 %wgrad_rows.1.refs_21_ = bf16[8,2,4,2,48,384]{5,4,3,2,1,0:T(8,128)(2,1)} custom-call(bf16[1024,3072]{1,0:T(8,128)(2,1)} %get-tuple-element.69.a_ref, bf16[1024,768]{1,0:T(8,128)(2,1)} %get-tuple-element.70.b_ref), custom_call_target="tpu_custom_call" | custom-call | flops 4831838208 | bytes 12582912 | tf_op jit(solution)/shard_map/wgrad_rows/pallas_call | solution.py:634
  137.8 9.2 %wgrad_cols.2.refs_22_ = bf16[8,2,4,2,48,384]{5,4,3,2,1,0:T(8,128)(2,1)} custom-call(bf16[1024,768]{1,0:T(8,128)(2,1)} %get-tuple-element.71.a_ref, bf16[1024,3072]{1,0:T(8,128)(2,1)} %get-tuple-element.72.b_ref), custom_call_target="tpu_custom_call" | custom-call | flops 4831838208 | bytes 12582912 | tf_op jit(solution)/shard_map/wgrad_cols/pallas_call | solution.py:614
  146.9 104.2 %tail.1 = (bf16[1024,768]{1,0:T(8,128)(2,1)}, bf16[768,768]{1,0:T(8,128)(2,1)}, bf16[192,3072]{1,0:T(8,128)(2,1)}, bf16[192,768]{1,0:T(8,128)(2,1)}, bf16[192,23...) custom-call(s32[1]{0:T(128)S(6)} %copy.43.refs_0_.len_ref, ...), custom_call_target="tpu_custom_call" | custom-call | flops 24159191040 | bytes 31457280 | tf_op jit(solution)/shard_map/tail/pallas_call | solution.py:1037
  251.1 1.2 slice_bitcast_fusion
  252.3 1.3 reduce
  253.6 1.3 reduce.1
  254.9 1.4 fusion.1
  256.3 5.2 %widen.1 = (f32[768,768]{1,0:T(8,128)}, f32[192,3072]{1,0:T(8,128)}, f32[192,768]{1,0:T(8,128)}, f32[192,2304]{1,0:T(8,128)}) custom-call(bf16[768,768]{1,0:T(8,128)(2,1)} %get-tuple-element.76.refs_0_, bf16[192,3072]{1,0:T(8,128)(2,1)} %get-tuple-element.77.refs_1_, bf16[192,768]{1,0:T(8,128)(2,1)} %get-tuple-element.78.refs_2_, ...), custom_call_target="tpu_custom_call" | custom-call | bytes 10616832 | tf_op jit(solution)/shard_map/widen/pallas_call | solution.py:1063
  261.6 0.0 copy-done
  261.6 0.0 copy-start.1
  261.6 1.1 copy.45
  262.7 0.3 copy-done.1
  263.0 0.8 copy.46
  263.8 0.0 copy-done.2
  263.8 0.8 copy.47
  (10 shorter events, 0.1 us)
Async XLA Ops:
  0.6 11.0 %copy-start.3 = (s32[1,1024]{1,0:T(1,128)S(1)}, s32[1,1024]{1,0:T(1,128)}, u32[]{:S(2)}) copy-start(s32[1,1024]{1,0:T(1,128)} %param.18) | copy-start | bytes 12292
  256.3 5.2 %copy-start = (bf16[1024,768]{1,0:T(8,128)(2,1)S(1)}, bf16[1024,768]{1,0:T(8,128)(2,1)}, u32[]{:S(2)}) copy-start(bf16[1024,768]{1,0:T(8,128)(2,1)} %get-tuple-element.74) | copy-start | bytes 4718596
  261.6 1.4 copy-start.1
  261.6 2.2 copy-start.2

commit v9 on v8

--- a/solution.py
+++ b/solution.py
@@ -940,18 +940,20 @@
     return g1, g2, gb2, gemb, gb1[0], gada, gbada[0], table, rms[0, :3]
 
 
-def tail_kernel(shape, counts, rows, post, pairs, *refs):
+def tail_kernel(shape, counts, rows, post, pairs, inner, *refs):
     n = len(counts)
+    extra, refs = refs[21:21 + 2 * inner], refs[:21] + refs[21 + 2 * inner:]
+    m = n - 1 - inner
     (len_ref, q_ref, k_ref, v_ref, o_ref, g_ref, lse_ref, cos_ref, sin_ref, n1_ref, w_ref, tok_ref, flag_ref, gh1_ref,
      vpre_ref, vmid_ref, sums_ref, sb1_ref, condp_ref, meta_ref, ada_ref) = refs[:21]
-    srcs = refs[21:20 + n]
-    outs = refs[20 + n:21 + 2 * n]
-    igrad_ref, reduced, small_out = outs[0], outs[1:1 + n], refs[21 + 2 * n:27 + 2 * n]
-    dqs, dks, dvs, dqkv, gq, sums1 = refs[27 + 2 * n:33 + 2 * n]
-    rscratch, sscratch = refs[33 + 2 * n:54 + 2 * n], refs[54 + 2 * n:]
+    srcs, outs, work = refs[21:21 + m], refs[21 + m:28 + m + n], refs[28 + m + n:]
+    igrad_ref, reduced, small_out = outs[0], outs[1:1 + n], outs[1 + n:]
+    dqs, dks, dvs, dqkv, gq, sums1 = work[:6]
+    held, work = work[6:6 + inner], work[6 + inner:]
+    rscratch, sscratch = work[:21], work[21:]
     step, steps = pl.program_id(0), 2 * pairs + post
     p = Place(shape)
-    r = Reduce(p, counts, ["rows"] + ["cols"] * (n - 2) + ["qkv"], list(srcs) + [gq], reduced, rscratch, 2, 2)
+    r = Reduce(p, counts, ["rows"] + ["cols"] * (n - 2) + ["qkv"], list(srcs) + list(held) + [gq], reduced, rscratch, 2, 2)
     small = Small(p, sscratch)
 
     @pl.when(step == 0)
@@ -960,6 +962,19 @@
         r.begin(0)
 
     r.tick(2 * step)
+
+    if inner:
+        n2_ref, gpre_ref = extra
+        held_ref = held[0]
+
+        @pl.when(step < held_ref.shape[0] // 2)
+        def _():
+            y = dot(n2_ref[...], gpre_ref[...], TN).astype(bf16)
+            _, _, gr, _, rr, c = held_ref.shape
+            for core in (0, 1):
+                z = y[:, core * c:(core + 1) * c].reshape(gr, 2, 2, rr, c)
+                for half in (0, 1):
+                    held_ref[2 * step + half, core] = z[:, half]
 
     @pl.when(step < 2 * pairs)
     def _():
@@ -1011,17 +1026,21 @@
 
 
 def tail_call(shape, length, qkv, att, gatt, lse, cos, sin, n1t, w, tok, flag, gh1, vpre, vmid, sums, sb1, condp, meta,
-              ada, grads, table_rows, rows=256):
+              ada, grads, n2, gpre, table_rows, rows=256):
     groups = shape["fsdp"]
     s, d3 = qkv.shape
     d = d3 // 3
     pairs = d // 128
     r, c = 2 * grads[0].shape[-2], grads[0].shape[-1]
     post = 256 if r % 32 == 0 else 128
+    ff, n_mod = sb1.shape[1], ada.shape[0]
     blocks = s // post
     steps = 2 * pairs + blocks
-    ff, n_mod = sb1.shape[1], ada.shape[0]
-    counts = [g.shape[0] for g in grads] + [pairs]
+    inner = int(r % 32 == 0)
+    if not inner:
+        grads = grads + [wgrad_cols(n2, gpre, groups)]
+    chunks = [grads[0].shape[0], grads[1].shape[0], 2 * ff // d]
+    counts = chunks + [pairs]
     pair = lambda i: jnp.minimum(i // 2, pairs - 1)
     blk = lambda i: jnp.maximum(i - 2 * pairs, 0)
     once = pl.Buffered(1)
@@ -1030,25 +1049,27 @@
     row = lambda cc: pl.BlockSpec((post, cc), lambda i: (blk(i), 0))
     sd = jax.ShapeDtypeStruct
     shard = d // groups
-    red = [sd((shard * (g.shape[0] // 2), d), bf16) if i == 0 else sd((shard, d * (g.shape[0] // 2)), bf16)
-           for i, g in enumerate(grads)] + [sd((shard, d3), bf16)]
+    red = [sd((shard * (g // 2), d), bf16) if i == 0 else sd((shard, d * (g // 2)), bf16)
+           for i, g in enumerate(chunks)] + [sd((shard, d3), bf16)]
     smalls = small_shapes(shape, d, ff, n_mod, table_rows)
     const = lambda x: pl.BlockSpec(x.shape, lambda i: (0, 0), pipeline_mode=once)
     res = pl.pallas_call(
-        functools.partial(tail_kernel, shape, counts, rows, blocks, pairs), grid=(steps,),
+        functools.partial(tail_kernel, shape, counts, rows, blocks, pairs, inner), grid=(steps,),
         in_specs=[pl.BlockSpec(memory_space=pltpu.SMEM), col(0), col(pairs), col(2 * pairs), col(0), col(0), whole(lse),
                   whole(cos), whole(sin), whole(n1t), whole(w), row(d), row(1), row(d)]
-        + [whole(x) for x in (vpre, vmid, sums, sb1, condp, meta, ada)] + [ANY] * len(grads),
+        + [whole(x) for x in (vpre, vmid, sums, sb1, condp, meta, ada)]
+        + [whole(n2), pl.BlockSpec((s, d), lambda i: (0, jnp.minimum(i, ff // d - 1)))] * inner + [ANY] * len(grads),
         out_specs=[row(d)] + [ANY] * len(red) + [const(x) for x in smalls],
         out_shape=[sd((s, d), bf16)] + red + smalls,
         scratch_shapes=[pltpu.VMEM((128, s), f32), pltpu.VMEM((s, 128), f32), pltpu.VMEM((s, 128), f32),
                         pltpu.VMEM((3, pairs, s, 128), bf16), pltpu.VMEM((pairs, 2, groups, 2, r // 2, c), bf16),
                         pltpu.VMEM((8, d), f32)]
+        + [pltpu.VMEM((2 * ff // d, 2, groups, 2, r // 2, c), bf16)] * inner
         + Reduce.scratch(sum(counts), groups, r, c) + Small.scratch(shape, d, ff, n_mod),
         compiler_params=pltpu.CompilerParams(collective_id=3, has_side_effects=True, vmem_limit_bytes=65000 * 1024),
         cost_estimate=pl.CostEstimate(flops=30 * s * s * d, bytes_accessed=40 * s * d, transcendentals=s * s * 12),
         name="tail")(length, qkv, qkv, qkv, att, gatt, lse, cos, sin, n1t, w, tok, flag, gh1, vpre, vmid, sums, sb1, condp,
-                     meta, ada, *grads)
+                     meta, ada, *([n2, gpre] * inner), *grads)
     return res[0], res[1:1 + len(red)], res[1 + len(red):]
 
 
@@ -1095,12 +1116,11 @@
     out, gh1, gatt, n2, act, gm, gpre, gap, sums, gb1 = mid_call(
         lengths, att, tok, flag, cot, vec_mid, b1, out_all, fc1_all, fc2_all)
     g_fc2 = wgrad_rows(act, gm, groups)
-    g_fc1 = wgrad_cols(n2, gpre, groups)
     g_out = wgrad_cols(att, gap, groups)
     meta = jnp.concatenate([jnp.zeros((3,), f32), lengths.astype(f32), time_ids.astype(f32), jnp.zeros((123,), f32)])[None]
-    igrad, (r_fc2, r_fc1, r_out, r_qkv), smalls = tail_call(
+    igrad, (r_fc2, r_out, r_fc1, r_qkv), smalls = tail_call(
         shape, lengths, qkv, att, gatt, lse, cos, sin, n1, qkv_all, tok, flag, gh1, vec_pre, vec_mid, sums, gb1, cond_pre,
-        meta, ada_all, [g_fc2, g_fc1, g_out], time_table.shape[0])
+        meta, ada_all, [g_fc2, g_out], n2, gpre, time_table.shape[0])
     g1, g2, gb2, gemb, gb1, g_ada, gbada, table, rms = small_results(shape, smalls, sizes)
     r_fc2, r_fc1, r_out, r_qkv = widen([r_fc2, r_fc1, r_out, r_qkv], d // 256)
     return (out[None], igrad[None], g1, r_qkv, r_out, g2, r_fc1, gb1, r_fc2, gb2, g_ada, gbada, gemb, table, rms)

time: 265 us -> 261 us (0.985)
  Pallas kernels: 244 us -> 240 us
    pallas_call x2 -> x1, Pallas kernels: 13.5 us -> 4.35 us  [wgrad_cols(): pl.pallas_call(wgrad_cols_kernel, grid=(n // m,), in_specs=[pl.BlockSpec(...]
    pallas_call x1, Pallas kernels: 104 us -> 109 us  [tail_call(): pl.pallas_call(functools.partial(tail_kernel, shape, counts, rows, blocks...]
where the time goes in v9:
time: 261 us
  Pallas kernels  240 us (92%)
  local copies, waits for them, and re-layouts  11.9 us (5%)
  other arithmetic  6.93 us (3%)
    pallas_call x1, Pallas kernels, tail_call(): pl.pallas_call(functools.partial(tail_kernel, shape, counts, rows, blocks...  109 us
    pallas_call x1, Pallas kernels, front_call(): pl.pallas_call(functools.partial(front_kernel, shape, sizes, rows), grid=...  73.8 us
    pallas_call x1, Pallas kernels, mid_call(): pl.pallas_call(functools.partial(mid_kernel, cut=cut), grid=(s // rows,),...  37.7 us
    pallas_call x1, Pallas kernels, wgrad_rows(): pl.pallas_call(wgrad_rows_kernel, grid=(groups,), in_specs=[pl.BlockSpec(...  9.23 us
    pallas_call x1, Pallas kernels, widen(): pl.pallas_call(widen_kernel, grid=(pieces,), in_specs=specs, out_specs=sp...  5.23 us

profile of v9, /device:TPU:0, one launch (start us, length us, event | category | flops | bytes accessed | tf_op | source)
XLA Modules:
  0.0 260.6 jit_solution(16412426316242188146)
XLA Ops:
  0.6 0.0 copy-start.3
  2.0 1.2 constant_dynamic-slice_fusion.refs_5_.refs_18_
  3.2 0.7 pad.17
  3.8 0.7 pad.18
  4.5 0.7 pad.19
  5.2 0.7 pad.20
  5.8 0.6 maximum_bitcast_fusion.refs_19_
  6.5 0.7 constant_dynamic-update-slice_fusion.1
  7.2 0.7 constant_dynamic-update-slice_fusion
  7.9 0.6 concatenate.13.refs_6_
  8.5 0.1 iota_multiply_fusion
  8.6 3.0 %sine_multiply_fusion = (f32[1024,128]{1,0:T(8,128)}, f32[1024,128]{1,0:T(8,128)}) fusion(f32[1024,32]{1,0:T(8,128)S(1)} %iota_multiply_fusion, f32[128]{0:T(128)S(1)} %compare_select_fusion), kind=kLoop, calls=%fused_computation.1 | loop fusion | flops 524288 | bytes 1180160 | tf_op jit(solution)/shard_map/mul | solution.py:1100
  11.6 0.0 copy-done.3
  11.6 1.0 copy.32.refs_2_.flag_ref.refs_12_
  12.6 73.8 %front.1 = (bf16[1024,768]{1,0:T(8,128)(2,1)}, f32[1024,128]{1,0:T(8,128)}, f32[8,768]{1,0:T(8,128)}, f32[8,768]{1,0:T(8,128)}, f32[1,3072]{1,0:T(1,128)}, /*ind...) custom-call(s32[1]{0:T(128)S(6)} %copy.43.refs_0_.len_ref, ...), custom_call_target="tpu_custom_call" | custom-call | flops 10066329600 | bytes 15728640 | tf_op jit(solution)/shard_map/front/pallas_call | solution.py:789
  86.4 37.7 %mid.1 = (bf16[1024,768]{1,0:T(8,128)(2,1)}, f32[1024,768]{1,0:T(8,128)}, bf16[1024,768]{1,0:T(8,128)(2,1)}, bf16[1024,768]{1,0:T(8,128)(2,1)}, bf16[1024,3072]{...) custom-call(s32[1]{0:T(128)S(6)} %copy.43.refs_0_.len_ref, ...), custom_call_target="tpu_custom_call" | custom-call | flops 21743271936 | bytes 23592960 | tf_op jit(solution)/shard_map/mid/pallas_call | solution.py:195
  124.2 4.3 %wgrad_cols.1.refs_24_ = bf16[2,2,4,2,48,384]{5,4,3,2,1,0:T(8,128)(2,1)} custom-call(bf16[1024,768]{1,0:T(8,128)(2,1)} %get-tuple-element.52.att_ref.a_ref.refs_4_, bf16[1024,768]{1,0:T(8,128)(2,1)} %get-tuple-element.73.b_ref), custom_call_target="tpu_custom_call" | custom-call | flops 1207959552 | bytes 4325376 | tf_op jit(solution)/shard_map/wgrad_cols/pallas_call | solution.py:614
  128.5 9.2 %wgrad_rows.1.refs_23_ = bf16[8,2,4,2,48,384]{5,4,3,2,1,0:T(8,128)(2,1)} custom-call(bf16[1024,3072]{1,0:T(8,128)(2,1)} %get-tuple-element.71.a_ref, bf16[1024,768]{1,0:T(8,128)(2,1)} %get-tuple-element.72.b_ref), custom_call_target="tpu_custom_call" | custom-call | flops 4831838208 | bytes 12582912 | tf_op jit(solution)/shard_map/wgrad_rows/pallas_call | solution.py:634
  137.8 109.3 %tail.1 = (bf16[1024,768]{1,0:T(8,128)(2,1)}, bf16[768,768]{1,0:T(8,128)(2,1)}, bf16[192,768]{1,0:T(8,128)(2,1)}, bf16[192,3072]{1,0:T(8,128)(2,1)}, bf16[192,23...) custom-call(s32[1]{0:T(128)S(6)} %copy.43.refs_0_.len_ref, ...), custom_call_target="tpu_custom_call" | custom-call | flops 24159191040 | bytes 31457280 | tf_op jit(solution)/shard_map/tail/pallas_call | solution.py:1056
  247.1 1.2 slice_bitcast_fusion
  248.3 1.3 reduce
  249.6 1.3 reduce.1
  250.9 1.4 fusion.1
  252.3 5.2 %widen.1 = (f32[768,768]{1,0:T(8,128)}, f32[192,3072]{1,0:T(8,128)}, f32[192,768]{1,0:T(8,128)}, f32[192,2304]{1,0:T(8,128)}) custom-call(bf16[768,768]{1,0:T(8,128)(2,1)} %get-tuple-element.76.refs_0_, bf16[192,3072]{1,0:T(8,128)(2,1)} %get-tuple-element.77.refs_1_, bf16[192,768]{1,0:T(8,128)(2,1)} %get-tuple-element.78.refs_2_, ...), custom_call_target="tpu_custom_call" | custom-call | bytes 10616832 | tf_op jit(solution)/shard_map/widen/pallas_call | solution.py:1084
  257.5 0.0 copy-done
  257.5 0.0 copy-start.1
  257.5 0.0 copy-start.2
  257.5 1.1 copy.45
  258.7 0.3 copy-done.1
  258.9 0.8 copy.46
  259.8 0.0 copy-done.2
  259.8 0.8 copy.47
  (9 shorter events, 0.1 us)
Async XLA Ops:
  0.6 11.0 %copy-start.3 = (s32[1,1024]{1,0:T(1,128)S(1)}, s32[1,1024]{1,0:T(1,128)}, u32[]{:S(2)}) copy-start(s32[1,1024]{1,0:T(1,128)} %param.18) | copy-start | bytes 12292
  252.3 5.2 %copy-start = (bf16[1024,768]{1,0:T(8,128)(2,1)S(1)}, bf16[1024,768]{1,0:T(8,128)(2,1)}, u32[]{:S(2)}) copy-start(bf16[1024,768]{1,0:T(8,128)(2,1)} %get-tuple-element.74) | copy-start | bytes 4718596
  257.5 1.4 copy-start.1
  257.5 2.2 copy-start.2
